TPU v7x, 8 devices: a whole 2x2x1 slice. The times are simulated.
8 devices in a mesh: rep: 1 (over z), data: 2 (over y), expert: 4 (over x, core).
Axes of the slice: x: 2, y: 2, z: 1, core: 2. Of those that a mesh axis runs over, the one named last changes fastest.
Arguments:
- x_tok: bfloat16 [16384, 896], P(('rep', 'expert', 'data'))
- expert_idx: int32 [16384, 8], P(('rep', 'expert', 'data'))
- gate_val: float32 [16384, 8], P(('rep', 'expert', 'data'))
- w_gate: bfloat16 [64, 896, 640], P('expert', 'data')
- w_up: bfloat16 [64, 896, 640], P('expert', 'data')
- w_down: bfloat16 [64, 640, 896], P('expert', None, 'data')
- ws_gate: bfloat16 [896, 5120], P(('expert', 'data'))
- ws_up: bfloat16 [896, 5120], P(('expert', 'data'))
- ws_down: bfloat16 [5120, 896], P(None, ('expert', 'data'))
Outputs:
- output: bfloat16 [16384, 896], P(('rep', 'expert', 'data'))
All inputs are finite; a program needn't handle non-finite values.
Results may differ from a plain program's by a relative error of at most 0.001.
Values are sent between devices in bfloat16 or wider.
A program may use at most 1 GiB of HBM per device.

v0:
```python
import functools

import jax
import jax.numpy as jnp
from jax import lax
from jax.experimental import pallas as pl
from jax.experimental.pallas import tpu as pltpu
from jax.sharding import PartitionSpec as P


CAP_NUM = 5
CAP_DEN = 4
BF16 = jnp.bfloat16
F32 = jnp.float32
CHUNKS = (2, 2, 2, 1, 1)
LANES = 128
TILE = 8
VMEM_LIMIT = 56 * 1024 * 1024


def capacity_of(tok_count, top_count, n_exp):
    return max(8, ((CAP_NUM * top_count * tok_count) // (CAP_DEN * n_exp) + 7) // 8 * 8)


def params(sem):
    return pltpu.CompilerParams(dimension_semantics=sem, vmem_limit_bytes=VMEM_LIMIT)


def cost(flops, nbytes):
    return pl.CostEstimate(flops=int(flops) // 64, bytes_accessed=int(nbytes), transcendentals=0)


def gather_kernel(per_step, capacity, pos_ref, x_ref, *refs):
    out_ref, hot_ref = refs[-2], refs[-1]
    step = pl.program_id(0)
    tok_count = x_ref.shape[0]
    slot = lax.broadcasted_iota(jnp.int32, (capacity, tok_count), 0)
    for i in range(per_step):
        pos = pos_ref[pl.ds(step * per_step + i, 1), :]
        hot_ref[i * capacity:(i + 1) * capacity, :] = jnp.where(pos == slot, 1.0, 0.0).astype(BF16)
    rows = jnp.dot(hot_ref[...], x_ref[...], preferred_element_type=F32).astype(BF16)
    out_ref[...] = rows.reshape(out_ref.shape)


def gather_rows(rel, n_blocks, pos, x_blk, buffer, capacity):
    pos_rows, tok_count = pos.shape
    n_exp = pos_rows - TILE
    d_model = x_blk.shape[1]
    per_step = 2
    in_specs = [pl.BlockSpec((pos_rows, tok_count), lambda i: (0, 0)), pl.BlockSpec((tok_count, d_model), lambda i: (0, 0))]
    args = [pos, x_blk]
    aliases = {}
    if buffer is not None:
        in_specs.append(pl.BlockSpec(memory_space=pl.ANY))
        args.append(buffer)
        aliases = {2: 0}
    rows = n_exp * capacity
    return pl.pallas_call(
        functools.partial(gather_kernel, per_step, capacity),
        out_shape=jax.ShapeDtypeStruct((n_blocks, n_exp, capacity, d_model), BF16),
        grid=(n_exp // per_step,),
        in_specs=in_specs,
        out_specs=pl.BlockSpec((1, per_step, capacity, d_model), lambda i: (rel, i, 0, 0)),
        scratch_shapes=[pltpu.VMEM((per_step * capacity, tok_count), BF16)],
        input_output_aliases=aliases,
        compiler_params=params(("arbitrary",)),
        cost_estimate=cost(2 * rows * tok_count * d_model, rows * d_model * 2),
        name="gather_rows",
    )(*args)


def swiglu(x, w_gate_up, w_down_t):
    width = w_down_t.shape[1]
    pre = jnp.dot(x, w_gate_up, preferred_element_type=F32)
    hidden = (jax.nn.silu(pre[:, :width]) * pre[:, width:]).astype(BF16)
    return lax.dot_general(hidden, w_down_t, (((1,), (1,)), ((), ())), preferred_element_type=F32)


def expert_kernel(half, y_ref, xg_ref, og_ref, ou_ref, od_ref, rv_ref, out_ref, wgu_ref, wd_ref):
    width = wd_ref.shape[1]

    @pl.when(pl.program_id(1) == 0)
    def _():
        mine = pl.multiple_of(y_ref[0] * half, 64)
        other = pl.multiple_of((1 - y_ref[0]) * half, 64)
        wgu_ref[pl.ds(mine, half), :width] = og_ref[0]
        wgu_ref[pl.ds(mine, half), width:] = ou_ref[0]
        wd_ref[pl.ds(mine, half), :] = od_ref[0]
        wgu_ref[pl.ds(other, half), :width] = rv_ref[0, 0]
        wgu_ref[pl.ds(other, half), width:] = rv_ref[1, 0]
        wd_ref[pl.ds(other, half), :] = rv_ref[2, 0]

    n_blk, _, capacity, d_model = xg_ref.shape
    x = xg_ref[...].reshape(n_blk * capacity, d_model)
    out = swiglu(x, wgu_ref[...], wd_ref[...])
    out_ref[...] = out.astype(BF16).reshape(out_ref.shape)


def expert_rows(first, count, y_arr, xg, wg, wu, wdt, recv):
    n_blocks, n_exp, capacity, d_model = xg.shape
    half, width = wg.shape[1:]
    per_step = 2
    own = pl.BlockSpec((1, half, width), lambda i, m, y: (y[0] * n_exp + first + i, 0, 0))
    return pl.pallas_call(
        functools.partial(expert_kernel, half),
        out_shape=jax.ShapeDtypeStruct((count, n_blocks, capacity, d_model), BF16),
        grid_spec=pltpu.PrefetchScalarGridSpec(
            num_scalar_prefetch=1,
            grid=(count, n_blocks // per_step),
            in_specs=[
                pl.BlockSpec((per_step, 1, capacity, d_model), lambda i, m, y: (m, first + i, 0, 0)),
                own, own, own,
                pl.BlockSpec((3, 1, half, width), lambda i, m, y: (0, i, 0, 0)),
            ],
            out_specs=pl.BlockSpec((1, per_step, capacity, d_model), lambda i, m, y: (i, m, 0, 0)),
            scratch_shapes=[pltpu.VMEM((2 * half, 2 * width), BF16), pltpu.VMEM((2 * half, width), BF16)],
        ),
        compiler_params=params(("arbitrary", "arbitrary")),
        cost_estimate=cost(6 * count * n_blocks * capacity * d_model * width, 4 * count * n_blocks * capacity * d_model),
        name="expert_rows",
    )(y_arr, xg, wg, wu, wdt, recv)


def shared_kernel(x_ref, wgu_ref, wd_ref, out_ref):
    out_ref[...] = swiglu(x_ref[...], wgu_ref[...], wd_ref[...])


def shared_part(x_blk, wgu, wdt):
    tok_count, d_model = x_blk.shape
    width = wdt.shape[1]
    tile = 512
    rows = pl.BlockSpec((tile, d_model), lambda i: (i, 0))
    return pl.pallas_call(
        shared_kernel,
        out_shape=jax.ShapeDtypeStruct((tok_count, d_model), F32),
        grid=(tok_count // tile,),
        in_specs=[rows, pl.BlockSpec((d_model, 2 * width), lambda i: (0, 0)), pl.BlockSpec((d_model, width), lambda i: (0, 0))],
        out_specs=rows,
        compiler_params=params(("arbitrary",)),
        cost_estimate=cost(6 * tok_count * d_model * width, 6 * tok_count * d_model),
        name="shared_part",
    )(x_blk, wgu, wdt)


def combine_kernel(rel, n_base, where_of, halves, capacity, group, *refs):
    cnt_ref, tok_ref, gate_ref = refs[:3]
    bases = refs[3:3 + n_base]
    n_chunks = max(c for c, _, _ in where_of) + 1
    outs = refs[3 + n_base:3 + n_base + n_chunks]
    n_out = 2 if halves else 1
    pos = 3 + n_base + n_chunks
    y_refs = refs[pos:pos + n_out]
    acc, tmps, rows, wide, sem_in, sem_rows, sem_out = refs[pos + n_out:]
    tok_count, d_model = bases[0].shape
    n_col = d_model // LANES
    step = 256
    n_step = tok_count // step

    def in_copy(k, b):
        at = pl.ds(b * step, step)
        return pltpu.make_async_copy(bases[k].at[at], tmps.at[k, at], sem_in.at[k, b])

    def out_copy(b):
        at = b * step
        per_out = tok_count // n_out
        dst = y_refs[at // per_out].at[pl.ds(at % per_out, step)]
        return pltpu.make_async_copy(tmps.at[0, pl.ds(at, step)], dst, sem_out.at[b])

    def row_copy(i):
        c, local, _ = where_of[i]
        return pltpu.make_async_copy(outs[c].at[local, rel], rows.at[i % 2], sem_rows.at[i % 2])

    for b in range(n_step):
        for k in range(n_base):
            in_copy(k, b).start()
    row_copy(0).start()

    for b in range(n_step):
        for k in range(n_base):
            in_copy(k, b).wait()

        @pl.loop(0, step // 32)
        def _(q):
            at = pl.multiple_of(b * step + q * 32, 32)
            val = tmps[0, pl.ds(at, 32), :]
            for k in range(1, n_base):
                val = val + tmps[k, pl.ds(at, 32), :]
            for j in range(n_col):
                acc[pl.ds(at * TILE + j, 32, stride=TILE), :] = val[:, j * LANES:(j + 1) * LANES]

    for i in range(len(where_of)):
        row_copy(i).wait()
        if i + 1 < len(where_of):
            row_copy(i + 1).start()
        e = where_of[i][2]
        slot = i % 2

        @pl.loop(0, capacity // 32)
        def _(q):
            at = pl.multiple_of(q * 32, 32)
            val = rows[slot, pl.ds(at, 32), :].astype(F32)
            for j in range(n_col):
                wide[pl.ds(at * TILE + j, 32, stride=TILE), :] = val[:, j * LANES:(j + 1) * LANES]

        @pl.loop(0, (cnt_ref[0, e] + (group - 1)) // group)
        def _(q):
            sums, toks = [], []
            for i in range(group):
                s = q * group + i
                t = pl.multiple_of(tok_ref[0, e * capacity + s], TILE)
                g = gate_ref[0, e * capacity + s]
                toks.append(t)
                sums.append(acc[pl.ds(t, TILE), :] + g * wide[pl.ds(pl.multiple_of(s * TILE, TILE), TILE), :])
            for i in range(group):
                acc[pl.ds(toks[i], TILE), :] = sums[i]

    for b in range(n_step):

        @pl.loop(0, step // 32)
        def _(q):
            at = pl.multiple_of(b * step + q * 32, 32)
            for j in range(n_col):
                tmps[0, pl.ds(at, 32), j * LANES:(j + 1) * LANES] = acc[pl.ds(at * TILE + j, 32, stride=TILE), :]

        out_copy(b).start()
    for b in range(n_step):
        out_copy(b).wait()


def combine(rel, cnt, toks, gates, bases, outs, first, halves):
    tok_count, d_model = bases[0].shape
    capacity = outs[0].shape[2]
    where_of = []
    for c, o in enumerate(outs):
        for i in range(o.shape[0]):
            where_of.append((c, i, first + len(where_of)))
    smem = pl.BlockSpec(memory_space=pltpu.SMEM)
    hbm = pl.BlockSpec(memory_space=pl.ANY)
    n_base = len(bases)
    if halves:
        out_shape = [jax.ShapeDtypeStruct((tok_count // 2, d_model), F32)] * 2
        out_specs = [hbm, hbm]
    else:
        out_shape, out_specs = jax.ShapeDtypeStruct((tok_count, d_model), F32), hbm
    return pl.pallas_call(
        functools.partial(combine_kernel, rel, n_base, tuple(where_of), halves, capacity, 8),
        out_shape=out_shape,
        in_specs=[smem, smem, smem] + [hbm] * (n_base + len(outs)),
        out_specs=out_specs,
        scratch_shapes=[
            pltpu.VMEM(((tok_count + 1) * TILE, LANES), F32),
            pltpu.VMEM((n_base, tok_count, d_model), F32),
            pltpu.VMEM((2, capacity, d_model), BF16),
            pltpu.VMEM((capacity * TILE, LANES), F32),
            pltpu.SemaphoreType.DMA((n_base, tok_count // 256)),
            pltpu.SemaphoreType.DMA((2,)),
            pltpu.SemaphoreType.DMA((tok_count // 256,)),
        ],
        compiler_params=pltpu.CompilerParams(vmem_limit_bytes=VMEM_LIMIT),
        cost_estimate=cost(len(where_of) * capacity * tok_count * d_model, tok_count * d_model * 8),
        name="combine",
    )(cnt, toks, gates, *bases, *outs)


def solution(mesh):
    exp_n = mesh.shape["expert"]
    data_n = mesh.shape["data"]
    assert exp_n == 4 and data_n == 2
    tok_spec = P(("rep", "expert", "data"), None)
    group_axes = ("expert", "data")
    n_dev = exp_n * data_n

    def over_y(v):
        return lax.ppermute(v, "data", [(i, i ^ 1) for i in range(data_n)])

    def over_core(v):
        return lax.ppermute(v, "expert", [(i, i ^ 1) for i in range(exp_n)])

    def over_x(v):
        return lax.ppermute(v, "expert", [(i, i ^ 2) for i in range(exp_n)])

    def device_fn(x_loc, idx_loc, gate_loc, wg_loc, wu_loc, wd_loc, wsg_loc, wsu_loc, wsd_loc):
        tok_count, d_model = x_loc.shape
        top = idx_loc.shape[1]
        n_local, _, _ = wg_loc.shape
        n_mine = n_local // data_n
        capacity = capacity_of(tok_count, top, n_local * exp_n)
        y = lax.axis_index("data")
        p = lax.axis_index("expert")
        me = p * data_n + y
        wdt_loc = jnp.swapaxes(wd_loc, 1, 2)

        meta = jnp.concatenate([idx_loc.T.astype(F32), gate_loc.T], axis=0)
        meta_all = lax.all_gather(meta, group_axes, axis=0)

        blocks = [None] * n_dev
        blocks[0] = x_loc
        blocks[1] = over_y(x_loc)
        blocks[4] = over_x(x_loc)
        blocks[2] = over_core(x_loc)
        blocks[6] = over_core(blocks[4])
        blocks[3] = over_core(blocks[1])
        blocks[5] = over_x(blocks[1])
        blocks[7] = over_core(blocks[5])

        ws = jnp.stack([wsg_loc, wsu_loc, wsd_loc.T])
        rows_s, width_s = ws.shape[1], ws.shape[2] // n_dev
        ws = ws.reshape(3, rows_s, n_dev, width_s).transpose(2, 0, 1, 3)
        ws = lax.all_to_all(ws, group_axes, 0, 0, tiled=True)
        ws = ws.transpose(1, 0, 2, 3).reshape(3, d_model, width_s)
        wgu_s, wdt_s = jnp.concatenate([ws[0], ws[1]], axis=1), ws[2]

        recvs = []
        start = 0
        for n in CHUNKS:
            at = (1 - y) * n_mine + start
            piece = jnp.stack([lax.dynamic_slice_in_dim(w, at, n, 0) for w in (wg_loc, wu_loc, wdt_loc)])
            recvs.append(over_y(piece))
            start += n

        meta_rel = jnp.take(meta_all, me ^ jnp.arange(n_dev, dtype=jnp.int32), axis=0)
        ids = meta_rel[:, :top].astype(jnp.int32)
        gts = meta_rel[:, top:]
        mine = p * n_local + y * n_mine + jnp.arange(n_mine, dtype=jnp.int32)
        hit = ids[:, None] == mine[None, :, None, None]
        chosen = jnp.any(hit, axis=2).reshape(n_dev * n_mine, tok_count)
        t_ids = jnp.arange(tok_count, dtype=jnp.int32)
        before = (t_ids[:, None] < t_ids[None, :]).astype(BF16)
        rank = jnp.dot(chosen.astype(BF16), before, preferred_element_type=F32).astype(jnp.int32)
        pos = jnp.where(chosen & (rank < capacity), rank, -1)
        pos_pad = jnp.pad(pos.reshape(n_dev, n_mine, tok_count), ((0, 0), (0, TILE), (0, 0)), constant_values=-1)

        last = [pos_pad]

        def after(*vals):
            done, vals = lax.optimization_barrier((last[0], vals))
            last[0] = done
            return vals if len(vals) > 1 else vals[0]

        xg = None

        def gather(r):
            nonlocal xg
            x_blk = after(blocks[r])
            xg = gather_rows(r, n_dev, pos_pad[r], x_blk, xg, capacity)
            last[0] = xg

        base = [None] * n_dev

        def shared(r):
            x_blk = after(blocks[r])
            base[r] = shared_part(x_blk, wgu_s, wdt_s)
            last[0] = base[r]

        y_arr = y.astype(jnp.int32).reshape(1)
        outs = []

        def experts(c):
            start = sum(CHUNKS[:c])
            outs.append(expert_rows(start, CHUNKS[c], y_arr, xg, wg_loc, wu_loc, wdt_loc, after(recvs[c])))
            last[0] = outs[-1]

        lists = []

        def make_lists():
            p_in, ids_in, gts_in = after(pos, ids, gts)
            hit_in = ids_in[:, None] == mine[None, :, None, None]
            gate_of = jnp.sum(jnp.where(hit_in, gts_in[:, None], 0.0), axis=2).reshape(n_dev * n_mine, tok_count)
            same = p_in[:, None, :] == jnp.arange(capacity, dtype=jnp.int32)[None, :, None]
            toks = jnp.sum(jnp.where(same, t_ids[None, None, :] - tok_count, 0), axis=2) + tok_count
            slot_gate = jnp.sum(jnp.where(same, gate_of[:, None, :], 0.0), axis=2)
            count = jnp.sum((p_in >= 0).astype(jnp.int32), axis=1).reshape(n_dev, 1, n_mine)
            toks = (toks * TILE).reshape(n_dev, 1, n_mine * capacity)
            slot_gate = slot_gate.reshape(n_dev, 1, n_mine * capacity)
            lists.extend([count, toks, slot_gate])
            last[0] = (toks, slot_gate)

        def part(r, bases, first, halves):
            count, toks, slot_gate = lists
            c0 = 0
            while sum(CHUNKS[:c0]) < first:
                c0 += 1
            (b0, *rest) = bases
            args = [after(b0), *rest]
            out = combine(r, count[r], toks[r], slot_gate[r], args, outs[c0:], first, halves)
            last[0] = out[0] if halves else out
            return out

        gather(0)
        gather(2)
        gather(1)
        gather(4)
        make_lists()
        gather(3)
        gather(6)
        gather(5)
        gather(7)
        experts(0)
        shared(7)
        shared(5)
        experts(1)
        shared(6)
        shared(4)
        experts(2)
        shared(3)
        n_pre = sum(CHUNKS[:3])
        pre7 = part(7, [base[7]], 0, False)
        pre5 = part(5, [base[5]], 0, False)
        experts(3)
        shared(1)
        experts(4)
        mate7 = over_core(part(7, [pre7], n_pre, False))
        mate6 = over_core(part(6, [base[6]], 0, False))
        diag = part(5, [pre5, mate7], n_pre, True)
        diag_x = over_x(diag[0])
        diag_y = over_y(diag[1])
        to_x = part(4, [base[4], mate6], 0, True)
        x_top = over_x(to_x[0])
        mate3 = over_core(part(3, [base[3]], 0, False))
        shared(2)
        mate2 = over_core(part(2, [base[2]], 0, False))
        to_y = part(1, [base[1], mate3], 0, True)
        y_bot = over_y(to_y[1])
        shared(0)
        own = part(0, [base[0], mate2], 0, True)
        up_x, up_y, to_x1, to_y0 = after(diag_y, diag_x, to_x[1], to_y[0])
        x_bot = over_x(to_x1 + up_x)
        y_top = over_y(to_y0 + up_y)
        h = tok_count // 2
        top_rows = x_loc[:h].astype(F32) + own[0] + x_top + y_top
        bot_rows = x_loc[h:].astype(F32) + own[1] + x_bot + y_bot
        return jnp.concatenate([top_rows.astype(BF16), bot_rows.astype(BF16)], axis=0)

    in_specs = (tok_spec, tok_spec, tok_spec, P("expert", "data", None), P("expert", "data", None), P("expert", None, "data"), P(group_axes, None), P(group_axes, None), P(None, group_axes))
    return jax.shard_map(device_fn, mesh=mesh, in_specs=in_specs, out_specs=tok_spec, check_vma=False)
```

profile of v0, /device:TPU:6, one launch (start us, length us, event | category | flops | bytes accessed | tf_op | source)
XLA Modules:
  0.0 998.1 jit_solution(2715569912783682204)
XLA Ops:
  7.9 1.5 pad_maximum_fusion.7
  9.5 3.7 dynamic-slice_bitcast_fusion
  13.2 5.6 dynamic-slice_bitcast_fusion.1
  18.8 2.0 pad_maximum_fusion.1
  20.8 2.0 collective-permute-start.7
  23.9 2.2 copy.21
  26.1 4.5 all-to-all-start
  30.6 3.6 pad_maximum_fusion.2
  34.7 58.6 %collective-permute-done.1.x_ref = bf16[2048,896]{1,0:T(8,128)(2,1)} collective-permute-done((bf16[2048,896]{1,0:T(8,128)(2,1)}, bf16[2048,896]{1,0:T(8,128)(2,1)}, u32[]{:S(2)}, u32[]{:S(2)}) %collective-permute-start.1) | collective-permute-done | bytes 3670048 | tf_op jit(solution)/shard_map/ppermute | solution.py:274
  93.8 1.3 dynamic-slice_bitcast_fusion.9
  95.2 1.8 dynamic-slice_bitcast_fusion.10
  97.0 1.4 pad_maximum_fusion.5
  98.4 1.5 pad_maximum_fusion.6
  99.9 2.1 pad_maximum_fusion.3
  102.0 2.8 gather_fusion
  104.8 1.4 broadcast_select_fusion
  107.9 1.6 compare_reduce_fusion
  112.4 14.6 %gather_rows.8.refs_0_ = bf16[8,8,320,896]{3,2,1,0:T(8,128)(2,1)} custom-call(s32[16,2048]{1,0:T(8,128)} %get-tuple-element.116.pos_ref, bf16[2048,896]{1,0:T(8,128)(2,1)} %x_ref.1), custom_call_target="tpu_custom_call" | custom-call | flops 146800640 | bytes 4587520 | tf_op jit(solution)/shard_map/gather_rows/pallas_call | solution.py:58
  127.0 76.8 %all-to-all-done = bf16[8,3,112,640]{3,2,1,0:T(8,128)(2,1)S(1)} async-done(((bf16[8,3,112,640]{3,2,1,0:T(8,128)(2,1)}), bf16[8,3,112,640]{3,2,1,0:T(8,128)(2,1)S(1)}, u32[]{:S(2)}, u32[]{:S(2)}) %all-to-all-start) | async-done | bytes 3440672 | tf_op jit(solution)/shard_map/all_to_all | solution.py:309
  203.8 1.4 fusion.15
  205.1 1.5 pad_maximum_fusion.4.wgu_ref
  206.7 14.6 %gather_rows.9.refs_0_ = bf16[8,8,320,896]{3,2,1,0:T(8,128)(2,1)} custom-call(s32[16,2048]{1,0:T(8,128)} %get-tuple-element.115.pos_ref, bf16[2048,896]{1,0:T(8,128)(2,1)} %collective-permute-done.x_ref, bf16[8,8,320,896]{3,2,1,0:T(8,128)(2,1)} %gather_rows.8.refs_0_), custom_call_target="tpu_custom_call", output_to_operand_aliasing={{}: (2, {})} | custom-call | flops 146800640 | bytes 4587520 | tf_op jit(solution)/shard_map/gather_rows/pallas_call | solution.py:58
  221.3 14.7 %gather_rows.10.refs_0_ = bf16[8,8,320,896]{3,2,1,0:T(8,128)(2,1)} custom-call(s32[16,2048]{1,0:T(8,128)} %get-tuple-element.114.pos_ref, bf16[2048,896]{1,0:T(8,128)(2,1)} %collective-permute-done.1.x_ref, bf16[8,8,320,896]{3,2,1,0:T(8,128)(2,1)} %gather_rows.9.refs_0_), custom_call_target="tpu_custom_call", output_to_operand_aliasing={{}: (2, {})} | custom-call | flops 146800640 | bytes 4587520 | tf_op jit(solution)/shard_map/gather_rows/pallas_call | solution.py:58
  236.0 15.0 %gather_rows.11.refs_0_ = bf16[8,8,320,896]{3,2,1,0:T(8,128)(2,1)} custom-call(s32[16,2048]{1,0:T(8,128)} %get-tuple-element.120.pos_ref, bf16[2048,896]{1,0:T(8,128)(2,1)} %collective-permute-done.2.x_ref, bf16[8,8,320,896]{3,2,1,0:T(8,128)(2,1)} %gather_rows.10.refs_0_), custom_call_target="tpu_custom_call", output_to_operand_aliasing={{}: (2, {})} | custom-call | flops 146800640 | bytes 4587520 | tf_op jit(solution)/shard_map/gather_rows/pallas_call | solution.py:58
  251.5 1.3 select_reduce_fusion.2
  252.9 30.6 %select_reduce_fusion = f32[64,320]{1,0:T(8,128)S(1)} fusion(f32[64,2048]{1,0:T(8,128)S(1)} %bitcast.126, s32[64,2048]{1,0:T(8,128)S(1)} %copy-done.1), kind=kLoop, calls=%fused_computation.1 | loop fusion | flops 125808640 | bytes 1130496 | tf_op jit(solution)/shard_map/reduce_sum | solution.py:371
  284.3 1.3 collective-permute-start.10
  286.3 30.7 %select_reduce_fusion.1 = s32[64,320]{1,0:T(8,128)S(1)} fusion(s32[2048]{0:T(1024)S(1)} %iota_add_fusion, s32[64,2048]{1,0:T(8,128)S(1)} %copy-done.1), kind=kLoop, calls=%fused_computation.2 | loop fusion | flops 125808640 | bytes 614400 | tf_op jit(solution)/shard_map/reduce_sum | solution.py:370
  323.2 14.7 %gather_rows.12.refs_0_ = bf16[8,8,320,896]{3,2,1,0:T(8,128)(2,1)} custom-call(s32[16,2048]{1,0:T(8,128)} %get-tuple-element.113.pos_ref, bf16[2048,896]{1,0:T(8,128)(2,1)} %collective-permute-done.3.x_ref, bf16[8,8,320,896]{3,2,1,0:T(8,128)(2,1)} %gather_rows.11.refs_0_), custom_call_target="tpu_custom_call", output_to_operand_aliasing={{}: (2, {})} | custom-call | flops 146800640 | bytes 4587520 | tf_op jit(solution)/shard_map/gather_rows/pallas_call | solution.py:58
  337.9 14.7 %gather_rows.13.refs_0_ = bf16[8,8,320,896]{3,2,1,0:T(8,128)(2,1)} custom-call(s32[16,2048]{1,0:T(8,128)} %get-tuple-element.119.pos_ref, bf16[2048,896]{1,0:T(8,128)(2,1)} %collective-permute-done.4.x_ref, bf16[8,8,320,896]{3,2,1,0:T(8,128)(2,1)} %gather_rows.12.refs_0_), custom_call_target="tpu_custom_call", output_to_operand_aliasing={{}: (2, {})} | custom-call | flops 146800640 | bytes 4587520 | tf_op jit(solution)/shard_map/gather_rows/pallas_call | solution.py:58
  352.5 14.6 %gather_rows.14.refs_0_ = bf16[8,8,320,896]{3,2,1,0:T(8,128)(2,1)} custom-call(s32[16,2048]{1,0:T(8,128)} %get-tuple-element.118.pos_ref, bf16[2048,896]{1,0:T(8,128)(2,1)} %collective-permute-done.5.x_ref, bf16[8,8,320,896]{3,2,1,0:T(8,128)(2,1)} %gather_rows.13.refs_0_), custom_call_target="tpu_custom_call", output_to_operand_aliasing={{}: (2, {})} | custom-call | flops 146800640 | bytes 4587520 | tf_op jit(solution)/shard_map/gather_rows/pallas_call | solution.py:58
  367.1 14.6 %gather_rows.15.xg_ref = bf16[8,8,320,896]{3,2,1,0:T(8,128)(2,1)} custom-call(s32[16,2048]{1,0:T(8,128)} %get-tuple-element.117.pos_ref, bf16[2048,896]{1,0:T(8,128)(2,1)} %collective-permute-done.6.x_ref, bf16[8,8,320,896]{3,2,1,0:T(8,128)(2,1)} %gather_rows.14.refs_0_), custom_call_target="tpu_custom_call", output_to_operand_aliasing={{}: (2, {})} | custom-call | flops 146800640 | bytes 4587520 | tf_op jit(solution)/shard_map/gather_rows/pallas_call | solution.py:58
  381.8 32.1 %expert_rows.5.refs_4_.refs_5_ = bf16[2,8,320,896]{3,2,1,0:T(8,128)(2,1)} custom-call(s32[1]{0:T(128)} %bitcast.19.y_ref, bf16[8,8,320,896]{3,2,1,0:T(8,128)(2,1)} %gather_rows.15.xg_ref, bf16[16,448,640]{2,1,0:T(8,128)(2,1)} %og_ref.9, bf16[16,448,640]{2,1,0:T(8,128)(2,1)} %ou_ref.9, bf16[16,448,640]{2,1,0:T(8,128)(2,1)} %bitcast.106, ...), custom_call_target="tpu_custom_call" | custom-call | flops 275251200 | bytes 18350080 | tf_op jit(solution)/shard_map/expert_rows/pallas_call | solution.py:104
  413.9 14.6 %shared_part.8.refs_3_ = f32[2048,896]{1,0:T(8,128)} custom-call(bf16[2048,896]{1,0:T(8,128)(2,1)} %collective-permute-done.6.x_ref, bf16[896,1280]{1,0:T(8,128)(2,1)} %pad_maximum_fusion.4.wgu_ref, bf16[896,640]{1,0:T(8,128)(2,1)} %bitcast.111), custom_call_target="tpu_custom_call" | custom-call | flops 110100480 | bytes 11010048 | tf_op jit(solution)/shard_map/shared_part/pallas_call | solution.py:133
  428.5 14.6 %shared_part.9.refs_3_ = f32[2048,896]{1,0:T(8,128)} custom-call(bf16[2048,896]{1,0:T(8,128)(2,1)} %collective-permute-done.5.x_ref, bf16[896,1280]{1,0:T(8,128)(2,1)} %pad_maximum_fusion.4.wgu_ref, bf16[896,640]{1,0:T(8,128)(2,1)} %bitcast.112), custom_call_target="tpu_custom_call" | custom-call | flops 110100480 | bytes 11010048 | tf_op jit(solution)/shard_map/shared_part/pallas_call | solution.py:133
  443.1 31.7 %expert_rows.6.refs_5_.refs_6_ = bf16[2,8,320,896]{3,2,1,0:T(8,128)(2,1)} custom-call(s32[1]{0:T(128)} %bitcast.19.y_ref, bf16[8,8,320,896]{3,2,1,0:T(8,128)(2,1)} %gather_rows.15.xg_ref, bf16[16,448,640]{2,1,0:T(8,128)(2,1)} %og_ref.9, bf16[16,448,640]{2,1,0:T(8,128)(2,1)} %ou_ref.9, bf16[16,448,640]{2,1,0:T(8,128)(2,1)} %bitcast.107, ...), custom_call_target="tpu_custom_call" | custom-call | flops 275251200 | bytes 18350080 | tf_op jit(solution)/shard_map/expert_rows/pallas_call | solution.py:104
  474.9 14.6 %shared_part.10.refs_3_ = f32[2048,896]{1,0:T(8,128)} custom-call(bf16[2048,896]{1,0:T(8,128)(2,1)} %collective-permute-done.4.x_ref, bf16[896,1280]{1,0:T(8,128)(2,1)} %pad_maximum_fusion.4.wgu_ref, bf16[896,640]{1,0:T(8,128)(2,1)} %bitcast.113), custom_call_target="tpu_custom_call" | custom-call | flops 110100480 | bytes 11010048 | tf_op jit(solution)/shard_map/shared_part/pallas_call | solution.py:133
  489.4 14.8 %shared_part.11.refs_3_ = f32[2048,896]{1,0:T(8,128)} custom-call(bf16[2048,896]{1,0:T(8,128)(2,1)} %collective-permute-done.2.x_ref, bf16[896,1280]{1,0:T(8,128)(2,1)} %pad_maximum_fusion.4.wgu_ref, bf16[896,640]{1,0:T(8,128)(2,1)} %bitcast.114), custom_call_target="tpu_custom_call" | custom-call | flops 110100480 | bytes 11010048 | tf_op jit(solution)/shard_map/shared_part/pallas_call | solution.py:133
  504.2 31.8 %expert_rows.7.refs_6_.refs_7_ = bf16[2,8,320,896]{3,2,1,0:T(8,128)(2,1)} custom-call(s32[1]{0:T(128)} %bitcast.19.y_ref, bf16[8,8,320,896]{3,2,1,0:T(8,128)(2,1)} %gather_rows.15.xg_ref, bf16[16,448,640]{2,1,0:T(8,128)(2,1)} %og_ref.9, bf16[16,448,640]{2,1,0:T(8,128)(2,1)} %ou_ref.9, bf16[16,448,640]{2,1,0:T(8,128)(2,1)} %bitcast.108, ...), custom_call_target="tpu_custom_call" | custom-call | flops 275251200 | bytes 18350080 | tf_op jit(solution)/shard_map/expert_rows/pallas_call | solution.py:104
  536.0 14.6 %shared_part.12.refs_3_ = f32[2048,896]{1,0:T(8,128)} custom-call(bf16[2048,896]{1,0:T(8,128)(2,1)} %collective-permute-done.3.x_ref, bf16[896,1280]{1,0:T(8,128)(2,1)} %pad_maximum_fusion.4.wgu_ref, bf16[896,640]{1,0:T(8,128)(2,1)} %bitcast.115), custom_call_target="tpu_custom_call" | custom-call | flops 110100480 | bytes 11010048 | tf_op jit(solution)/shard_map/shared_part/pallas_call | solution.py:133
  550.6 13.8 %combine.10.refs_3_ = f32[2048,896]{1,0:T(8,128)} custom-call(s32[1,8]{1,0:T(1,128)} %get-tuple-element.138.refs_0_, s32[1,2560]{1,0:T(1,128)} %squeeze.137.refs_1_, f32[1,2560]{1,0:T(1,128)} %squeeze.138.refs_2_, f32[2048,896]{1,0:T(8,128)} %shared_part.8.refs_3_, bf16[2,8,320,896]{3,2,1,0:T(8,128)(2,1)} %expert_rows.5.refs_4_.refs_5_, ...), custom_call_target="tpu_custom_call" | custom-call | flops 55050240 | bytes 14680064 | tf_op jit(solution)/shard_map/combine/pallas_call | solution.py:245
  564.4 13.9 %combine.11.refs_3_ = f32[2048,896]{1,0:T(8,128)} custom-call(s32[1,8]{1,0:T(1,128)} %get-tuple-element.140.refs_0_, s32[1,2560]{1,0:T(1,128)} %squeeze.131.refs_1_, f32[1,2560]{1,0:T(1,128)} %squeeze.132.refs_2_, f32[2048,896]{1,0:T(8,128)} %shared_part.9.refs_3_, bf16[2,8,320,896]{3,2,1,0:T(8,128)(2,1)} %expert_rows.5.refs_4_.refs_5_, ...), custom_call_target="tpu_custom_call" | custom-call | flops 55050240 | bytes 14680064 | tf_op jit(solution)/shard_map/combine/pallas_call | solution.py:245
  578.4 17.3 %expert_rows.8.refs_4_.refs_7_.refs_5_.refs_8_ = bf16[1,8,320,896]{3,2,1,0:T(8,128)(2,1)} custom-call(s32[1]{0:T(128)} %bitcast.19.y_ref, bf16[8,8,320,896]{3,2,1,0:T(8,128)(2,1)} %gather_rows.15.xg_ref, bf16[16,448,640]{2,1,0:T(8,128)(2,1)} %og_ref.9, bf16[16,448,640]{2,1,0:T(8,128)(2,1)} %ou_ref.9, bf16[16,448,640]{2,1,0:T(8,128)(2,1)} %bitcast.109, ...), custom_call_target="tpu_custom_call" | custom-call | flops 137625600 | bytes 9175040 | tf_op jit(solution)/shard_map/expert_rows/pallas_call | solution.py:104
  595.7 14.6 %shared_part.13.refs_3_ = f32[2048,896]{1,0:T(8,128)} custom-call(bf16[2048,896]{1,0:T(8,128)(2,1)} %collective-permute-done.1.x_ref, bf16[896,1280]{1,0:T(8,128)(2,1)} %pad_maximum_fusion.4.wgu_ref, bf16[896,640]{1,0:T(8,128)(2,1)} %bitcast.116), custom_call_target="tpu_custom_call" | custom-call | flops 110100480 | bytes 11010048 | tf_op jit(solution)/shard_map/shared_part/pallas_call | solution.py:133
  610.3 17.3 %expert_rows.9.refs_5_.refs_8_.refs_6_.refs_9_ = bf16[1,8,320,896]{3,2,1,0:T(8,128)(2,1)} custom-call(s32[1]{0:T(128)} %bitcast.19.y_ref, bf16[8,8,320,896]{3,2,1,0:T(8,128)(2,1)} %gather_rows.15.xg_ref, bf16[16,448,640]{2,1,0:T(8,128)(2,1)} %og_ref.9, bf16[16,448,640]{2,1,0:T(8,128)(2,1)} %ou_ref.9, bf16[16,448,640]{2,1,0:T(8,128)(2,1)} %bitcast.110, ...), custom_call_target="tpu_custom_call" | custom-call | flops 137625600 | bytes 9175040 | tf_op jit(solution)/shard_map/expert_rows/pallas_call | solution.py:104
  627.6 8.9 combine.12
  636.6 15.8 %combine.13 = f32[2048,896]{1,0:T(8,128)} custom-call(s32[1,8]{1,0:T(1,128)} %get-tuple-element.139.refs_0_, s32[1,2560]{1,0:T(1,128)} %squeeze.134.refs_1_, f32[1,2560]{1,0:T(1,128)} %squeeze.135.refs_2_, f32[2048,896]{1,0:T(8,128)} %shared_part.10.refs_3_, bf16[2,8,320,896]{3,2,1,0:T(8,128)(2,1)} %expert_rows.5.refs_4_.refs_5_, ...), custom_call_target="tpu_custom_call" | custom-call | flops 73400320 | bytes 14680064 | tf_op jit(solution)/shard_map/combine/pallas_call | solution.py:245
  656.0 12.0 %combine.14 = (f32[1024,896]{1,0:T(8,128)}, f32[1024,896]{1,0:T(8,128)}) custom-call(s32[1,8]{1,0:T(1,128)} %get-tuple-element.140.refs_0_, s32[1,2560]{1,0:T(1,128)} %squeeze.131.refs_1_, f32[1,2560]{1,0:T(1,128)} %squeeze.132.refs_2_, f32[2048,896]{1,0:T(8,128)} %combine.11.refs_3_, f32[2048,896]{1,0:T(8,128)} %collective-permute-done.12.refs_4_, ...), custom_call_target="tpu_custom_call" | custom-call | flops 18350080 | bytes 14680064 | tf_op jit(solution)/shard_map/combine/pallas_call | solution.py:245
  668.0 18.1 %combine.15 = (f32[1024,896]{1,0:T(8,128)}, f32[1024,896]{1,0:T(8,128)}) custom-call(s32[1,8]{1,0:T(1,128)} %get-tuple-element.141.refs_0_, s32[1,2560]{1,0:T(1,128)} %squeeze.128.refs_1_, f32[1,2560]{1,0:T(1,128)} %squeeze.129.refs_2_, f32[2048,896]{1,0:T(8,128)} %shared_part.11.refs_3_, f32[2048,896]{1,0:T(8,128)} %collective-permute-done.13.refs_4_, ...), custom_call_target="tpu_custom_call" | custom-call | flops 73400320 | bytes 14680064 | tf_op jit(solution)/shard_map/combine/pallas_call | solution.py:245
  686.1 15.8 %combine.16 = f32[2048,896]{1,0:T(8,128)} custom-call(s32[1,8]{1,0:T(1,128)} %get-tuple-element.142.refs_0_, s32[1,2560]{1,0:T(1,128)} %squeeze.125.refs_1_, f32[1,2560]{1,0:T(1,128)} %squeeze.126.refs_2_, f32[2048,896]{1,0:T(8,128)} %shared_part.12.refs_3_, bf16[2,8,320,896]{3,2,1,0:T(8,128)(2,1)} %expert_rows.5.refs_4_.refs_5_, ...), custom_call_target="tpu_custom_call" | custom-call | flops 73400320 | bytes 14680064 | tf_op jit(solution)/shard_map/combine/pallas_call | solution.py:245
  702.9 14.6 %shared_part.14.refs_3_ = f32[2048,896]{1,0:T(8,128)} custom-call(bf16[2048,896]{1,0:T(8,128)(2,1)} %collective-permute-done.x_ref, bf16[896,1280]{1,0:T(8,128)(2,1)} %pad_maximum_fusion.4.wgu_ref, bf16[896,640]{1,0:T(8,128)(2,1)} %bitcast.117), custom_call_target="tpu_custom_call" | custom-call | flops 110100480 | bytes 11010048 | tf_op jit(solution)/shard_map/shared_part/pallas_call | solution.py:133
  717.5 15.4 %combine.17 = f32[2048,896]{1,0:T(8,128)} custom-call(s32[1,8]{1,0:T(1,128)} %get-tuple-element.143.refs_0_, s32[1,2560]{1,0:T(1,128)} %squeeze.122.refs_1_, f32[1,2560]{1,0:T(1,128)} %squeeze.123.refs_2_, f32[2048,896]{1,0:T(8,128)} %shared_part.14.refs_3_, bf16[2,8,320,896]{3,2,1,0:T(8,128)(2,1)} %expert_rows.5.refs_4_.refs_5_, ...), custom_call_target="tpu_custom_call" | custom-call | flops 73400320 | bytes 14680064 | tf_op jit(solution)/shard_map/combine/pallas_call | solution.py:245
  738.4 1.3 collective-permute-start.16
  739.7 18.2 %combine.18 = (f32[1024,896]{1,0:T(8,128)}, f32[1024,896]{1,0:T(8,128)}) custom-call(s32[1,8]{1,0:T(1,128)} %get-tuple-element.144.refs_0_, s32[1,2560]{1,0:T(1,128)} %squeeze.119.refs_1_, f32[1,2560]{1,0:T(1,128)} %squeeze.120.refs_2_, f32[2048,896]{1,0:T(8,128)} %shared_part.13.refs_3_, f32[2048,896]{1,0:T(8,128)} %collective-permute-done.14.refs_4_, ...), custom_call_target="tpu_custom_call" | custom-call | flops 73400320 | bytes 14680064 | tf_op jit(solution)/shard_map/combine/pallas_call | solution.py:245
  757.8 14.6 %shared_part.15.refs_3_ = f32[2048,896]{1,0:T(8,128)} custom-call(bf16[2048,896]{1,0:T(8,128)(2,1)} %x_ref.1, bf16[896,1280]{1,0:T(8,128)(2,1)} %pad_maximum_fusion.4.wgu_ref, bf16[896,640]{1,0:T(8,128)(2,1)} %bitcast.118), custom_call_target="tpu_custom_call" | custom-call | flops 110100480 | bytes 11010048 | tf_op jit(solution)/shard_map/shared_part/pallas_call | solution.py:133
  772.4 17.9 %combine.19 = (f32[1024,896]{1,0:T(8,128)}, f32[1024,896]{1,0:T(8,128)}) custom-call(s32[1,8]{1,0:T(1,128)} %get-tuple-element.137.refs_0_, s32[1,2560]{1,0:T(1,128)} %squeeze.116.refs_1_, f32[1,2560]{1,0:T(1,128)} %squeeze.117.refs_2_, f32[2048,896]{1,0:T(8,128)} %shared_part.15.refs_3_, f32[2048,896]{1,0:T(8,128)} %collective-permute-done.15.refs_4_, ...), custom_call_target="tpu_custom_call" | custom-call | flops 73400320 | bytes 14680064 | tf_op jit(solution)/shard_map/combine/pallas_call | solution.py:245
  790.4 25.1 %collective-permute-done.17 = f32[1024,896]{1,0:T(8,128)} collective-permute-done((f32[1024,896]{1,0:T(8,128)}, f32[1024,896]{1,0:T(8,128)}, u32[]{:S(2)}, u32[]{:S(2)}) %collective-permute-start.17) | collective-permute-done | bytes 3670048 | tf_op jit(solution)/shard_map/ppermute | solution.py:274
  815.4 2.0 collective-permute-done.18
  817.5 4.5 add.133
  823.9 4.2 add.136
  828.9 67.2 %collective-permute-done.16 = f32[1024,896]{1,0:T(8,128)} collective-permute-done((f32[1024,896]{1,0:T(8,128)}, f32[1024,896]{1,0:T(8,128)}, u32[]{:S(2)}, u32[]{:S(2)}) %collective-permute-start.16) | collective-permute-done | bytes 3670048 | tf_op jit(solution)/shard_map/ppermute | solution.py:280
  896.1 8.3 collective-permute-done.19
  904.4 75.7 %collective-permute-done.21 = f32[1024,896]{1,0:T(8,128)} collective-permute-done((f32[1024,896]{1,0:T(8,128)}, f32[1024,896]{1,0:T(8,128)}, u32[]{:S(2)}, u32[]{:S(2)}) %collective-permute-start.21) | collective-permute-done | bytes 3670048 | tf_op jit(solution)/shard_map/ppermute | solution.py:274
  980.1 10.9 %add_convert_fusion.1 = (bf16[2048,896]{1,0:T(8,128)(2,1)}, bf16[2048,896]{1,0:T(8,128)(2,1)}) fusion(f32[1024,896]{1,0:T(8,128)} %collective-permute-done.19, f32[1024,896]{1,0:T(8,128)} %collective-permute-done.16, f32[1024,896]{1,0:T(8,128)} %get-tuple-element.82, bf16[2048,896]{1,0:T(8,128)(2,1)} %x_ref.1, ...), kind=kLoop, output_to_operand_aliasing={{0}: (7, {}), {1}: (7, {})}, calls=%fused_computation.10 | loop fusion | flops 9175040 | bytes 29360128 | tf_op jit(solution)/shard_map/convert_element_type | solution.py:432
  (119 shorter events, 29.2 us)
Async XLA Ops:
  6.5 95.4 %all-gather.3.cloned.1.call-start = ((), (), s32[]{:S(2)}) async-start(), calls=%async_computation.1 | async-start | bytes 1179648 | tf_op jit(solution)/shard_map/all_gather | solution.py:294
  6.5 86.7 %collective-permute-start.1 = (bf16[2048,896]{1,0:T(8,128)(2,1)}, bf16[2048,896]{1,0:T(8,128)(2,1)}, u32[]{:S(2)}, u32[]{:S(2)}) collective-permute-start(bf16[2048,896]{1,0:T(8,128)(2,1)} %x_ref.1), channel_id=1, source_target_pairs={{0,4},{4,0},{1,5},{5,1},{2,6},{6,2},{3,7},{7,3}} | collective-permute-start | bytes 11010056 | tf_op jit(solution)/shard_map/ppermute | solution.py:274
  7.0 199.6 %collective-permute-start = (bf16[2048,896]{1,0:T(8,128)(2,1)}, bf16[2048,896]{1,0:T(8,128)(2,1)}, u32[]{:S(2)}, u32[]{:S(2)}) collective-permute-start(bf16[2048,896]{1,0:T(8,128)(2,1)} %x_ref.1), channel_id=1, source_target_pairs={{0,1},{1,0},{2,3},{3,2},{4,5},{5,4},{6,7},{7,6}} | collective-permute-start | bytes 11010056 | tf_op jit(solution)/shard_map/ppermute | solution.py:277
  7.0 228.9 %collective-permute-start.2 = (bf16[2048,896]{1,0:T(8,128)(2,1)}, bf16[2048,896]{1,0:T(8,128)(2,1)}, u32[]{:S(2)}, u32[]{:S(2)}) collective-permute-start(bf16[2048,896]{1,0:T(8,128)(2,1)} %x_ref.1), channel_id=1, source_target_pairs={{0,2},{1,3},{2,0},{3,1},{4,6},{5,7},{6,4},{7,5}} | collective-permute-start | bytes 11010056 | tf_op jit(solution)/shard_map/ppermute | solution.py:280
  18.8 4.1 copy-start.10
  18.8 4.2 copy-start.11
  20.8 2.4 copy-start.12
  20.8 361.0 %collective-permute-start.7 = (bf16[3,2,448,640]{3,2,1,0:T(8,128)(2,1)}, bf16[3,2,448,640]{3,2,1,0:T(8,128)(2,1)}, u32[]{:S(2)}, u32[]{:S(2)}) collective-permute-start(bf16[3,2,448,640]{3,2,1,0:T(8,128)(2,1)} %pad_maximum_fusion.1), channel_id=1, source_target_pairs={{0,4},{4,0},{1,5},{5,1},{2,6},{6,2},{3,7},{7,3}} | collective-permute-start | bytes 10321928 | tf_op jit(solution)/shard_map/ppermute | solution.py:274
  26.1 177.7 %all-to-all-start = ((bf16[8,3,112,640]{3,2,1,0:T(8,128)(2,1)}), bf16[8,3,112,640]{3,2,1,0:T(8,128)(2,1)S(1)}, u32[]{:S(2)}, u32[]{:S(2)}) async-start(bf16[8,3,112,640]{3,2,1,0:T(8,128)(2,1)} %copy.21), calls=%async_computation | async-start | bytes 6881280 | tf_op jit(solution)/shard_map/all_to_all | solution.py:309
  34.1 409.0 %collective-permute-start.8 = (bf16[3,2,448,640]{3,2,1,0:T(8,128)(2,1)}, bf16[3,2,448,640]{3,2,1,0:T(8,128)(2,1)}, u32[]{:S(2)}, u32[]{:S(2)}) collective-permute-start(bf16[3,2,448,640]{3,2,1,0:T(8,128)(2,1)} %pad_maximum_fusion.2), channel_id=1, source_target_pairs={{0,4},{4,0},{1,5},{5,1},{2,6},{6,2},{3,7},{7,3}} | collective-permute-start | bytes 10321928 | tf_op jit(solution)/shard_map/ppermute | solution.py:274
  93.3 159.6 %collective-permute-start.5 = (bf16[2048,896]{1,0:T(8,128)(2,1)}, bf16[2048,896]{1,0:T(8,128)(2,1)}, u32[]{:S(2)}, u32[]{:S(2)}) collective-permute-start(bf16[2048,896]{1,0:T(8,128)(2,1)} %collective-permute-done.1.x_ref), channel_id=1, source_target_pairs={{0,2},{1,3},{2,0},{3,1},{4,6},{5,7},{6,4},{7,5}} | collective-permute-start | bytes 11010056 | tf_op jit(solution)/shard_map/ppermute | solution.py:280
  96.9 3.0 copy-start.4
  97.0 2.9 copy-start.5
  97.0 2.9 copy-start.6
  107.1 0.8 copy-start.2
  110.6 0.8 copy-start
  236.0 15.5 %copy-start.3 = (s32[8,8,2048]{2,1,0:T(8,128)S(1)}, s32[8,8,2048]{2,1,0:T(8,128)}, u32[]{:S(2)}) copy-start(s32[8,8,2048]{2,1,0:T(8,128)} %copy-done.2) | copy-start | bytes 1572868
  236.0 15.5 %copy-start.9 = (f32[8,8,2048]{2,1,0:T(8,128)S(1)}, f32[8,8,2048]{2,1,0:T(8,128)}, u32[]{:S(2)}) copy-start(f32[8,8,2048]{2,1,0:T(8,128)} %get-tuple-element.54) | copy-start | bytes 1572868
  236.0 16.9 %copy-start.1 = (s32[64,2048]{1,0:T(8,128)S(1)}, s32[64,2048]{1,0:T(8,128)}, u32[]{:S(2)}) copy-start(s32[64,2048]{1,0:T(8,128)} %copy-done) | copy-start | bytes 1572868
  251.0 32.6 %collective-permute-start.3 = (bf16[2048,896]{1,0:T(8,128)(2,1)}, bf16[2048,896]{1,0:T(8,128)(2,1)}, u32[]{:S(2)}, u32[]{:S(2)}) collective-permute-start(bf16[2048,896]{1,0:T(8,128)(2,1)} %collective-permute-done.1.x_ref), channel_id=1, source_target_pairs={{0,1},{1,0},{2,3},{3,2},{4,5},{5,4},{6,7},{7,6}} | collective-permute-start | bytes 11010056 | tf_op jit(solution)/shard_map/ppermute | solution.py:277
  251.0 33.3 %collective-permute-start.4 = (bf16[2048,896]{1,0:T(8,128)(2,1)}, bf16[2048,896]{1,0:T(8,128)(2,1)}, u32[]{:S(2)}, u32[]{:S(2)}) collective-permute-start(bf16[2048,896]{1,0:T(8,128)(2,1)} %collective-permute-done.2.x_ref), channel_id=1, source_target_pairs={{0,1},{1,0},{2,3},{3,2},{4,5},{5,4},{6,7},{7,6}} | collective-permute-start | bytes 11010056 | tf_op jit(solution)/shard_map/ppermute | solution.py:277
  252.9 32.8 %collective-permute-start.6 = (bf16[2048,896]{1,0:T(8,128)(2,1)}, bf16[2048,896]{1,0:T(8,128)(2,1)}, u32[]{:S(2)}, u32[]{:S(2)}) collective-permute-start(bf16[2048,896]{1,0:T(8,128)(2,1)} %collective-permute-done.5.x_ref), channel_id=1, source_target_pairs={{0,1},{1,0},{2,3},{3,2},{4,5},{5,4},{6,7},{7,6}} | collective-permute-start | bytes 11010056 | tf_op jit(solution)/shard_map/ppermute | solution.py:277
  283.6 220.7 %collective-permute-start.9 = (bf16[3,2,448,640]{3,2,1,0:T(8,128)(2,1)}, bf16[3,2,448,640]{3,2,1,0:T(8,128)(2,1)}, u32[]{:S(2)}, u32[]{:S(2)}) collective-permute-start(bf16[3,2,448,640]{3,2,1,0:T(8,128)(2,1)} %pad_maximum_fusion.3), channel_id=1, source_target_pairs={{0,4},{4,0},{1,5},{5,1},{2,6},{6,2},{3,7},{7,3}} | collective-permute-start | bytes 10321928 | tf_op jit(solution)/shard_map/ppermute | solution.py:274
  284.3 294.1 %collective-permute-start.10 = (bf16[3,1,448,640]{3,2,1,0:T(8,128)(2,1)}, bf16[3,1,448,640]{3,2,1,0:T(8,128)(2,1)}, u32[]{:S(2)}, u32[]{:S(2)}) collective-permute-start(bf16[3,1,448,640]{3,2,1,0:T(8,128)(2,1)} %pad_maximum_fusion.5), channel_id=1, source_target_pairs={{0,4},{4,0},{1,5},{5,1},{2,6},{6,2},{3,7},{7,3}} | collective-permute-start | bytes 5160968 | tf_op jit(solution)/shard_map/ppermute | solution.py:274
  285.6 324.7 %collective-permute-start.11 = (bf16[3,1,448,640]{3,2,1,0:T(8,128)(2,1)}, bf16[3,1,448,640]{3,2,1,0:T(8,128)(2,1)}, u32[]{:S(2)}, u32[]{:S(2)}) collective-permute-start(bf16[3,1,448,640]{3,2,1,0:T(8,128)(2,1)} %pad_maximum_fusion.6), channel_id=1, source_target_pairs={{0,4},{4,0},{1,5},{5,1},{2,6},{6,2},{3,7},{7,3}} | collective-permute-start | bytes 5160968 | tf_op jit(solution)/shard_map/ppermute | solution.py:274
  636.5 19.5 %collective-permute-start.12 = (f32[2048,896]{1,0:T(8,128)}, f32[2048,896]{1,0:T(8,128)}, u32[]{:S(2)}, u32[]{:S(2)}) collective-permute-start(f32[2048,896]{1,0:T(8,128)} %combine.12), channel_id=1, source_target_pairs={{0,1},{1,0},{2,3},{3,2},{4,5},{5,4},{6,7},{7,6}} | collective-permute-start | bytes 22020104 | tf_op jit(solution)/shard_map/ppermute | solution.py:277
  636.6 16.1 %copy-start.20 = (s32[8,320]{1,0:T(8,128)S(1)}, s32[8,320]{1,0:T(8,128)}, u32[]{:S(2)}) copy-start(s32[8,320]{1,0:T(8,128)} %get-tuple-element.135) | copy-start | bytes 30724
  636.6 16.7 %copy-start.19 = (s32[8,320]{1,0:T(8,128)S(1)}, s32[8,320]{1,0:T(8,128)}, u32[]{:S(2)}) copy-start(s32[8,320]{1,0:T(8,128)} %get-tuple-element.134) | copy-start | bytes 30724
  636.6 17.4 %copy-start.22 = (f32[8,320]{1,0:T(8,128)S(1)}, f32[8,320]{1,0:T(8,128)}, u32[]{:S(2)}) copy-start(f32[8,320]{1,0:T(8,128)} %get-tuple-element.126) | copy-start | bytes 30724
  636.6 18.1 %copy-start.18 = (s32[8,320]{1,0:T(8,128)S(1)}, s32[8,320]{1,0:T(8,128)}, u32[]{:S(2)}) copy-start(s32[8,320]{1,0:T(8,128)} %get-tuple-element.133) | copy-start | bytes 30724
  636.6 18.7 %copy-start.21 = (f32[8,320]{1,0:T(8,128)S(1)}, f32[8,320]{1,0:T(8,128)}, u32[]{:S(2)}) copy-start(f32[8,320]{1,0:T(8,128)} %get-tuple-element.125) | copy-start | bytes 30724
  652.4 15.6 %collective-permute-start.13 = (f32[2048,896]{1,0:T(8,128)}, f32[2048,896]{1,0:T(8,128)}, u32[]{:S(2)}, u32[]{:S(2)}) collective-permute-start(f32[2048,896]{1,0:T(8,128)} %combine.13), channel_id=1, source_target_pairs={{0,1},{1,0},{2,3},{3,2},{4,5},{5,4},{6,7},{7,6}} | collective-permute-start | bytes 22020104 | tf_op jit(solution)/shard_map/ppermute | solution.py:277
  686.1 16.1 %copy-start.17 = (f32[8,320]{1,0:T(8,128)S(1)}, f32[8,320]{1,0:T(8,128)}, u32[]{:S(2)}) copy-start(f32[8,320]{1,0:T(8,128)} %get-tuple-element.127) | copy-start | bytes 30724
  702.0 37.7 %collective-permute-start.14 = (f32[2048,896]{1,0:T(8,128)}, f32[2048,896]{1,0:T(8,128)}, u32[]{:S(2)}, u32[]{:S(2)}) collective-permute-start(f32[2048,896]{1,0:T(8,128)} %combine.16), channel_id=1, source_target_pairs={{0,1},{1,0},{2,3},{3,2},{4,5},{5,4},{6,7},{7,6}} | collective-permute-start | bytes 22020104 | tf_op jit(solution)/shard_map/ppermute | solution.py:277
  717.5 18.2 %copy-start.14 = (s32[8,320]{1,0:T(8,128)S(1)}, s32[8,320]{1,0:T(8,128)}, u32[]{:S(2)}) copy-start(s32[8,320]{1,0:T(8,128)} %get-tuple-element.129) | copy-start | bytes 30724
  717.5 18.9 %copy-start.16 = (f32[8,320]{1,0:T(8,128)S(1)}, f32[8,320]{1,0:T(8,128)}, u32[]{:S(2)}) copy-start(f32[8,320]{1,0:T(8,128)} %get-tuple-element.121) | copy-start | bytes 30724
  717.5 19.6 %copy-start.13 = (s32[8,320]{1,0:T(8,128)S(1)}, s32[8,320]{1,0:T(8,128)}, u32[]{:S(2)}) copy-start(s32[8,320]{1,0:T(8,128)} %get-tuple-element.136) | copy-start | bytes 30724
  717.5 20.2 %copy-start.15 = (f32[8,320]{1,0:T(8,128)S(1)}, f32[8,320]{1,0:T(8,128)}, u32[]{:S(2)}) copy-start(f32[8,320]{1,0:T(8,128)} %get-tuple-element.128) | copy-start | bytes 30724
  732.8 39.6 %collective-permute-start.15 = (f32[2048,896]{1,0:T(8,128)}, f32[2048,896]{1,0:T(8,128)}, u32[]{:S(2)}, u32[]{:S(2)}) collective-permute-start(f32[2048,896]{1,0:T(8,128)} %combine.17), channel_id=1, source_target_pairs={{0,1},{1,0},{2,3},{3,2},{4,5},{5,4},{6,7},{7,6}} | collective-permute-start | bytes 22020104 | tf_op jit(solution)/shard_map/ppermute | solution.py:277
  733.8 81.6 %collective-permute-start.17 = (f32[1024,896]{1,0:T(8,128)}, f32[1024,896]{1,0:T(8,128)}, u32[]{:S(2)}, u32[]{:S(2)}) collective-permute-start(f32[1024,896]{1,0:T(8,128)} %get-tuple-element.83), channel_id=1, source_target_pairs={{0,4},{4,0},{1,5},{5,1},{2,6},{6,2},{3,7},{7,3}} | collective-permute-start | bytes 11010056 | tf_op jit(solution)/shard_map/ppermute | solution.py:274
  734.9 82.5 %collective-permute-start.18 = (f32[1024,896]{1,0:T(8,128)}, f32[1024,896]{1,0:T(8,128)}, u32[]{:S(2)}, u32[]{:S(2)}) collective-permute-start(f32[1024,896]{1,0:T(8,128)} %get-tuple-element.74), channel_id=1, source_target_pairs={{0,2},{1,3},{2,0},{3,1},{4,6},{5,7},{6,4},{7,5}} | collective-permute-start | bytes 11010056 | tf_op jit(solution)/shard_map/ppermute | solution.py:280
  738.4 157.7 %collective-permute-start.16 = (f32[1024,896]{1,0:T(8,128)}, f32[1024,896]{1,0:T(8,128)}, u32[]{:S(2)}, u32[]{:S(2)}) collective-permute-start(f32[1024,896]{1,0:T(8,128)} %get-tuple-element.76), channel_id=1, source_target_pairs={{0,2},{1,3},{2,0},{3,1},{4,6},{5,7},{6,4},{7,5}} | collective-permute-start | bytes 11010056 | tf_op jit(solution)/shard_map/ppermute | solution.py:280
  772.4 45.0 %copy-start.8 = (f32[1024,896]{1,0:T(8,128)S(1)}, f32[1024,896]{1,0:T(8,128)}, u32[]{:S(2)}) copy-start(f32[1024,896]{1,0:T(8,128)} %get-tuple-element.85) | copy-start | bytes 11010052
  817.4 6.5 copy-start.7
  821.9 82.5 %collective-permute-start.19 = (f32[1024,896]{1,0:T(8,128)}, f32[1024,896]{1,0:T(8,128)}, u32[]{:S(2)}, u32[]{:S(2)}) collective-permute-start(f32[1024,896]{1,0:T(8,128)} %add.133), channel_id=1, source_target_pairs={{0,4},{4,0},{1,5},{5,1},{2,6},{6,2},{3,7},{7,3}} | collective-permute-start | bytes 11010056 | tf_op jit(solution)/shard_map/ppermute | solution.py:274
  822.9 157.2 %collective-permute-start.21 = (f32[1024,896]{1,0:T(8,128)}, f32[1024,896]{1,0:T(8,128)}, u32[]{:S(2)}, u32[]{:S(2)}) collective-permute-start(f32[1024,896]{1,0:T(8,128)} %get-tuple-element.90), channel_id=1, source_target_pairs={{0,4},{4,0},{1,5},{5,1},{2,6},{6,2},{3,7},{7,3}} | collective-permute-start | bytes 11010056 | tf_op jit(solution)/shard_map/ppermute | solution.py:274
  828.2 151.9 %collective-permute-start.20 = (f32[1024,896]{1,0:T(8,128)}, f32[1024,896]{1,0:T(8,128)}, u32[]{:S(2)}, u32[]{:S(2)}) collective-permute-start(f32[1024,896]{1,0:T(8,128)} %add.136), channel_id=1, source_target_pairs={{0,2},{1,3},{2,0},{3,1},{4,6},{5,7},{6,4},{7,5}} | collective-permute-start | bytes 11010056 | tf_op jit(solution)/shard_map/ppermute | solution.py:280
Sparse Core Ops, SparseCore 0:
  9.6 22.8 all-gather.2
where the time goes:
time: 1010 us; the launch traced here: 998 us
  Pallas kernels  514 us (51%)
  waiting for transfers between devices  314 us (31%)
  other arithmetic  101 us (10%)
  local copies, waits for them, and re-layouts  34.7 us (3%)
  starting transfers between devices  18.8 us (2%)
  between operations  14.1 us (1%)
    ppermute x9, waiting for transfers between devices, over_y(): return lax.ppermute(v, 'data', [(i, i ^ 1) for i in range(data_n)])  168 us
    pallas_call x10, Pallas kernels, combine(): pl.pallas_call(functools.partial(combine_kernel, rel, n_base, tuple(where...  150 us
    pallas_call x5, Pallas kernels, expert_rows(): pl.pallas_call(functools.partial(expert_kernel, half), out_shape=jax.Shap...  130 us
    pallas_call x8, Pallas kernels, gather_rows(): pl.pallas_call(functools.partial(gather_kernel, per_step, capacity), out_...  117 us
    pallas_call x8, Pallas kernels, shared_part(): pl.pallas_call(shared_kernel, out_shape=jax.ShapeDtypeStruct((tok_count,...  117 us
    all_to_all x1, waiting for transfers between devices, device_fn(): ws = lax.all_to_all(ws, group_axes, 0, 0, tiled=True)  76.8 us
    ppermute x5, waiting for transfers between devices, over_x(): return lax.ppermute(v, 'expert', [(i, i ^ 2) for i in range(exp_n)])  69.2 us
    reduce_sum x1, other arithmetic, make_lists(): jnp.sum(jnp.where(same, t_ids[None, None, :] - tok_count, 0), axis=2)  30.7 us
  transfers between devices with their start and end apart: 24, of which 7 were waited for; matrix products, arithmetic and copies ran while one was open for 12% of the time, Pallas kernels for 46%

commit v1 on v0

--- a/solution.py
+++ b/solution.py
@@ -69,30 +69,28 @@
     )(*args)
 
 
-def swiglu(x, w_gate_up, w_down_t):
-    width = w_down_t.shape[1]
-    pre = jnp.dot(x, w_gate_up, preferred_element_type=F32)
-    hidden = (jax.nn.silu(pre[:, :width]) * pre[:, width:]).astype(BF16)
+def swiglu(x, w_gate, w_up, w_down_t):
+    gate_pre = jnp.dot(x, w_gate, preferred_element_type=F32)
+    up_pre = jnp.dot(x, w_up, preferred_element_type=F32)
+    hidden = (jax.nn.silu(gate_pre) * up_pre).astype(BF16)
     return lax.dot_general(hidden, w_down_t, (((1,), (1,)), ((), ())), preferred_element_type=F32)
 
 
-def expert_kernel(half, y_ref, xg_ref, og_ref, ou_ref, od_ref, rv_ref, out_ref, wgu_ref, wd_ref):
-    width = wd_ref.shape[1]
-
+def expert_kernel(half, y_ref, xg_ref, og_ref, ou_ref, od_ref, rv_ref, out_ref, wg_ref, wu_ref, wd_ref):
     @pl.when(pl.program_id(1) == 0)
     def _():
         mine = pl.multiple_of(y_ref[0] * half, 64)
         other = pl.multiple_of((1 - y_ref[0]) * half, 64)
-        wgu_ref[pl.ds(mine, half), :width] = og_ref[0]
-        wgu_ref[pl.ds(mine, half), width:] = ou_ref[0]
+        wg_ref[pl.ds(mine, half), :] = og_ref[0]
+        wu_ref[pl.ds(mine, half), :] = ou_ref[0]
         wd_ref[pl.ds(mine, half), :] = od_ref[0]
-        wgu_ref[pl.ds(other, half), :width] = rv_ref[0, 0]
-        wgu_ref[pl.ds(other, half), width:] = rv_ref[1, 0]
+        wg_ref[pl.ds(other, half), :] = rv_ref[0, 0]
+        wu_ref[pl.ds(other, half), :] = rv_ref[1, 0]
         wd_ref[pl.ds(other, half), :] = rv_ref[2, 0]
 
     n_blk, _, capacity, d_model = xg_ref.shape
     x = xg_ref[...].reshape(n_blk * capacity, d_model)
-    out = swiglu(x, wgu_ref[...], wd_ref[...])
+    out = swiglu(x, wg_ref[...], wu_ref[...], wd_ref[...])
     out_ref[...] = out.astype(BF16).reshape(out_ref.shape)
 
 
@@ -113,7 +111,7 @@
                 pl.BlockSpec((3, 1, half, width), lambda i, m, y: (0, i, 0, 0)),
             ],
             out_specs=pl.BlockSpec((1, per_step, capacity, d_model), lambda i, m, y: (i, m, 0, 0)),
-            scratch_shapes=[pltpu.VMEM((2 * half, 2 * width), BF16), pltpu.VMEM((2 * half, width), BF16)],
+            scratch_shapes=[pltpu.VMEM((2 * half, width), BF16)] * 3,
         ),
         compiler_params=params(("arbitrary", "arbitrary")),
         cost_estimate=cost(6 * count * n_blocks * capacity * d_model * width, 4 * count * n_blocks * capacity * d_model),
@@ -121,11 +119,11 @@
     )(y_arr, xg, wg, wu, wdt, recv)
 
 
-def shared_kernel(x_ref, wgu_ref, wd_ref, out_ref):
-    out_ref[...] = swiglu(x_ref[...], wgu_ref[...], wd_ref[...])
-
-
-def shared_part(x_blk, wgu, wdt):
+def shared_kernel(x_ref, wg_ref, wu_ref, wd_ref, out_ref):
+    out_ref[...] = swiglu(x_ref[...], wg_ref[...], wu_ref[...], wd_ref[...])
+
+
+def shared_part(x_blk, wg, wu, wdt):
     tok_count, d_model = x_blk.shape
     width = wdt.shape[1]
     tile = 512
@@ -134,12 +132,12 @@
         shared_kernel,
         out_shape=jax.ShapeDtypeStruct((tok_count, d_model), F32),
         grid=(tok_count // tile,),
-        in_specs=[rows, pl.BlockSpec((d_model, 2 * width), lambda i: (0, 0)), pl.BlockSpec((d_model, width), lambda i: (0, 0))],
+        in_specs=[rows] + [pl.BlockSpec((d_model, width), lambda i: (0, 0))] * 3,
         out_specs=rows,
         compiler_params=params(("arbitrary",)),
         cost_estimate=cost(6 * tok_count * d_model * width, 6 * tok_count * d_model),
         name="shared_part",
-    )(x_blk, wgu, wdt)
+    )(x_blk, wg, wu, wdt)
 
 
 def combine_kernel(rel, n_base, where_of, halves, capacity, group, *refs):
@@ -307,8 +305,6 @@
         rows_s, width_s = ws.shape[1], ws.shape[2] // n_dev
         ws = ws.reshape(3, rows_s, n_dev, width_s).transpose(2, 0, 1, 3)
         ws = lax.all_to_all(ws, group_axes, 0, 0, tiled=True)
-        ws = ws.transpose(1, 0, 2, 3).reshape(3, d_model, width_s)
-        wgu_s, wdt_s = jnp.concatenate([ws[0], ws[1]], axis=1), ws[2]
 
         recvs = []
         start = 0
@@ -346,10 +342,14 @@
             last[0] = xg
 
         base = [None] * n_dev
+        shared_w = []
 
         def shared(r):
+            if not shared_w:
+                whole = after(ws).transpose(1, 0, 2, 3).reshape(3, d_model, width_s)
+                shared_w.extend([whole[0], whole[1], whole[2]])
             x_blk = after(blocks[r])
-            base[r] = shared_part(x_blk, wgu_s, wdt_s)
+            base[r] = shared_part(x_blk, *shared_w)
             last[0] = base[r]
 
         y_arr = y.astype(jnp.int32).reshape(1)
@@ -390,37 +390,37 @@
         gather(2)
         gather(1)
         gather(4)
-        make_lists()
         gather(3)
         gather(6)
+        make_lists()
         gather(5)
         gather(7)
         experts(0)
+        experts(1)
         shared(7)
         shared(5)
-        experts(1)
-        shared(6)
-        shared(4)
         experts(2)
-        shared(3)
         n_pre = sum(CHUNKS[:3])
         pre7 = part(7, [base[7]], 0, False)
         pre5 = part(5, [base[5]], 0, False)
         experts(3)
-        shared(1)
+        shared(6)
         experts(4)
         mate7 = over_core(part(7, [pre7], n_pre, False))
         mate6 = over_core(part(6, [base[6]], 0, False))
         diag = part(5, [pre5, mate7], n_pre, True)
         diag_x = over_x(diag[0])
         diag_y = over_y(diag[1])
+        shared(4)
         to_x = part(4, [base[4], mate6], 0, True)
         x_top = over_x(to_x[0])
+        shared(3)
         mate3 = over_core(part(3, [base[3]], 0, False))
+        shared(1)
+        to_y = part(1, [base[1], mate3], 0, True)
+        y_bot = over_y(to_y[1])
         shared(2)
         mate2 = over_core(part(2, [base[2]], 0, False))
-        to_y = part(1, [base[1], mate3], 0, True)
-        y_bot = over_y(to_y[1])
         shared(0)
         own = part(0, [base[0], mate2], 0, True)
         up_x, up_y, to_x1, to_y0 = after(diag_y, diag_x, to_x[1], to_y[0])

time: 1010 us -> 937 us (0.928)
  waiting for transfers between devices: 314 us -> 265 us
  Pallas kernels: 514 us -> 496 us
    all_to_all x1, waiting for transfers between devices: 76.8 us -> 0.01 us  [device_fn(): ws = lax.all_to_all(ws, group_axes, 0, 0, tiled=True)]
    ppermute x9, waiting for transfers between devices: 168 us -> 199 us  [over_y(): return lax.ppermute(v, 'data', [(i, i ^ 1) for i in range(data_n)])]
  transfers between devices with their start and end apart: 24 -> 24, of which waited for: 7 -> 5; matrix products, arithmetic and copies ran while one was open for 12% -> 13% of each run, Pallas kernels for 46% -> 41%
where the time goes in v1:
time: 937 us; the launch traced here: 926 us
  Pallas kernels  496 us (53%)
  waiting for transfers between devices  265 us (28%)
  other arithmetic  95.6 us (10%)
  local copies, waits for them, and re-layouts  32.7 us (3%)
  starting transfers between devices  20.9 us (2%)
  between operations  14.1 us (2%)
    ppermute x9, waiting for transfers between devices, over_y(): return lax.ppermute(v, 'data', [(i, i ^ 1) for i in range(data_n)])  199 us
    pallas_call x10, Pallas kernels, combine(): pl.pallas_call(functools.partial(combine_kernel, rel, n_base, tuple(where...  150 us
    pallas_call x5, Pallas kernels, expert_rows(): pl.pallas_call(functools.partial(expert_kernel, half), out_shape=jax.Shap...  121 us
    pallas_call x8, Pallas kernels, gather_rows(): pl.pallas_call(functools.partial(gather_kernel, per_step, capacity), out_...  117 us
    pallas_call x8, Pallas kernels, shared_part(): pl.pallas_call(shared_kernel, out_shape=jax.ShapeDtypeStruct((tok_count,...  109 us
    ppermute x5, waiting for transfers between devices, over_x(): return lax.ppermute(v, 'expert', [(i, i ^ 2) for i in range(exp_n)])  66.9 us
    reduce_sum x1, other arithmetic, make_lists(): jnp.sum(jnp.where(same, t_ids[None, None, :] - tok_count, 0), axis=2)  30.7 us
    reduce_sum x1, other arithmetic, make_lists(): slot_gate = jnp.sum(jnp.where(same, gate_of[:, None, :], 0.0), axis=2)  30.6 us
  transfers between devices with their start and end apart: 24, of which 5 were waited for; matrix products, arithmetic and copies ran while one was open for 13% of the time, Pallas kernels for 41%

profile of v1, /device:TPU:6, one launch (start us, length us, event | category | flops | bytes accessed | tf_op | source)
XLA Modules:
  0.0 926.2 jit_solution(6841796105217379698)
XLA Ops:
  7.9 1.5 pad_maximum_fusion.6
  9.4 2.3 dynamic-slice_bitcast_fusion
  11.7 5.1 dynamic-slice_bitcast_fusion.1
  16.8 75.4 %collective-permute-done.1.x_ref = bf16[2048,896]{1,0:T(8,128)(2,1)} collective-permute-done((bf16[2048,896]{1,0:T(8,128)(2,1)}, bf16[2048,896]{1,0:T(8,128)(2,1)}, u32[]{:S(2)}, u32[]{:S(2)}) %collective-permute-start.1) | collective-permute-done | bytes 3670048 | tf_op jit(solution)/shard_map/ppermute | solution.py:272
  92.7 1.9 pad_maximum_fusion.1
  94.6 1.2 collective-permute-start.7
  97.4 2.2 copy.21
  99.6 5.2 all-to-all-start
  104.8 1.3 dynamic-slice_bitcast_fusion.9
  106.2 1.8 dynamic-slice_bitcast_fusion.10
  108.0 1.4 pad_maximum_fusion.4
  109.4 1.4 pad_maximum_fusion.5
  110.8 2.0 pad_maximum_fusion.2
  112.8 2.0 pad_maximum_fusion.3
  114.8 1.8 gather_fusion
  116.9 1.6 compare_reduce_fusion
  118.5 1.1 fusion.3
  120.6 14.6 %gather_rows.8.refs_0_ = bf16[8,8,320,896]{3,2,1,0:T(8,128)(2,1)} custom-call(s32[16,2048]{1,0:T(8,128)} %get-tuple-element.112.pos_ref, bf16[2048,896]{1,0:T(8,128)(2,1)} %x_ref.1), custom_call_target="tpu_custom_call" | custom-call | flops 146800640 | bytes 4587520 | tf_op jit(solution)/shard_map/gather_rows/pallas_call | solution.py:58
  135.8 14.6 %gather_rows.9.refs_0_ = bf16[8,8,320,896]{3,2,1,0:T(8,128)(2,1)} custom-call(s32[16,2048]{1,0:T(8,128)} %get-tuple-element.111.pos_ref, bf16[2048,896]{1,0:T(8,128)(2,1)} %collective-permute-done.x_ref, bf16[8,8,320,896]{3,2,1,0:T(8,128)(2,1)} %gather_rows.8.refs_0_), custom_call_target="tpu_custom_call", output_to_operand_aliasing={{}: (2, {})} | custom-call | flops 146800640 | bytes 4587520 | tf_op jit(solution)/shard_map/gather_rows/pallas_call | solution.py:58
  150.4 14.7 %gather_rows.10.refs_0_ = bf16[8,8,320,896]{3,2,1,0:T(8,128)(2,1)} custom-call(s32[16,2048]{1,0:T(8,128)} %get-tuple-element.110.pos_ref, bf16[2048,896]{1,0:T(8,128)(2,1)} %collective-permute-done.1.x_ref, bf16[8,8,320,896]{3,2,1,0:T(8,128)(2,1)} %gather_rows.9.refs_0_), custom_call_target="tpu_custom_call", output_to_operand_aliasing={{}: (2, {})} | custom-call | flops 146800640 | bytes 4587520 | tf_op jit(solution)/shard_map/gather_rows/pallas_call | solution.py:58
  165.1 14.7 %gather_rows.11.refs_0_ = bf16[8,8,320,896]{3,2,1,0:T(8,128)(2,1)} custom-call(s32[16,2048]{1,0:T(8,128)} %get-tuple-element.109.pos_ref, bf16[2048,896]{1,0:T(8,128)(2,1)} %collective-permute-done.2.x_ref, bf16[8,8,320,896]{3,2,1,0:T(8,128)(2,1)} %gather_rows.10.refs_0_), custom_call_target="tpu_custom_call", output_to_operand_aliasing={{}: (2, {})} | custom-call | flops 146800640 | bytes 4587520 | tf_op jit(solution)/shard_map/gather_rows/pallas_call | solution.py:58
  179.8 1.5 collective-permute-start.9
  181.3 14.9 %gather_rows.12.refs_0_ = bf16[8,8,320,896]{3,2,1,0:T(8,128)(2,1)} custom-call(s32[16,2048]{1,0:T(8,128)} %get-tuple-element.108.pos_ref, bf16[2048,896]{1,0:T(8,128)(2,1)} %collective-permute-done.3.x_ref, bf16[8,8,320,896]{3,2,1,0:T(8,128)(2,1)} %gather_rows.11.refs_0_), custom_call_target="tpu_custom_call", output_to_operand_aliasing={{}: (2, {})} | custom-call | flops 146800640 | bytes 4587520 | tf_op jit(solution)/shard_map/gather_rows/pallas_call | solution.py:58
  196.7 14.7 %gather_rows.13.refs_0_ = bf16[8,8,320,896]{3,2,1,0:T(8,128)(2,1)} custom-call(s32[16,2048]{1,0:T(8,128)} %get-tuple-element.114.pos_ref, bf16[2048,896]{1,0:T(8,128)(2,1)} %collective-permute-done.4.x_ref, bf16[8,8,320,896]{3,2,1,0:T(8,128)(2,1)} %gather_rows.12.refs_0_), custom_call_target="tpu_custom_call", output_to_operand_aliasing={{}: (2, {})} | custom-call | flops 146800640 | bytes 4587520 | tf_op jit(solution)/shard_map/gather_rows/pallas_call | solution.py:58
  211.3 1.3 select_reduce_fusion.2
  212.7 30.6 %select_reduce_fusion = f32[64,320]{1,0:T(8,128)S(1)} fusion(f32[64,2048]{1,0:T(8,128)S(1)} %bitcast.139, s32[64,2048]{1,0:T(8,128)S(1)} %fusion.3), kind=kLoop, calls=%fused_computation.1 | loop fusion | flops 125808640 | bytes 1130496 | tf_op jit(solution)/shard_map/reduce_sum | solution.py:371
  243.4 1.5 collective-permute-start.11
  244.9 30.7 %select_reduce_fusion.1 = s32[64,320]{1,0:T(8,128)S(1)} fusion(s32[2048]{0:T(1024)S(1)} %iota_add_fusion, s32[64,2048]{1,0:T(8,128)S(1)} %fusion.3), kind=kLoop, calls=%fused_computation.2 | loop fusion | flops 125808640 | bytes 614400 | tf_op jit(solution)/shard_map/reduce_sum | solution.py:370
  279.6 14.6 %gather_rows.14.refs_0_ = bf16[8,8,320,896]{3,2,1,0:T(8,128)(2,1)} custom-call(s32[16,2048]{1,0:T(8,128)} %get-tuple-element.107.pos_ref, bf16[2048,896]{1,0:T(8,128)(2,1)} %collective-permute-done.5.x_ref, bf16[8,8,320,896]{3,2,1,0:T(8,128)(2,1)} %gather_rows.13.refs_0_), custom_call_target="tpu_custom_call", output_to_operand_aliasing={{}: (2, {})} | custom-call | flops 146800640 | bytes 4587520 | tf_op jit(solution)/shard_map/gather_rows/pallas_call | solution.py:58
  295.0 14.6 %gather_rows.15.xg_ref = bf16[8,8,320,896]{3,2,1,0:T(8,128)(2,1)} custom-call(s32[16,2048]{1,0:T(8,128)} %get-tuple-element.113.pos_ref, bf16[2048,896]{1,0:T(8,128)(2,1)} %collective-permute-done.6.x_ref, bf16[8,8,320,896]{3,2,1,0:T(8,128)(2,1)} %gather_rows.14.refs_0_), custom_call_target="tpu_custom_call", output_to_operand_aliasing={{}: (2, {})} | custom-call | flops 146800640 | bytes 4587520 | tf_op jit(solution)/shard_map/gather_rows/pallas_call | solution.py:58
  309.7 29.7 %expert_rows.5.refs_4_.refs_5_ = bf16[2,8,320,896]{3,2,1,0:T(8,128)(2,1)} custom-call(s32[1]{0:T(128)} %bitcast.21.y_ref, bf16[8,8,320,896]{3,2,1,0:T(8,128)(2,1)} %gather_rows.15.xg_ref, bf16[16,448,640]{2,1,0:T(8,128)(2,1)} %og_ref.9, bf16[16,448,640]{2,1,0:T(8,128)(2,1)} %ou_ref.9, bf16[16,448,640]{2,1,0:T(8,128)(2,1)} %bitcast.106, ...), custom_call_target="tpu_custom_call" | custom-call | flops 275251200 | bytes 18350080 | tf_op jit(solution)/shard_map/expert_rows/pallas_call | solution.py:102
  339.4 29.3 %expert_rows.6.refs_5_.refs_6_ = bf16[2,8,320,896]{3,2,1,0:T(8,128)(2,1)} custom-call(s32[1]{0:T(128)} %bitcast.21.y_ref, bf16[8,8,320,896]{3,2,1,0:T(8,128)(2,1)} %gather_rows.15.xg_ref, bf16[16,448,640]{2,1,0:T(8,128)(2,1)} %og_ref.9, bf16[16,448,640]{2,1,0:T(8,128)(2,1)} %ou_ref.9, bf16[16,448,640]{2,1,0:T(8,128)(2,1)} %bitcast.107, ...), custom_call_target="tpu_custom_call" | custom-call | flops 275251200 | bytes 18350080 | tf_op jit(solution)/shard_map/expert_rows/pallas_call | solution.py:102
  368.7 3.8 fusion.15
  372.5 13.6 %shared_part.8.refs_3_ = f32[2048,896]{1,0:T(8,128)} custom-call(bf16[2048,896]{1,0:T(8,128)(2,1)} %collective-permute-done.6.x_ref, bf16[896,640]{1,0:T(8,128)(2,1)} %bitcast.127, bf16[896,640]{1,0:T(8,128)(2,1)} %bitcast.119, bf16[896,640]{1,0:T(8,128)(2,1)} %bitcast.111), custom_call_target="tpu_custom_call" | custom-call | flops 110100480 | bytes 11010048 | tf_op jit(solution)/shard_map/shared_part/pallas_call | solution.py:131
  386.1 13.6 %shared_part.9.refs_3_ = f32[2048,896]{1,0:T(8,128)} custom-call(bf16[2048,896]{1,0:T(8,128)(2,1)} %collective-permute-done.5.x_ref, bf16[896,640]{1,0:T(8,128)(2,1)} %bitcast.128, bf16[896,640]{1,0:T(8,128)(2,1)} %bitcast.120, bf16[896,640]{1,0:T(8,128)(2,1)} %bitcast.112), custom_call_target="tpu_custom_call" | custom-call | flops 110100480 | bytes 11010048 | tf_op jit(solution)/shard_map/shared_part/pallas_call | solution.py:131
  399.7 29.5 %expert_rows.7.refs_6_.refs_7_ = bf16[2,8,320,896]{3,2,1,0:T(8,128)(2,1)} custom-call(s32[1]{0:T(128)} %bitcast.21.y_ref, bf16[8,8,320,896]{3,2,1,0:T(8,128)(2,1)} %gather_rows.15.xg_ref, bf16[16,448,640]{2,1,0:T(8,128)(2,1)} %og_ref.9, bf16[16,448,640]{2,1,0:T(8,128)(2,1)} %ou_ref.9, bf16[16,448,640]{2,1,0:T(8,128)(2,1)} %bitcast.108, ...), custom_call_target="tpu_custom_call" | custom-call | flops 275251200 | bytes 18350080 | tf_op jit(solution)/shard_map/expert_rows/pallas_call | solution.py:102
  429.3 13.7 %combine.10.refs_3_ = f32[2048,896]{1,0:T(8,128)} custom-call(s32[1,8]{1,0:T(1,128)} %get-tuple-element.132.refs_0_, s32[1,2560]{1,0:T(1,128)} %squeeze.139.refs_1_, f32[1,2560]{1,0:T(1,128)} %squeeze.140.refs_2_, f32[2048,896]{1,0:T(8,128)} %shared_part.8.refs_3_, bf16[2,8,320,896]{3,2,1,0:T(8,128)(2,1)} %expert_rows.5.refs_4_.refs_5_, ...), custom_call_target="tpu_custom_call" | custom-call | flops 55050240 | bytes 14680064 | tf_op jit(solution)/shard_map/combine/pallas_call | solution.py:243
  443.0 13.7 %combine.11.refs_3_ = f32[2048,896]{1,0:T(8,128)} custom-call(s32[1,8]{1,0:T(1,128)} %get-tuple-element.134.refs_0_, s32[1,2560]{1,0:T(1,128)} %squeeze.133.refs_1_, f32[1,2560]{1,0:T(1,128)} %squeeze.134.refs_2_, f32[2048,896]{1,0:T(8,128)} %shared_part.9.refs_3_, bf16[2,8,320,896]{3,2,1,0:T(8,128)(2,1)} %expert_rows.5.refs_4_.refs_5_, ...), custom_call_target="tpu_custom_call" | custom-call | flops 55050240 | bytes 14680064 | tf_op jit(solution)/shard_map/combine/pallas_call | solution.py:243
  456.7 16.1 %expert_rows.8.refs_4_.refs_7_.refs_5_.refs_8_ = bf16[1,8,320,896]{3,2,1,0:T(8,128)(2,1)} custom-call(s32[1]{0:T(128)} %bitcast.21.y_ref, bf16[8,8,320,896]{3,2,1,0:T(8,128)(2,1)} %gather_rows.15.xg_ref, bf16[16,448,640]{2,1,0:T(8,128)(2,1)} %og_ref.9, bf16[16,448,640]{2,1,0:T(8,128)(2,1)} %ou_ref.9, bf16[16,448,640]{2,1,0:T(8,128)(2,1)} %bitcast.109, ...), custom_call_target="tpu_custom_call" | custom-call | flops 137625600 | bytes 9175040 | tf_op jit(solution)/shard_map/expert_rows/pallas_call | solution.py:102
  472.8 13.6 %shared_part.10.refs_3_ = f32[2048,896]{1,0:T(8,128)} custom-call(bf16[2048,896]{1,0:T(8,128)(2,1)} %collective-permute-done.4.x_ref, bf16[896,640]{1,0:T(8,128)(2,1)} %bitcast.129, bf16[896,640]{1,0:T(8,128)(2,1)} %bitcast.121, bf16[896,640]{1,0:T(8,128)(2,1)} %bitcast.113), custom_call_target="tpu_custom_call" | custom-call | flops 110100480 | bytes 11010048 | tf_op jit(solution)/shard_map/shared_part/pallas_call | solution.py:131
  486.4 16.1 %expert_rows.9.refs_5_.refs_8_.refs_6_.refs_9_ = bf16[1,8,320,896]{3,2,1,0:T(8,128)(2,1)} custom-call(s32[1]{0:T(128)} %bitcast.21.y_ref, bf16[8,8,320,896]{3,2,1,0:T(8,128)(2,1)} %gather_rows.15.xg_ref, bf16[16,448,640]{2,1,0:T(8,128)(2,1)} %og_ref.9, bf16[16,448,640]{2,1,0:T(8,128)(2,1)} %ou_ref.9, bf16[16,448,640]{2,1,0:T(8,128)(2,1)} %bitcast.110, ...), custom_call_target="tpu_custom_call" | custom-call | flops 137625600 | bytes 9175040 | tf_op jit(solution)/shard_map/expert_rows/pallas_call | solution.py:102
  502.5 9.1 combine.12
  513.0 15.8 %combine.13 = f32[2048,896]{1,0:T(8,128)} custom-call(s32[1,8]{1,0:T(1,128)} %get-tuple-element.133.refs_0_, s32[1,2560]{1,0:T(1,128)} %squeeze.136.refs_1_, f32[1,2560]{1,0:T(1,128)} %squeeze.137.refs_2_, f32[2048,896]{1,0:T(8,128)} %shared_part.10.refs_3_, bf16[2,8,320,896]{3,2,1,0:T(8,128)(2,1)} %expert_rows.5.refs_4_.refs_5_, ...), custom_call_target="tpu_custom_call" | custom-call | flops 73400320 | bytes 14680064 | tf_op jit(solution)/shard_map/combine/pallas_call | solution.py:243
  531.7 11.9 %combine.14 = (f32[1024,896]{1,0:T(8,128)}, f32[1024,896]{1,0:T(8,128)}) custom-call(s32[1,8]{1,0:T(1,128)} %get-tuple-element.134.refs_0_, s32[1,2560]{1,0:T(1,128)} %squeeze.133.refs_1_, f32[1,2560]{1,0:T(1,128)} %squeeze.134.refs_2_, f32[2048,896]{1,0:T(8,128)} %combine.11.refs_3_, f32[2048,896]{1,0:T(8,128)} %collective-permute-done.12.refs_4_, ...), custom_call_target="tpu_custom_call" | custom-call | flops 18350080 | bytes 14680064 | tf_op jit(solution)/shard_map/combine/pallas_call | solution.py:243
  543.6 13.6 %shared_part.11.refs_3_ = f32[2048,896]{1,0:T(8,128)} custom-call(bf16[2048,896]{1,0:T(8,128)(2,1)} %collective-permute-done.2.x_ref, bf16[896,640]{1,0:T(8,128)(2,1)} %bitcast.130, bf16[896,640]{1,0:T(8,128)(2,1)} %bitcast.122, bf16[896,640]{1,0:T(8,128)(2,1)} %bitcast.114), custom_call_target="tpu_custom_call" | custom-call | flops 110100480 | bytes 11010048 | tf_op jit(solution)/shard_map/shared_part/pallas_call | solution.py:131
  557.2 18.1 %combine.15 = (f32[1024,896]{1,0:T(8,128)}, f32[1024,896]{1,0:T(8,128)}) custom-call(s32[1,8]{1,0:T(1,128)} %get-tuple-element.135.refs_0_, s32[1,2560]{1,0:T(1,128)} %squeeze.130.refs_1_, f32[1,2560]{1,0:T(1,128)} %squeeze.131.refs_2_, f32[2048,896]{1,0:T(8,128)} %shared_part.11.refs_3_, f32[2048,896]{1,0:T(8,128)} %collective-permute-done.13.refs_4_, ...), custom_call_target="tpu_custom_call" | custom-call | flops 73400320 | bytes 14680064 | tf_op jit(solution)/shard_map/combine/pallas_call | solution.py:243
  575.3 13.6 %shared_part.12.refs_3_ = f32[2048,896]{1,0:T(8,128)} custom-call(bf16[2048,896]{1,0:T(8,128)(2,1)} %collective-permute-done.3.x_ref, bf16[896,640]{1,0:T(8,128)(2,1)} %bitcast.131, bf16[896,640]{1,0:T(8,128)(2,1)} %bitcast.123, bf16[896,640]{1,0:T(8,128)(2,1)} %bitcast.115), custom_call_target="tpu_custom_call" | custom-call | flops 110100480 | bytes 11010048 | tf_op jit(solution)/shard_map/shared_part/pallas_call | solution.py:131
  588.9 15.5 %combine.16 = f32[2048,896]{1,0:T(8,128)} custom-call(s32[1,8]{1,0:T(1,128)} %get-tuple-element.136.refs_0_, s32[1,2560]{1,0:T(1,128)} %squeeze.127.refs_1_, f32[1,2560]{1,0:T(1,128)} %squeeze.128.refs_2_, f32[2048,896]{1,0:T(8,128)} %shared_part.12.refs_3_, bf16[2,8,320,896]{3,2,1,0:T(8,128)(2,1)} %expert_rows.5.refs_4_.refs_5_, ...), custom_call_target="tpu_custom_call" | custom-call | flops 73400320 | bytes 14680064 | tf_op jit(solution)/shard_map/combine/pallas_call | solution.py:243
  607.3 13.6 %shared_part.13.refs_3_ = f32[2048,896]{1,0:T(8,128)} custom-call(bf16[2048,896]{1,0:T(8,128)(2,1)} %collective-permute-done.1.x_ref, bf16[896,640]{1,0:T(8,128)(2,1)} %bitcast.132, bf16[896,640]{1,0:T(8,128)(2,1)} %bitcast.124, bf16[896,640]{1,0:T(8,128)(2,1)} %bitcast.116), custom_call_target="tpu_custom_call" | custom-call | flops 110100480 | bytes 11010048 | tf_op jit(solution)/shard_map/shared_part/pallas_call | solution.py:131
  620.8 18.2 %combine.17 = (f32[1024,896]{1,0:T(8,128)}, f32[1024,896]{1,0:T(8,128)}) custom-call(s32[1,8]{1,0:T(1,128)} %get-tuple-element.137.refs_0_, s32[1,2560]{1,0:T(1,128)} %squeeze.124.refs_1_, f32[1,2560]{1,0:T(1,128)} %squeeze.125.refs_2_, f32[2048,896]{1,0:T(8,128)} %shared_part.13.refs_3_, f32[2048,896]{1,0:T(8,128)} %collective-permute-done.14.refs_4_, ...), custom_call_target="tpu_custom_call" | custom-call | flops 73400320 | bytes 14680064 | tf_op jit(solution)/shard_map/combine/pallas_call | solution.py:243
  639.0 13.6 %shared_part.14.refs_3_ = f32[2048,896]{1,0:T(8,128)} custom-call(bf16[2048,896]{1,0:T(8,128)(2,1)} %collective-permute-done.x_ref, bf16[896,640]{1,0:T(8,128)(2,1)} %bitcast.133, bf16[896,640]{1,0:T(8,128)(2,1)} %bitcast.125, bf16[896,640]{1,0:T(8,128)(2,1)} %bitcast.117), custom_call_target="tpu_custom_call" | custom-call | flops 110100480 | bytes 11010048 | tf_op jit(solution)/shard_map/shared_part/pallas_call | solution.py:131
  652.6 15.7 %combine.18 = f32[2048,896]{1,0:T(8,128)} custom-call(s32[1,8]{1,0:T(1,128)} %get-tuple-element.131.refs_0_, s32[1,2560]{1,0:T(1,128)} %squeeze.121.refs_1_, f32[1,2560]{1,0:T(1,128)} %squeeze.122.refs_2_, f32[2048,896]{1,0:T(8,128)} %shared_part.14.refs_3_, bf16[2,8,320,896]{3,2,1,0:T(8,128)(2,1)} %expert_rows.5.refs_4_.refs_5_, ...), custom_call_target="tpu_custom_call" | custom-call | flops 73400320 | bytes 14680064 | tf_op jit(solution)/shard_map/combine/pallas_call | solution.py:243
  669.3 1.4 collective-permute-start.18
  672.7 13.6 %shared_part.15.refs_3_ = f32[2048,896]{1,0:T(8,128)} custom-call(bf16[2048,896]{1,0:T(8,128)(2,1)} %x_ref.1, bf16[896,640]{1,0:T(8,128)(2,1)} %bitcast.134, bf16[896,640]{1,0:T(8,128)(2,1)} %bitcast.126, bf16[896,640]{1,0:T(8,128)(2,1)} %bitcast.118), custom_call_target="tpu_custom_call" | custom-call | flops 110100480 | bytes 11010048 | tf_op jit(solution)/shard_map/shared_part/pallas_call | solution.py:131
  686.3 2.0 collective-permute-start.21
  688.3 18.1 %combine.19 = (f32[1024,896]{1,0:T(8,128)}, f32[1024,896]{1,0:T(8,128)}) custom-call(s32[1,8]{1,0:T(1,128)} %get-tuple-element.138.refs_0_, s32[1,2560]{1,0:T(1,128)} %squeeze.118.refs_1_, f32[1,2560]{1,0:T(1,128)} %squeeze.119.refs_2_, f32[2048,896]{1,0:T(8,128)} %shared_part.15.refs_3_, f32[2048,896]{1,0:T(8,128)} %collective-permute-done.15.refs_4_, ...), custom_call_target="tpu_custom_call" | custom-call | flops 73400320 | bytes 14680064 | tf_op jit(solution)/shard_map/combine/pallas_call | solution.py:243
  706.4 45.5 %collective-permute-done.17 = f32[1024,896]{1,0:T(8,128)} collective-permute-done((f32[1024,896]{1,0:T(8,128)}, f32[1024,896]{1,0:T(8,128)}, u32[]{:S(2)}, u32[]{:S(2)}) %collective-permute-start.17) | collective-permute-done | bytes 3670048 | tf_op jit(solution)/shard_map/ppermute | solution.py:272
  751.8 4.4 add.133
  756.2 2.0 collective-permute-start.19
  758.2 4.2 add.136
  762.4 1.4 collective-permute-start.20
  763.9 66.6 %collective-permute-done.16 = f32[1024,896]{1,0:T(8,128)} collective-permute-done((f32[1024,896]{1,0:T(8,128)}, f32[1024,896]{1,0:T(8,128)}, u32[]{:S(2)}, u32[]{:S(2)}) %collective-permute-start.16) | collective-permute-done | bytes 3670048 | tf_op jit(solution)/shard_map/ppermute | solution.py:278
  830.5 77.7 %collective-permute-done.19 = f32[1024,896]{1,0:T(8,128)} collective-permute-done((f32[1024,896]{1,0:T(8,128)}, f32[1024,896]{1,0:T(8,128)}, u32[]{:S(2)}, u32[]{:S(2)}) %collective-permute-start.19) | collective-permute-done | bytes 3670048 | tf_op jit(solution)/shard_map/ppermute | solution.py:272
  908.2 10.9 %add_convert_fusion.1 = (bf16[2048,896]{1,0:T(8,128)(2,1)}, bf16[2048,896]{1,0:T(8,128)(2,1)}) fusion(f32[1024,896]{1,0:T(8,128)} %collective-permute-done.19, f32[1024,896]{1,0:T(8,128)} %collective-permute-done.16, f32[1024,896]{1,0:T(8,128)} %get-tuple-element.76, bf16[2048,896]{1,0:T(8,128)(2,1)} %x_ref.1, ...), kind=kLoop, output_to_operand_aliasing={{0}: (7, {}), {1}: (7, {})}, calls=%fused_computation.10 | loop fusion | flops 9175040 | bytes 29360128 | tf_op jit(solution)/shard_map/convert_element_type | solution.py:432
  (112 shorter events, 21.0 us)
Async XLA Ops:
  6.5 108.2 %all-gather.3.cloned.1.call-start = ((), (), s32[]{:S(2)}) async-start(), calls=%async_computation.1 | async-start | bytes 1179648 | tf_op jit(solution)/shard_map/all_gather | solution.py:292
  6.5 85.6 %collective-permute-start.1 = (bf16[2048,896]{1,0:T(8,128)(2,1)}, bf16[2048,896]{1,0:T(8,128)(2,1)}, u32[]{:S(2)}, u32[]{:S(2)}) collective-permute-start(bf16[2048,896]{1,0:T(8,128)(2,1)} %x_ref.1), channel_id=1, source_target_pairs={{0,4},{4,0},{1,5},{5,1},{2,6},{6,2},{3,7},{7,3}} | collective-permute-start | bytes 11010056 | tf_op jit(solution)/shard_map/ppermute | solution.py:272
  7.0 85.3 %collective-permute-start.2 = (bf16[2048,896]{1,0:T(8,128)(2,1)}, bf16[2048,896]{1,0:T(8,128)(2,1)}, u32[]{:S(2)}, u32[]{:S(2)}) collective-permute-start(bf16[2048,896]{1,0:T(8,128)(2,1)} %x_ref.1), channel_id=1, source_target_pairs={{0,2},{1,3},{2,0},{3,1},{4,6},{5,7},{6,4},{7,5}} | collective-permute-start | bytes 11010056 | tf_op jit(solution)/shard_map/ppermute | solution.py:278
  7.1 128.2 %collective-permute-start = (bf16[2048,896]{1,0:T(8,128)(2,1)}, bf16[2048,896]{1,0:T(8,128)(2,1)}, u32[]{:S(2)}, u32[]{:S(2)}) collective-permute-start(bf16[2048,896]{1,0:T(8,128)(2,1)} %x_ref.1), channel_id=1, source_target_pairs={{0,1},{1,0},{2,3},{3,2},{4,5},{5,4},{6,7},{7,6}} | collective-permute-start | bytes 11010056 | tf_op jit(solution)/shard_map/ppermute | solution.py:275
  16.8 79.1 %copy-start.5 = (bf16[5120,112]{0,1:T(8,128)(2,1)S(1)}, bf16[5120,112]{0,1:T(8,128)(2,1)}, u32[]{:S(2)}) copy-start(bf16[5120,112]{0,1:T(8,128)(2,1)} %param.17) | copy-start | bytes 3440644
  92.1 87.6 %collective-permute-start.3 = (bf16[2048,896]{1,0:T(8,128)(2,1)}, bf16[2048,896]{1,0:T(8,128)(2,1)}, u32[]{:S(2)}, u32[]{:S(2)}) collective-permute-start(bf16[2048,896]{1,0:T(8,128)(2,1)} %collective-permute-done.1.x_ref), channel_id=1, source_target_pairs={{0,1},{1,0},{2,3},{3,2},{4,5},{5,4},{6,7},{7,6}} | collective-permute-start | bytes 11010056 | tf_op jit(solution)/shard_map/ppermute | solution.py:275
  92.4 103.8 %collective-permute-start.4 = (bf16[2048,896]{1,0:T(8,128)(2,1)}, bf16[2048,896]{1,0:T(8,128)(2,1)}, u32[]{:S(2)}, u32[]{:S(2)}) collective-permute-start(bf16[2048,896]{1,0:T(8,128)(2,1)} %collective-permute-done.2.x_ref), channel_id=1, source_target_pairs={{0,1},{1,0},{2,3},{3,2},{4,5},{5,4},{6,7},{7,6}} | collective-permute-start | bytes 11010056 | tf_op jit(solution)/shard_map/ppermute | solution.py:275
  92.7 3.4 copy-start.6
  94.6 1.6 copy-start.7
  94.6 215.1 %collective-permute-start.7 = (bf16[3,2,448,640]{3,2,1,0:T(8,128)(2,1)}, bf16[3,2,448,640]{3,2,1,0:T(8,128)(2,1)}, u32[]{:S(2)}, u32[]{:S(2)}) collective-permute-start(bf16[3,2,448,640]{3,2,1,0:T(8,128)(2,1)} %pad_maximum_fusion.1), channel_id=1, source_target_pairs={{0,4},{4,0},{1,5},{5,1},{2,6},{6,2},{3,7},{7,3}} | collective-permute-start | bytes 10321928 | tf_op jit(solution)/shard_map/ppermute | solution.py:272
  96.4 116.3 %collective-permute-start.5 = (bf16[2048,896]{1,0:T(8,128)(2,1)}, bf16[2048,896]{1,0:T(8,128)(2,1)}, u32[]{:S(2)}, u32[]{:S(2)}) collective-permute-start(bf16[2048,896]{1,0:T(8,128)(2,1)} %collective-permute-done.1.x_ref), channel_id=1, source_target_pairs={{0,2},{1,3},{2,0},{3,1},{4,6},{5,7},{6,4},{7,5}} | collective-permute-start | bytes 11010056 | tf_op jit(solution)/shard_map/ppermute | solution.py:278
  99.6 269.1 %all-to-all-start = ((bf16[8,3,112,640]{3,2,1,0:T(8,128)(2,1)}), bf16[8,3,112,640]{3,2,1,0:T(8,128)(2,1)}, u32[]{:S(2)}, u32[]{:S(2)}) async-start(bf16[8,3,112,640]{3,2,1,0:T(8,128)(2,1)} %copy.21), calls=%async_computation | async-start | bytes 6881280 | tf_op jit(solution)/shard_map/all_to_all | solution.py:307
  108.0 2.9 copy-start.1
  108.0 2.8 copy-start.2
  110.8 2.0 copy-start
  135.3 204.1 %collective-permute-start.8 = (bf16[3,2,448,640]{3,2,1,0:T(8,128)(2,1)}, bf16[3,2,448,640]{3,2,1,0:T(8,128)(2,1)}, u32[]{:S(2)}, u32[]{:S(2)}) collective-permute-start(bf16[3,2,448,640]{3,2,1,0:T(8,128)(2,1)} %pad_maximum_fusion.2), channel_id=1, source_target_pairs={{0,4},{4,0},{1,5},{5,1},{2,6},{6,2},{3,7},{7,3}} | collective-permute-start | bytes 10321928 | tf_op jit(solution)/shard_map/ppermute | solution.py:272
  179.8 220.0 %collective-permute-start.9 = (bf16[3,2,448,640]{3,2,1,0:T(8,128)(2,1)}, bf16[3,2,448,640]{3,2,1,0:T(8,128)(2,1)}, u32[]{:S(2)}, u32[]{:S(2)}) collective-permute-start(bf16[3,2,448,640]{3,2,1,0:T(8,128)(2,1)} %pad_maximum_fusion.3), channel_id=1, source_target_pairs={{0,4},{4,0},{1,5},{5,1},{2,6},{6,2},{3,7},{7,3}} | collective-permute-start | bytes 10321928 | tf_op jit(solution)/shard_map/ppermute | solution.py:272
  196.2 260.6 %collective-permute-start.10 = (bf16[3,1,448,640]{3,2,1,0:T(8,128)(2,1)}, bf16[3,1,448,640]{3,2,1,0:T(8,128)(2,1)}, u32[]{:S(2)}, u32[]{:S(2)}) collective-permute-start(bf16[3,1,448,640]{3,2,1,0:T(8,128)(2,1)} %pad_maximum_fusion.4), channel_id=1, source_target_pairs={{0,4},{4,0},{1,5},{5,1},{2,6},{6,2},{3,7},{7,3}} | collective-permute-start | bytes 5160968 | tf_op jit(solution)/shard_map/ppermute | solution.py:272
  212.7 30.7 %collective-permute-start.6 = (bf16[2048,896]{1,0:T(8,128)(2,1)}, bf16[2048,896]{1,0:T(8,128)(2,1)}, u32[]{:S(2)}, u32[]{:S(2)}) collective-permute-start(bf16[2048,896]{1,0:T(8,128)(2,1)} %collective-permute-done.5.x_ref), channel_id=1, source_target_pairs={{0,1},{1,0},{2,3},{3,2},{4,5},{5,4},{6,7},{7,6}} | collective-permute-start | bytes 11010056 | tf_op jit(solution)/shard_map/ppermute | solution.py:275
  243.4 243.1 %collective-permute-start.11 = (bf16[3,1,448,640]{3,2,1,0:T(8,128)(2,1)}, bf16[3,1,448,640]{3,2,1,0:T(8,128)(2,1)}, u32[]{:S(2)}, u32[]{:S(2)}) collective-permute-start(bf16[3,1,448,640]{3,2,1,0:T(8,128)(2,1)} %pad_maximum_fusion.5), channel_id=1, source_target_pairs={{0,4},{4,0},{1,5},{5,1},{2,6},{6,2},{3,7},{7,3}} | collective-permute-start | bytes 5160968 | tf_op jit(solution)/shard_map/ppermute | solution.py:272
  502.5 9.1 copy-start.18
  502.5 9.8 %copy-start.19 = (f32[8,320]{1,0:T(8,128)S(1)}, f32[8,320]{1,0:T(8,128)}, u32[]{:S(2)}) copy-start(f32[8,320]{1,0:T(8,128)} %get-tuple-element.117) | copy-start | bytes 30724
  511.5 20.2 %collective-permute-start.12 = (f32[2048,896]{1,0:T(8,128)}, f32[2048,896]{1,0:T(8,128)}, u32[]{:S(2)}, u32[]{:S(2)}) collective-permute-start(f32[2048,896]{1,0:T(8,128)} %combine.12), channel_id=1, source_target_pairs={{0,1},{1,0},{2,3},{3,2},{4,5},{5,4},{6,7},{7,6}} | collective-permute-start | bytes 22020104 | tf_op jit(solution)/shard_map/ppermute | solution.py:275
  513.0 16.0 %copy-start.15 = (s32[8,320]{1,0:T(8,128)S(1)}, s32[8,320]{1,0:T(8,128)}, u32[]{:S(2)}) copy-start(s32[8,320]{1,0:T(8,128)} %get-tuple-element.128) | copy-start | bytes 30724
  513.0 16.7 %copy-start.17 = (f32[8,320]{1,0:T(8,128)S(1)}, f32[8,320]{1,0:T(8,128)}, u32[]{:S(2)}) copy-start(f32[8,320]{1,0:T(8,128)} %get-tuple-element.120) | copy-start | bytes 30724
  513.0 17.4 %copy-start.14 = (s32[8,320]{1,0:T(8,128)S(1)}, s32[8,320]{1,0:T(8,128)}, u32[]{:S(2)}) copy-start(s32[8,320]{1,0:T(8,128)} %get-tuple-element.127) | copy-start | bytes 30724
  513.0 18.1 %copy-start.16 = (f32[8,320]{1,0:T(8,128)S(1)}, f32[8,320]{1,0:T(8,128)}, u32[]{:S(2)}) copy-start(f32[8,320]{1,0:T(8,128)} %get-tuple-element.119) | copy-start | bytes 30724
  528.7 28.5 %collective-permute-start.13 = (f32[2048,896]{1,0:T(8,128)}, f32[2048,896]{1,0:T(8,128)}, u32[]{:S(2)}, u32[]{:S(2)}) collective-permute-start(f32[2048,896]{1,0:T(8,128)} %combine.13), channel_id=1, source_target_pairs={{0,1},{1,0},{2,3},{3,2},{4,5},{5,4},{6,7},{7,6}} | collective-permute-start | bytes 22020104 | tf_op jit(solution)/shard_map/ppermute | solution.py:275
  588.9 15.7 %copy-start.11 = (s32[8,320]{1,0:T(8,128)S(1)}, s32[8,320]{1,0:T(8,128)}, u32[]{:S(2)}) copy-start(s32[8,320]{1,0:T(8,128)} %get-tuple-element.123) | copy-start | bytes 30724
  588.9 16.4 %copy-start.13 = (f32[8,320]{1,0:T(8,128)S(1)}, f32[8,320]{1,0:T(8,128)}, u32[]{:S(2)}) copy-start(f32[8,320]{1,0:T(8,128)} %get-tuple-element.115) | copy-start | bytes 30724
  588.9 17.0 %copy-start.10 = (s32[8,320]{1,0:T(8,128)S(1)}, s32[8,320]{1,0:T(8,128)}, u32[]{:S(2)}) copy-start(s32[8,320]{1,0:T(8,128)} %get-tuple-element.129) | copy-start | bytes 30724
  588.9 17.7 %copy-start.12 = (f32[8,320]{1,0:T(8,128)S(1)}, f32[8,320]{1,0:T(8,128)}, u32[]{:S(2)}) copy-start(f32[8,320]{1,0:T(8,128)} %get-tuple-element.121) | copy-start | bytes 30724
  604.4 16.5 %collective-permute-start.14 = (f32[2048,896]{1,0:T(8,128)}, f32[2048,896]{1,0:T(8,128)}, u32[]{:S(2)}, u32[]{:S(2)}) collective-permute-start(f32[2048,896]{1,0:T(8,128)} %combine.16), channel_id=1, source_target_pairs={{0,1},{1,0},{2,3},{3,2},{4,5},{5,4},{6,7},{7,6}} | collective-permute-start | bytes 22020104 | tf_op jit(solution)/shard_map/ppermute | solution.py:275
  652.6 18.2 %copy-start.8 = (s32[8,320]{1,0:T(8,128)S(1)}, s32[8,320]{1,0:T(8,128)}, u32[]{:S(2)}) copy-start(s32[8,320]{1,0:T(8,128)} %get-tuple-element.130) | copy-start | bytes 30724
  652.6 18.8 %copy-start.9 = (f32[8,320]{1,0:T(8,128)S(1)}, f32[8,320]{1,0:T(8,128)}, u32[]{:S(2)}) copy-start(f32[8,320]{1,0:T(8,128)} %get-tuple-element.122) | copy-start | bytes 30724
  668.3 20.0 %collective-permute-start.15 = (f32[2048,896]{1,0:T(8,128)}, f32[2048,896]{1,0:T(8,128)}, u32[]{:S(2)}, u32[]{:S(2)}) collective-permute-start(f32[2048,896]{1,0:T(8,128)} %combine.18), channel_id=1, source_target_pairs={{0,1},{1,0},{2,3},{3,2},{4,5},{5,4},{6,7},{7,6}} | collective-permute-start | bytes 22020104 | tf_op jit(solution)/shard_map/ppermute | solution.py:275
  669.3 82.5 %collective-permute-start.17 = (f32[1024,896]{1,0:T(8,128)}, f32[1024,896]{1,0:T(8,128)}, u32[]{:S(2)}, u32[]{:S(2)}) collective-permute-start(f32[1024,896]{1,0:T(8,128)} %get-tuple-element.77), channel_id=1, source_target_pairs={{0,4},{4,0},{1,5},{5,1},{2,6},{6,2},{3,7},{7,3}} | collective-permute-start | bytes 11010056 | tf_op jit(solution)/shard_map/ppermute | solution.py:272
  669.3 82.5 %collective-permute-start.18 = (f32[1024,896]{1,0:T(8,128)}, f32[1024,896]{1,0:T(8,128)}, u32[]{:S(2)}, u32[]{:S(2)}) collective-permute-start(f32[1024,896]{1,0:T(8,128)} %get-tuple-element.68), channel_id=1, source_target_pairs={{0,2},{1,3},{2,0},{3,1},{4,6},{5,7},{6,4},{7,5}} | collective-permute-start | bytes 11010056 | tf_op jit(solution)/shard_map/ppermute | solution.py:278
  672.1 158.4 %collective-permute-start.16 = (f32[1024,896]{1,0:T(8,128)}, f32[1024,896]{1,0:T(8,128)}, u32[]{:S(2)}, u32[]{:S(2)}) collective-permute-start(f32[1024,896]{1,0:T(8,128)} %get-tuple-element.70), channel_id=1, source_target_pairs={{0,2},{1,3},{2,0},{3,1},{4,6},{5,7},{6,4},{7,5}} | collective-permute-start | bytes 11010056 | tf_op jit(solution)/shard_map/ppermute | solution.py:278
  686.3 144.2 %collective-permute-start.21 = (f32[1024,896]{1,0:T(8,128)}, f32[1024,896]{1,0:T(8,128)}, u32[]{:S(2)}, u32[]{:S(2)}) collective-permute-start(f32[1024,896]{1,0:T(8,128)} %get-tuple-element.84), channel_id=1, source_target_pairs={{0,4},{4,0},{1,5},{5,1},{2,6},{6,2},{3,7},{7,3}} | collective-permute-start | bytes 11010056 | tf_op jit(solution)/shard_map/ppermute | solution.py:272
  688.3 63.5 %copy-start.4 = (f32[1024,896]{1,0:T(8,128)S(1)}, f32[1024,896]{1,0:T(8,128)}, u32[]{:S(2)}) copy-start(f32[1024,896]{1,0:T(8,128)} %get-tuple-element.79) | copy-start | bytes 11010052
  751.8 6.4 copy-start.3
  756.2 152.0 %collective-permute-start.19 = (f32[1024,896]{1,0:T(8,128)}, f32[1024,896]{1,0:T(8,128)}, u32[]{:S(2)}, u32[]{:S(2)}) collective-permute-start(f32[1024,896]{1,0:T(8,128)} %add.133), channel_id=1, source_target_pairs={{0,4},{4,0},{1,5},{5,1},{2,6},{6,2},{3,7},{7,3}} | collective-permute-start | bytes 11010056 | tf_op jit(solution)/shard_map/ppermute | solution.py:272
  762.4 145.8 %collective-permute-start.20 = (f32[1024,896]{1,0:T(8,128)}, f32[1024,896]{1,0:T(8,128)}, u32[]{:S(2)}, u32[]{:S(2)}) collective-permute-start(f32[1024,896]{1,0:T(8,128)} %add.136), channel_id=1, source_target_pairs={{0,2},{1,3},{2,0},{3,1},{4,6},{5,7},{6,4},{7,5}} | collective-permute-start | bytes 11010056 | tf_op jit(solution)/shard_map/ppermute | solution.py:278
Sparse Core Ops, SparseCore 0:
  9.6 22.9 all-gather.2

commit v2 on v1

--- a/solution.py
+++ b/solution.py
@@ -16,6 +16,9 @@
 LANES = 128
 TILE = 8
 VMEM_LIMIT = 56 * 1024 * 1024
+
+
+SLOT = {7: 0, 5: 1, 6: 2, 4: 3, 3: 4, 1: 5, 2: 6, 0: 7}
 
 
 def capacity_of(tok_count, top_count, n_exp):
@@ -42,7 +45,7 @@
     out_ref[...] = rows.reshape(out_ref.shape)
 
 
-def gather_rows(rel, n_blocks, pos, x_blk, buffer, capacity):
+def gather_rows(slot, n_blocks, pos, x_blk, buffer, capacity):
     pos_rows, tok_count = pos.shape
     n_exp = pos_rows - TILE
     d_model = x_blk.shape[1]
@@ -60,7 +63,7 @@
         out_shape=jax.ShapeDtypeStruct((n_blocks, n_exp, capacity, d_model), BF16),
         grid=(n_exp // per_step,),
         in_specs=in_specs,
-        out_specs=pl.BlockSpec((1, per_step, capacity, d_model), lambda i: (rel, i, 0, 0)),
+        out_specs=pl.BlockSpec((1, per_step, capacity, d_model), lambda i: (slot, i, 0, 0)),
         scratch_shapes=[pltpu.VMEM((per_step * capacity, tok_count), BF16)],
         input_output_aliases=aliases,
         compiler_params=params(("arbitrary",)),
@@ -94,10 +97,12 @@
     out_ref[...] = out.astype(BF16).reshape(out_ref.shape)
 
 
-def expert_rows(first, count, y_arr, xg, wg, wu, wdt, recv):
-    n_blocks, n_exp, capacity, d_model = xg.shape
+def expert_rows(first, count, slots, y_arr, xg, wg, wu, wdt, recv):
+    n_exp, capacity, d_model = xg.shape[1:]
     half, width = wg.shape[1:]
     per_step = 2
+    skip = slots[0] // per_step
+    n_blocks = slots[1] - slots[0]
     own = pl.BlockSpec((1, half, width), lambda i, m, y: (y[0] * n_exp + first + i, 0, 0))
     return pl.pallas_call(
         functools.partial(expert_kernel, half),
@@ -106,7 +111,7 @@
             num_scalar_prefetch=1,
             grid=(count, n_blocks // per_step),
             in_specs=[
-                pl.BlockSpec((per_step, 1, capacity, d_model), lambda i, m, y: (m, first + i, 0, 0)),
+                pl.BlockSpec((per_step, 1, capacity, d_model), lambda i, m, y: (m + skip, first + i, 0, 0)),
                 own, own, own,
                 pl.BlockSpec((3, 1, half, width), lambda i, m, y: (0, i, 0, 0)),
             ],
@@ -140,10 +145,10 @@
     )(x_blk, wg, wu, wdt)
 
 
-def combine_kernel(rel, n_base, where_of, halves, capacity, group, *refs):
+def combine_kernel(n_base, where_of, halves, capacity, group, *refs):
     cnt_ref, tok_ref, gate_ref = refs[:3]
     bases = refs[3:3 + n_base]
-    n_chunks = max(c for c, _, _ in where_of) + 1
+    n_chunks = max(w[0] for w in where_of) + 1
     outs = refs[3 + n_base:3 + n_base + n_chunks]
     n_out = 2 if halves else 1
     pos = 3 + n_base + n_chunks
@@ -165,8 +170,8 @@
         return pltpu.make_async_copy(tmps.at[0, pl.ds(at, step)], dst, sem_out.at[b])
 
     def row_copy(i):
-        c, local, _ = where_of[i]
-        return pltpu.make_async_copy(outs[c].at[local, rel], rows.at[i % 2], sem_rows.at[i % 2])
+        c, local, slot, _ = where_of[i]
+        return pltpu.make_async_copy(outs[c].at[local, slot], rows.at[i % 2], sem_rows.at[i % 2])
 
     for b in range(n_step):
         for k in range(n_base):
@@ -190,7 +195,7 @@
         row_copy(i).wait()
         if i + 1 < len(where_of):
             row_copy(i + 1).start()
-        e = where_of[i][2]
+        e = where_of[i][3]
         slot = i % 2
 
         @pl.loop(0, capacity // 32)
@@ -205,8 +210,9 @@
             sums, toks = [], []
             for i in range(group):
                 s = q * group + i
-                t = pl.multiple_of(tok_ref[0, e * capacity + s], TILE)
-                g = gate_ref[0, e * capacity + s]
+                t = tok_ref[0, e * capacity + s]
+                g = gate_ref[0, e * tok_count + t]
+                t = pl.multiple_of(t * TILE, TILE)
                 toks.append(t)
                 sums.append(acc[pl.ds(t, TILE), :] + g * wide[pl.ds(pl.multiple_of(s * TILE, TILE), TILE), :])
             for i in range(group):
@@ -225,13 +231,13 @@
         out_copy(b).wait()
 
 
-def combine(rel, cnt, toks, gates, bases, outs, first, halves):
+def combine(cnt, toks, gates, bases, outs, slots, first, halves):
     tok_count, d_model = bases[0].shape
     capacity = outs[0].shape[2]
     where_of = []
     for c, o in enumerate(outs):
         for i in range(o.shape[0]):
-            where_of.append((c, i, first + len(where_of)))
+            where_of.append((c, i, slots[c], first + len(where_of)))
     smem = pl.BlockSpec(memory_space=pltpu.SMEM)
     hbm = pl.BlockSpec(memory_space=pl.ANY)
     n_base = len(bases)
@@ -241,7 +247,7 @@
     else:
         out_shape, out_specs = jax.ShapeDtypeStruct((tok_count, d_model), F32), hbm
     return pl.pallas_call(
-        functools.partial(combine_kernel, rel, n_base, tuple(where_of), halves, capacity, 8),
+        functools.partial(combine_kernel, n_base, tuple(where_of), halves, capacity, 8),
         out_shape=out_shape,
         in_specs=[smem, smem, smem] + [hbm] * (n_base + len(outs)),
         out_specs=out_specs,
@@ -260,6 +266,33 @@
     )(cnt, toks, gates, *bases, *outs)
 
 
+def finish_kernel(n_half, a_ref, b_ref, c_ref, d_ref, out_ref):
+    @pl.when(pl.program_id(0) < n_half)
+    def _():
+        out_ref[...] = (a_ref[...] + b_ref[...]).astype(BF16)
+
+    @pl.when(pl.program_id(0) >= n_half)
+    def _():
+        out_ref[...] = (c_ref[...] + d_ref[...]).astype(BF16)
+
+
+def finish(top_sum, top_late, bot_sum, bot_late):
+    rows, d_model = top_sum.shape
+    tile = 256
+    n_half = rows // tile
+    top = pl.BlockSpec((tile, d_model), lambda i: (jnp.minimum(i, n_half - 1), 0))
+    bot = pl.BlockSpec((tile, d_model), lambda i: (jnp.maximum(i - n_half, 0), 0))
+    return pl.pallas_call(
+        functools.partial(finish_kernel, n_half),
+        out_shape=jax.ShapeDtypeStruct((2 * rows, d_model), BF16),
+        grid=(2 * n_half,),
+        in_specs=[top, top, bot, bot],
+        out_specs=pl.BlockSpec((tile, d_model), lambda i: (i, 0)),
+        compiler_params=params(("arbitrary",)),
+        name="finish",
+    )(top_sum, top_late, bot_sum, bot_late)
+
+
 def solution(mesh):
     exp_n = mesh.shape["expert"]
     data_n = mesh.shape["data"]
@@ -276,6 +309,10 @@
 
     def over_x(v):
         return lax.ppermute(v, "expert", [(i, i ^ 2) for i in range(exp_n)])
+
+    def over_all(v, r):
+        flip = (r & 1) * exp_n + (r >> 1)
+        return lax.ppermute(v, ("data", "expert"), [(i, i ^ flip) for i in range(n_dev)])
 
     def device_fn(x_loc, idx_loc, gate_loc, wg_loc, wu_loc, wd_loc, wsg_loc, wsu_loc, wsd_loc):
         tok_count, d_model = x_loc.shape
@@ -285,11 +322,12 @@
         capacity = capacity_of(tok_count, top, n_local * exp_n)
         y = lax.axis_index("data")
         p = lax.axis_index("expert")
-        me = p * data_n + y
         wdt_loc = jnp.swapaxes(wd_loc, 1, 2)
 
         meta = jnp.concatenate([idx_loc.T.astype(F32), gate_loc.T], axis=0)
-        meta_all = lax.all_gather(meta, group_axes, axis=0)
+        meta_rel = [meta]
+        for r in range(1, n_dev):
+            meta_rel.append(over_all(meta, r))
 
         blocks = [None] * n_dev
         blocks[0] = x_loc
@@ -304,7 +342,11 @@
         ws = jnp.stack([wsg_loc, wsu_loc, wsd_loc.T])
         rows_s, width_s = ws.shape[1], ws.shape[2] // n_dev
         ws = ws.reshape(3, rows_s, n_dev, width_s).transpose(2, 0, 1, 3)
-        ws = lax.all_to_all(ws, group_axes, 0, 0, tiled=True)
+        by_rel = (p * data_n + y) ^ jnp.arange(n_dev, dtype=jnp.int32)
+        ws = jnp.take(ws, by_rel, axis=0)
+        ws_parts = [ws[0]]
+        for r in range(1, n_dev):
+            ws_parts.append(over_all(ws[r], r))
 
         recvs = []
         start = 0
@@ -314,7 +356,7 @@
             recvs.append(over_y(piece))
             start += n
 
-        meta_rel = jnp.take(meta_all, me ^ jnp.arange(n_dev, dtype=jnp.int32), axis=0)
+        meta_rel = jnp.stack(meta_rel)
         ids = meta_rel[:, :top].astype(jnp.int32)
         gts = meta_rel[:, top:]
         mine = p * n_local + y * n_mine + jnp.arange(n_mine, dtype=jnp.int32)
@@ -338,7 +380,7 @@
         def gather(r):
             nonlocal xg
             x_blk = after(blocks[r])
-            xg = gather_rows(r, n_dev, pos_pad[r], x_blk, xg, capacity)
+            xg = gather_rows(SLOT[r], n_dev, pos_pad[r], x_blk, xg, capacity)
             last[0] = xg
 
         base = [None] * n_dev
@@ -346,43 +388,43 @@
 
         def shared(r):
             if not shared_w:
-                whole = after(ws).transpose(1, 0, 2, 3).reshape(3, d_model, width_s)
+                whole = jnp.take(jnp.stack(after(*ws_parts)), by_rel, axis=0)
+                whole = whole.transpose(1, 0, 2, 3).reshape(3, d_model, width_s)
                 shared_w.extend([whole[0], whole[1], whole[2]])
             x_blk = after(blocks[r])
             base[r] = shared_part(x_blk, *shared_w)
             last[0] = base[r]
 
         y_arr = y.astype(jnp.int32).reshape(1)
-        outs = []
-
-        def experts(c):
+
+        def experts(c, slots=(0, n_dev)):
             start = sum(CHUNKS[:c])
-            outs.append(expert_rows(start, CHUNKS[c], y_arr, xg, wg_loc, wu_loc, wdt_loc, after(recvs[c])))
-            last[0] = outs[-1]
+            recv = after(recvs[c])
+            out = expert_rows(start, CHUNKS[c], slots, y_arr, xg, wg_loc, wu_loc, wdt_loc, recv)
+            last[0] = out
+            return out
 
         lists = []
 
         def make_lists():
             p_in, ids_in, gts_in = after(pos, ids, gts)
             hit_in = ids_in[:, None] == mine[None, :, None, None]
-            gate_of = jnp.sum(jnp.where(hit_in, gts_in[:, None], 0.0), axis=2).reshape(n_dev * n_mine, tok_count)
+            gate_of = jnp.sum(jnp.where(hit_in, gts_in[:, None], 0.0), axis=2).reshape(n_dev, 1, n_mine * tok_count)
+            gate_of = jnp.pad(gate_of, ((0, 0), (0, 0), (0, LANES)))
             same = p_in[:, None, :] == jnp.arange(capacity, dtype=jnp.int32)[None, :, None]
             toks = jnp.sum(jnp.where(same, t_ids[None, None, :] - tok_count, 0), axis=2) + tok_count
-            slot_gate = jnp.sum(jnp.where(same, gate_of[:, None, :], 0.0), axis=2)
             count = jnp.sum((p_in >= 0).astype(jnp.int32), axis=1).reshape(n_dev, 1, n_mine)
-            toks = (toks * TILE).reshape(n_dev, 1, n_mine * capacity)
-            slot_gate = slot_gate.reshape(n_dev, 1, n_mine * capacity)
-            lists.extend([count, toks, slot_gate])
-            last[0] = (toks, slot_gate)
-
-        def part(r, bases, first, halves):
-            count, toks, slot_gate = lists
-            c0 = 0
-            while sum(CHUNKS[:c0]) < first:
-                c0 += 1
+            toks = toks.reshape(n_dev, 1, n_mine * capacity)
+            lists.extend([count, toks, gate_of])
+            last[0] = (toks, gate_of)
+
+        def part(r, bases, arrays, first, halves):
+            count, toks, gate_of = lists
+            outs_r = [o for o, _ in arrays]
+            slots_r = [SLOT[r] - s0 for _, s0 in arrays]
             (b0, *rest) = bases
             args = [after(b0), *rest]
-            out = combine(r, count[r], toks[r], slot_gate[r], args, outs[c0:], first, halves)
+            out = combine(count[r], toks[r], gate_of[r], args, outs_r, slots_r, first, halves)
             last[0] = out[0] if halves else out
             return out
 
@@ -395,41 +437,45 @@
         make_lists()
         gather(5)
         gather(7)
-        experts(0)
-        experts(1)
+        early = [(experts(0), 0), (experts(1), 0)]
         shared(7)
         shared(5)
-        experts(2)
+        early.append((experts(2), 0))
         n_pre = sum(CHUNKS[:3])
-        pre7 = part(7, [base[7]], 0, False)
-        pre5 = part(5, [base[5]], 0, False)
-        experts(3)
+        pre7 = part(7, [base[7]], early, 0, False)
+        pre5 = part(5, [base[5]], early, 0, False)
+        early.append((experts(3), 0))
         shared(6)
-        experts(4)
-        mate7 = over_core(part(7, [pre7], n_pre, False))
-        mate6 = over_core(part(6, [base[6]], 0, False))
-        diag = part(5, [pre5, mate7], n_pre, True)
+        pre6 = part(6, [base[6]], early, 0, False)
+        shared(4)
+        shared(3)
+        tail = experts(4, (0, 2))
+        late = [early[3], (tail, 0)]
+        mate7 = over_core(part(7, [pre7], late, n_pre, False))
+        rest = experts(4, (2, n_dev))
+        full = early + [(rest, 2)]
+        diag = part(5, [pre5, mate7], late, n_pre, True)
         diag_x = over_x(diag[0])
         diag_y = over_y(diag[1])
-        shared(4)
-        to_x = part(4, [base[4], mate6], 0, True)
+        mate6 = over_core(part(6, [pre6], [(rest, 2)], n_pre + CHUNKS[3], False))
+        mate3 = over_core(part(3, [base[3]], full, 0, False))
+        to_x = part(4, [base[4], mate6], full, 0, True)
         x_top = over_x(to_x[0])
-        shared(3)
-        mate3 = over_core(part(3, [base[3]], 0, False))
         shared(1)
-        to_y = part(1, [base[1], mate3], 0, True)
+        to_y = part(1, [base[1], mate3], full, 0, True)
         y_bot = over_y(to_y[1])
         shared(2)
-        mate2 = over_core(part(2, [base[2]], 0, False))
+        mate2 = over_core(part(2, [base[2]], full, 0, False))
         shared(0)
-        own = part(0, [base[0], mate2], 0, True)
+        own = part(0, [base[0], mate2], full, 0, True)
         up_x, up_y, to_x1, to_y0 = after(diag_y, diag_x, to_x[1], to_y[0])
         x_bot = over_x(to_x1 + up_x)
         y_top = over_y(to_y0 + up_y)
         h = tok_count // 2
-        top_rows = x_loc[:h].astype(F32) + own[0] + x_top + y_top
-        bot_rows = x_loc[h:].astype(F32) + own[1] + x_bot + y_bot
-        return jnp.concatenate([top_rows.astype(BF16), bot_rows.astype(BF16)], axis=0)
+        sum_top = x_loc[:h].astype(F32) + own[0] + x_top
+        sum_bot = x_loc[h:].astype(F32) + own[1] + y_bot
+        sum_top, sum_bot = lax.optimization_barrier((sum_top, sum_bot))
+        return finish(sum_top, y_top, sum_bot, x_bot)
 
     in_specs = (tok_spec, tok_spec, tok_spec, P("expert", "data", None), P("expert", "data", None), P("expert", None, "data"), P(group_axes, None), P(group_axes, None), P(None, group_axes))
     return jax.shard_map(device_fn, mesh=mesh, in_specs=in_specs, out_specs=tok_spec, check_vma=False)

time: 937 us -> 1110 us (1.18)
  waiting for transfers between devices: 265 us -> 419 us
  Pallas kernels: 496 us -> 527 us
  other arithmetic: 95.6 us -> 67 us
  local copies, waits for them, and re-layouts: 32.7 us -> 50.6 us
  between operations: 14.1 us -> 0.63 us
    ppermute x0 -> x14, waiting for transfers between devices: none -> 105 us  [over_all(): lax.ppermute(v, ('data', 'expert'), [(i, i ^ flip) for i in range(n_dev)])]
    ppermute x9, waiting for transfers between devices: 199 us -> 245 us  [over_y(): return lax.ppermute(v, 'data', [(i, i ^ 1) for i in range(data_n)])]
    reduce_sum x1 -> x0, other arithmetic: 30.6 us -> none  [make_lists(): slot_gate = jnp.sum(jnp.where(same, gate_of[:, None, :], 0.0), axis=2)]
    pallas_call x10 -> x12, Pallas kernels: 150 us -> 177 us  [the longest x11 167 us: combine(): pl.pallas_call(functools.partial(combine_kernel, n_base, tuple(where_of),...]
    unnamed x43 -> x62, local copies, waits for them, and re-layouts: 0.57 us -> 18.6 us
    pallas_call x5 -> x6, Pallas kernels: 121 us -> 124 us  [expert_rows(): pl.pallas_call(functools.partial(expert_kernel, half), out_shape=jax.Shap...]
  transfers between devices with their start and end apart: 24 -> 36, of which waited for: 5 -> 13; matrix products, arithmetic and copies ran while one was open for 13% -> 10% of each run, Pallas kernels for 41% -> 39%
where the time goes in v2:
time: 1110 us; the launch traced here: 1090 us
  Pallas kernels  527 us (47%)
  waiting for transfers between devices  419 us (38%)
  other arithmetic  67 us (6%)
  local copies, waits for them, and re-layouts  50.6 us (5%)
  starting transfers between devices  24.9 us (2%)
    ppermute x9, waiting for transfers between devices, over_y(): return lax.ppermute(v, 'data', [(i, i ^ 1) for i in range(data_n)])  245 us
    pallas_call x11, Pallas kernels, combine(): pl.pallas_call(functools.partial(combine_kernel, n_base, tuple(where_of),...  167 us
    pallas_call x6, Pallas kernels, expert_rows(): pl.pallas_call(functools.partial(expert_kernel, half), out_shape=jax.Shap...  124 us
    pallas_call x8, Pallas kernels, gather_rows(): pl.pallas_call(functools.partial(gather_kernel, per_step, capacity), out_...  118 us
    pallas_call x8, Pallas kernels, shared_part(): pl.pallas_call(shared_kernel, out_shape=jax.ShapeDtypeStruct((tok_count,...  109 us
    ppermute x14, waiting for transfers between devices, over_all(): lax.ppermute(v, ('data', 'expert'), [(i, i ^ flip) for i in range(n_dev)])  105 us
    ppermute x5, waiting for transfers between devices, over_x(): return lax.ppermute(v, 'expert', [(i, i ^ 2) for i in range(exp_n)])  69.8 us
    reduce_sum x1, other arithmetic, make_lists(): jnp.sum(jnp.where(same, t_ids[None, None, :] - tok_count, 0), axis=2)  30.7 us
  transfers between devices with their start and end apart: 36, of which 13 were waited for; matrix products, arithmetic and copies ran while one was open for 10% of the time, Pallas kernels for 39%

profile of v2, /device:TPU:6, one launch (start us, length us, event | category | flops | bytes accessed | tf_op | source)
XLA Modules:
  0.0 1090.7 jit_solution(10698808847364650674)
XLA Ops:
  10.4 2.2 maximum_bitcast_fusion
  12.6 2.7 gather_fusion
  21.3 2.2 dynamic-slice_bitcast_fusion
  23.5 3.7 dynamic-slice_bitcast_fusion.1
  27.3 2.0 pad_maximum_fusion.2
  29.2 1.9 pad_maximum_fusion.1
  31.2 2.0 pad_maximum_fusion
  34.9 1.8 slice_bitcast_fusion
  39.0 51.0 %collective-permute-done.8.x_ref = bf16[2048,896]{1,0:T(8,128)(2,1)} collective-permute-done((bf16[2048,896]{1,0:T(8,128)(2,1)}, bf16[2048,896]{1,0:T(8,128)(2,1)}, u32[]{:S(2)}, u32[]{:S(2)}) %collective-permute-start.8) | collective-permute-done | bytes 3670048 | tf_op jit(solution)/shard_map/ppermute | solution.py:305
  94.4 79.9 %collective-permute-done.3 = f32[16,2048]{1,0:T(8,128)S(1)} collective-permute-done((f32[16,2048]{1,0:T(8,128)}, f32[16,2048]{1,0:T(8,128)S(1)}, u32[]{:S(2)}, u32[]{:S(2)}) %collective-permute-start.3) | collective-permute-done | bytes 131104 | tf_op jit(solution)/shard_map/ppermute | solution.py:315
  174.6 5.9 collective-permute-done.4
  180.5 5.1 collective-permute-done.5
  186.1 5.8 collective-permute-done.6
  198.1 14.7 %gather_rows.8.refs_0_ = bf16[8,8,320,896]{3,2,1,0:T(8,128)(2,1)} custom-call(s32[16,2048]{1,0:T(8,128)} %get-tuple-element.155.pos_ref, bf16[2048,896]{1,0:T(8,128)(2,1)} %x_ref.1), custom_call_target="tpu_custom_call" | custom-call | flops 146800640 | bytes 4587520 | tf_op jit(solution)/shard_map/gather_rows/pallas_call | solution.py:61
  214.6 14.6 %gather_rows.9.refs_0_ = bf16[8,8,320,896]{3,2,1,0:T(8,128)(2,1)} custom-call(s32[16,2048]{1,0:T(8,128)} %get-tuple-element.154.pos_ref, bf16[2048,896]{1,0:T(8,128)(2,1)} %copy-done.2, bf16[8,8,320,896]{3,2,1,0:T(8,128)(2,1)} %gather_rows.8.refs_0_), custom_call_target="tpu_custom_call", output_to_operand_aliasing={{}: (2, {})} | custom-call | flops 146800640 | bytes 4587520 | tf_op jit(solution)/shard_map/gather_rows/pallas_call | solution.py:61
  229.2 15.1 %gather_rows.10.refs_0_ = bf16[8,8,320,896]{3,2,1,0:T(8,128)(2,1)} custom-call(s32[16,2048]{1,0:T(8,128)} %get-tuple-element.153.pos_ref, bf16[2048,896]{1,0:T(8,128)(2,1)} %collective-permute-done.8.x_ref, bf16[8,8,320,896]{3,2,1,0:T(8,128)(2,1)} %gather_rows.9.refs_0_), custom_call_target="tpu_custom_call", output_to_operand_aliasing={{}: (2, {})} | custom-call | flops 146800640 | bytes 4587520 | tf_op jit(solution)/shard_map/gather_rows/pallas_call | solution.py:61
  244.3 14.6 %gather_rows.11.refs_0_ = bf16[8,8,320,896]{3,2,1,0:T(8,128)(2,1)} custom-call(s32[16,2048]{1,0:T(8,128)} %get-tuple-element.152.pos_ref, bf16[2048,896]{1,0:T(8,128)(2,1)} %collective-permute-done.9.x_ref, bf16[8,8,320,896]{3,2,1,0:T(8,128)(2,1)} %gather_rows.10.refs_0_), custom_call_target="tpu_custom_call", output_to_operand_aliasing={{}: (2, {})} | custom-call | flops 146800640 | bytes 4587520 | tf_op jit(solution)/shard_map/gather_rows/pallas_call | solution.py:61
  259.0 2.1 collective-permute-start.14
  261.0 14.6 %gather_rows.12.refs_0_ = bf16[8,8,320,896]{3,2,1,0:T(8,128)(2,1)} custom-call(s32[16,2048]{1,0:T(8,128)} %get-tuple-element.151.pos_ref, bf16[2048,896]{1,0:T(8,128)(2,1)} %collective-permute-done.10.x_ref, bf16[8,8,320,896]{3,2,1,0:T(8,128)(2,1)} %gather_rows.11.refs_0_), custom_call_target="tpu_custom_call", output_to_operand_aliasing={{}: (2, {})} | custom-call | flops 146800640 | bytes 4587520 | tf_op jit(solution)/shard_map/gather_rows/pallas_call | solution.py:61
  275.7 14.7 %gather_rows.13.refs_0_ = bf16[8,8,320,896]{3,2,1,0:T(8,128)(2,1)} custom-call(s32[16,2048]{1,0:T(8,128)} %get-tuple-element.157.pos_ref, bf16[2048,896]{1,0:T(8,128)(2,1)} %collective-permute-done.11.x_ref, bf16[8,8,320,896]{3,2,1,0:T(8,128)(2,1)} %gather_rows.12.refs_0_), custom_call_target="tpu_custom_call", output_to_operand_aliasing={{}: (2, {})} | custom-call | flops 146800640 | bytes 4587520 | tf_op jit(solution)/shard_map/gather_rows/pallas_call | solution.py:61
  290.6 30.7 %select_reduce_fusion = s32[64,320]{1,0:T(8,128)S(1)} fusion(s32[2048]{0:T(1024)S(1)} %iota_add_fusion, s32[64,2048]{1,0:T(8,128)S(1)} %fusion.3), kind=kLoop, calls=%fused_computation.2 | loop fusion | flops 125808640 | bytes 614400 | tf_op jit(solution)/shard_map/reduce_sum | solution.py:415
  328.8 8.3 collective-permute-done.20
  337.9 7.9 collective-permute-done.14.rv_ref
  346.5 73.1 %collective-permute-done.15.rv_ref = bf16[3,2,448,640]{3,2,1,0:T(8,128)(2,1)} collective-permute-done((bf16[3,2,448,640]{3,2,1,0:T(8,128)(2,1)}, bf16[3,2,448,640]{3,2,1,0:T(8,128)(2,1)}, u32[]{:S(2)}, u32[]{:S(2)}) %collective-permute-start.15) | collective-permute-done | bytes 3440672 | tf_op jit(solution)/shard_map/ppermute | solution.py:305
  419.6 2.0 collective-permute-start.16
  421.6 14.6 %gather_rows.14.refs_0_ = bf16[8,8,320,896]{3,2,1,0:T(8,128)(2,1)} custom-call(s32[16,2048]{1,0:T(8,128)} %get-tuple-element.150.pos_ref, bf16[2048,896]{1,0:T(8,128)(2,1)} %collective-permute-done.12.x_ref, bf16[8,8,320,896]{3,2,1,0:T(8,128)(2,1)} %gather_rows.13.refs_0_), custom_call_target="tpu_custom_call", output_to_operand_aliasing={{}: (2, {})} | custom-call | flops 146800640 | bytes 4587520 | tf_op jit(solution)/shard_map/gather_rows/pallas_call | solution.py:61
  437.1 14.8 %gather_rows.15.xg_ref = bf16[8,8,320,896]{3,2,1,0:T(8,128)(2,1)} custom-call(s32[16,2048]{1,0:T(8,128)} %get-tuple-element.156.pos_ref, bf16[2048,896]{1,0:T(8,128)(2,1)} %collective-permute-done.13.x_ref, bf16[8,8,320,896]{3,2,1,0:T(8,128)(2,1)} %gather_rows.14.refs_0_), custom_call_target="tpu_custom_call", output_to_operand_aliasing={{}: (2, {})} | custom-call | flops 146800640 | bytes 4587520 | tf_op jit(solution)/shard_map/gather_rows/pallas_call | solution.py:61
  451.9 29.2 %expert_rows.6.refs_4_.refs_5_ = bf16[2,8,320,896]{3,2,1,0:T(8,128)(2,1)} custom-call(s32[1]{0:T(128)} %bitcast.32.y_ref, bf16[8,8,320,896]{3,2,1,0:T(8,128)(2,1)} %gather_rows.15.xg_ref, bf16[16,448,640]{2,1,0:T(8,128)(2,1)} %og_ref.11, bf16[16,448,640]{2,1,0:T(8,128)(2,1)} %ou_ref.11, bf16[16,448,640]{2,1,0:T(8,128)(2,1)} %bitcast.167, ...), custom_call_target="tpu_custom_call" | custom-call | flops 275251200 | bytes 18350080 | tf_op jit(solution)/shard_map/expert_rows/pallas_call | solution.py:107
  481.2 29.4 %expert_rows.7.refs_5_.refs_6_ = bf16[2,8,320,896]{3,2,1,0:T(8,128)(2,1)} custom-call(s32[1]{0:T(128)} %bitcast.32.y_ref, bf16[8,8,320,896]{3,2,1,0:T(8,128)(2,1)} %gather_rows.15.xg_ref, bf16[16,448,640]{2,1,0:T(8,128)(2,1)} %og_ref.11, bf16[16,448,640]{2,1,0:T(8,128)(2,1)} %ou_ref.11, bf16[16,448,640]{2,1,0:T(8,128)(2,1)} %bitcast.168, ...), custom_call_target="tpu_custom_call" | custom-call | flops 275251200 | bytes 18350080 | tf_op jit(solution)/shard_map/expert_rows/pallas_call | solution.py:107
  510.6 2.0 collective-permute-start.25
  517.4 1.8 bitcast_dynamic-update-slice_fusion.1
  520.0 3.3 gather_fusion.1
  523.7 1.9 fusion.14
  525.6 13.6 %shared_part.8.refs_3_ = f32[2048,896]{1,0:T(8,128)} custom-call(bf16[2048,896]{1,0:T(8,128)(2,1)} %collective-permute-done.13.x_ref, bf16[896,640]{1,0:T(8,128)(2,1)} %bitcast.189, bf16[896,640]{1,0:T(8,128)(2,1)} %bitcast.181, bf16[896,640]{1,0:T(8,128)(2,1)} %bitcast.173), custom_call_target="tpu_custom_call" | custom-call | flops 110100480 | bytes 11010048 | tf_op jit(solution)/shard_map/shared_part/pallas_call | solution.py:136
  539.2 13.8 %shared_part.9.refs_3_ = f32[2048,896]{1,0:T(8,128)} custom-call(bf16[2048,896]{1,0:T(8,128)(2,1)} %collective-permute-done.12.x_ref, bf16[896,640]{1,0:T(8,128)(2,1)} %bitcast.190, bf16[896,640]{1,0:T(8,128)(2,1)} %bitcast.182, bf16[896,640]{1,0:T(8,128)(2,1)} %bitcast.174), custom_call_target="tpu_custom_call" | custom-call | flops 110100480 | bytes 11010048 | tf_op jit(solution)/shard_map/shared_part/pallas_call | solution.py:136
  553.0 29.4 %expert_rows.8.refs_6_.refs_7_ = bf16[2,8,320,896]{3,2,1,0:T(8,128)(2,1)} custom-call(s32[1]{0:T(128)} %bitcast.32.y_ref, bf16[8,8,320,896]{3,2,1,0:T(8,128)(2,1)} %gather_rows.15.xg_ref, bf16[16,448,640]{2,1,0:T(8,128)(2,1)} %og_ref.11, bf16[16,448,640]{2,1,0:T(8,128)(2,1)} %ou_ref.11, bf16[16,448,640]{2,1,0:T(8,128)(2,1)} %bitcast.169, ...), custom_call_target="tpu_custom_call" | custom-call | flops 275251200 | bytes 18350080 | tf_op jit(solution)/shard_map/expert_rows/pallas_call | solution.py:107
  582.3 14.9 %combine.11.refs_3_ = f32[2048,896]{1,0:T(8,128)} custom-call(s32[1,8]{1,0:T(1,128)} %get-tuple-element.167.refs_0_, s32[1,2560]{1,0:T(1,128)} %squeeze.168.refs_1_, f32[1,16512]{1,0:T(1,128)} %get-tuple-element.148.refs_2_, f32[2048,896]{1,0:T(8,128)} %shared_part.8.refs_3_, bf16[2,8,320,896]{3,2,1,0:T(8,128)(2,1)} %expert_rows.6.refs_4_.refs_5_, ...), custom_call_target="tpu_custom_call" | custom-call | flops 55050240 | bytes 14680064 | tf_op jit(solution)/shard_map/combine/pallas_call | solution.py:249
  597.2 14.7 %combine.12.refs_3_ = f32[2048,896]{1,0:T(8,128)} custom-call(s32[1,8]{1,0:T(1,128)} %get-tuple-element.168.refs_0_, s32[1,2560]{1,0:T(1,128)} %squeeze.163.refs_1_, f32[1,16512]{1,0:T(1,128)} %get-tuple-element.147.refs_2_, f32[2048,896]{1,0:T(8,128)} %shared_part.9.refs_3_, bf16[2,8,320,896]{3,2,1,0:T(8,128)(2,1)} %expert_rows.6.refs_4_.refs_5_, ...), custom_call_target="tpu_custom_call" | custom-call | flops 55050240 | bytes 14680064 | tf_op jit(solution)/shard_map/combine/pallas_call | solution.py:249
  612.0 16.1 %expert_rows.9.refs_7_.refs_4_.refs_5_.refs_8_ = bf16[1,8,320,896]{3,2,1,0:T(8,128)(2,1)} custom-call(s32[1]{0:T(128)} %bitcast.32.y_ref, bf16[8,8,320,896]{3,2,1,0:T(8,128)(2,1)} %gather_rows.15.xg_ref, bf16[16,448,640]{2,1,0:T(8,128)(2,1)} %og_ref.11, bf16[16,448,640]{2,1,0:T(8,128)(2,1)} %ou_ref.11, bf16[16,448,640]{2,1,0:T(8,128)(2,1)} %bitcast.170, ...), custom_call_target="tpu_custom_call" | custom-call | flops 137625600 | bytes 9175040 | tf_op jit(solution)/shard_map/expert_rows/pallas_call | solution.py:107
  628.1 13.6 %shared_part.10.refs_3_ = f32[2048,896]{1,0:T(8,128)} custom-call(bf16[2048,896]{1,0:T(8,128)(2,1)} %collective-permute-done.11.x_ref, bf16[896,640]{1,0:T(8,128)(2,1)} %bitcast.191, bf16[896,640]{1,0:T(8,128)(2,1)} %bitcast.183, bf16[896,640]{1,0:T(8,128)(2,1)} %bitcast.175), custom_call_target="tpu_custom_call" | custom-call | flops 110100480 | bytes 11010048 | tf_op jit(solution)/shard_map/shared_part/pallas_call | solution.py:136
  641.6 15.6 %combine.13.refs_3_ = f32[2048,896]{1,0:T(8,128)} custom-call(s32[1,8]{1,0:T(1,128)} %get-tuple-element.169.refs_0_, s32[1,2560]{1,0:T(1,128)} %squeeze.160.refs_1_, f32[1,16512]{1,0:T(1,128)} %get-tuple-element.146.refs_2_, f32[2048,896]{1,0:T(8,128)} %shared_part.10.refs_3_, bf16[2,8,320,896]{3,2,1,0:T(8,128)(2,1)} %expert_rows.6.refs_4_.refs_5_, ...), custom_call_target="tpu_custom_call" | custom-call | flops 64225280 | bytes 14680064 | tf_op jit(solution)/shard_map/combine/pallas_call | solution.py:249
  657.2 13.6 %shared_part.11.refs_3_ = f32[2048,896]{1,0:T(8,128)} custom-call(bf16[2048,896]{1,0:T(8,128)(2,1)} %collective-permute-done.9.x_ref, bf16[896,640]{1,0:T(8,128)(2,1)} %bitcast.192, bf16[896,640]{1,0:T(8,128)(2,1)} %bitcast.184, bf16[896,640]{1,0:T(8,128)(2,1)} %bitcast.176), custom_call_target="tpu_custom_call" | custom-call | flops 110100480 | bytes 11010048 | tf_op jit(solution)/shard_map/shared_part/pallas_call | solution.py:136
  670.8 13.6 %shared_part.12.refs_3_ = f32[2048,896]{1,0:T(8,128)} custom-call(bf16[2048,896]{1,0:T(8,128)(2,1)} %collective-permute-done.10.x_ref, bf16[896,640]{1,0:T(8,128)(2,1)} %bitcast.193, bf16[896,640]{1,0:T(8,128)(2,1)} %bitcast.185, bf16[896,640]{1,0:T(8,128)(2,1)} %bitcast.177), custom_call_target="tpu_custom_call" | custom-call | flops 110100480 | bytes 11010048 | tf_op jit(solution)/shard_map/shared_part/pallas_call | solution.py:136
  684.4 6.6 expert_rows.10.refs_5_.refs_6_
  691.0 9.9 combine.14
  700.9 13.0 %expert_rows.11.refs_4_.refs_8_.refs_9_ = bf16[1,6,320,896]{3,2,1,0:T(8,128)(2,1)} custom-call(s32[1]{0:T(128)} %bitcast.32.y_ref, bf16[8,8,320,896]{3,2,1,0:T(8,128)(2,1)} %gather_rows.15.xg_ref, bf16[16,448,640]{2,1,0:T(8,128)(2,1)} %og_ref.11, bf16[16,448,640]{2,1,0:T(8,128)(2,1)} %ou_ref.11, bf16[16,448,640]{2,1,0:T(8,128)(2,1)} %bitcast.172, ...), custom_call_target="tpu_custom_call" | custom-call | flops 103219200 | bytes 6881280 | tf_op jit(solution)/shard_map/expert_rows/pallas_call | solution.py:107
  714.0 2.9 copy-done.4
  716.9 12.8 %combine.15 = (f32[1024,896]{1,0:T(8,128)}, f32[1024,896]{1,0:T(8,128)}) custom-call(s32[1,8]{1,0:T(1,128)} %get-tuple-element.168.refs_0_, s32[1,2560]{1,0:T(1,128)} %squeeze.163.refs_1_, f32[1,16512]{1,0:T(1,128)} %get-tuple-element.147.refs_2_, f32[2048,896]{1,0:T(8,128)} %combine.12.refs_3_, f32[2048,896]{1,0:T(8,128)} %copy-done.4, ...), custom_call_target="tpu_custom_call" | custom-call | flops 18350080 | bytes 14680064 | tf_op jit(solution)/shard_map/combine/pallas_call | solution.py:249
  729.7 9.3 combine.16
  739.9 16.6 %combine.17 = f32[2048,896]{1,0:T(8,128)} custom-call(s32[1,8]{1,0:T(1,128)} %get-tuple-element.170.refs_0_, s32[1,2560]{1,0:T(1,128)} %squeeze.157.refs_1_, f32[1,16512]{1,0:T(1,128)} %get-tuple-element.145.refs_2_, f32[2048,896]{1,0:T(8,128)} %shared_part.12.refs_3_, bf16[2,8,320,896]{3,2,1,0:T(8,128)(2,1)} %expert_rows.6.refs_4_.refs_5_, ...), custom_call_target="tpu_custom_call" | custom-call | flops 73400320 | bytes 14680064 | tf_op jit(solution)/shard_map/combine/pallas_call | solution.py:249
  758.7 19.2 %combine.18 = (f32[1024,896]{1,0:T(8,128)}, f32[1024,896]{1,0:T(8,128)}) custom-call(s32[1,8]{1,0:T(1,128)} %get-tuple-element.171.refs_0_, s32[1,2560]{1,0:T(1,128)} %squeeze.154.refs_1_, f32[1,16512]{1,0:T(1,128)} %get-tuple-element.144.refs_2_, f32[2048,896]{1,0:T(8,128)} %shared_part.11.refs_3_, f32[2048,896]{1,0:T(8,128)} %collective-permute-done.27.refs_4_, ...), custom_call_target="tpu_custom_call" | custom-call | flops 73400320 | bytes 14680064 | tf_op jit(solution)/shard_map/combine/pallas_call | solution.py:249
  777.9 13.6 %shared_part.13.refs_3_ = f32[2048,896]{1,0:T(8,128)} custom-call(bf16[2048,896]{1,0:T(8,128)(2,1)} %collective-permute-done.8.x_ref, bf16[896,640]{1,0:T(8,128)(2,1)} %bitcast.194, bf16[896,640]{1,0:T(8,128)(2,1)} %bitcast.186, bf16[896,640]{1,0:T(8,128)(2,1)} %bitcast.178), custom_call_target="tpu_custom_call" | custom-call | flops 110100480 | bytes 11010048 | tf_op jit(solution)/shard_map/shared_part/pallas_call | solution.py:136
  791.4 19.1 %combine.19 = (f32[1024,896]{1,0:T(8,128)}, f32[1024,896]{1,0:T(8,128)}) custom-call(s32[1,8]{1,0:T(1,128)} %get-tuple-element.166.refs_0_, s32[1,2560]{1,0:T(1,128)} %squeeze.151.refs_1_, f32[1,16512]{1,0:T(1,128)} %get-tuple-element.142.refs_2_, f32[2048,896]{1,0:T(8,128)} %shared_part.13.refs_3_, f32[2048,896]{1,0:T(8,128)} %collective-permute-done.28.refs_4_, ...), custom_call_target="tpu_custom_call" | custom-call | flops 73400320 | bytes 14680064 | tf_op jit(solution)/shard_map/combine/pallas_call | solution.py:249
  810.5 13.6 %shared_part.14.refs_3_ = f32[2048,896]{1,0:T(8,128)} custom-call(bf16[2048,896]{1,0:T(8,128)(2,1)} %copy-done.2, bf16[896,640]{1,0:T(8,128)(2,1)} %bitcast.195, bf16[896,640]{1,0:T(8,128)(2,1)} %bitcast.187, bf16[896,640]{1,0:T(8,128)(2,1)} %bitcast.179), custom_call_target="tpu_custom_call" | custom-call | flops 110100480 | bytes 11010048 | tf_op jit(solution)/shard_map/shared_part/pallas_call | solution.py:136
  824.1 16.3 %combine.20 = f32[2048,896]{1,0:T(8,128)} custom-call(s32[1,8]{1,0:T(1,128)} %get-tuple-element.172.refs_0_, s32[1,2560]{1,0:T(1,128)} %squeeze.148.refs_1_, f32[1,16512]{1,0:T(1,128)} %get-tuple-element.143.refs_2_, f32[2048,896]{1,0:T(8,128)} %shared_part.14.refs_3_, bf16[2,8,320,896]{3,2,1,0:T(8,128)(2,1)} %expert_rows.6.refs_4_.refs_5_, ...), custom_call_target="tpu_custom_call" | custom-call | flops 73400320 | bytes 14680064 | tf_op jit(solution)/shard_map/combine/pallas_call | solution.py:249
  846.4 13.6 %shared_part.15.refs_3_ = f32[2048,896]{1,0:T(8,128)} custom-call(bf16[2048,896]{1,0:T(8,128)(2,1)} %x_ref.1, bf16[896,640]{1,0:T(8,128)(2,1)} %bitcast.196, bf16[896,640]{1,0:T(8,128)(2,1)} %bitcast.188, bf16[896,640]{1,0:T(8,128)(2,1)} %bitcast.180), custom_call_target="tpu_custom_call" | custom-call | flops 110100480 | bytes 11010048 | tf_op jit(solution)/shard_map/shared_part/pallas_call | solution.py:136
  860.0 18.9 %combine.21 = (f32[1024,896]{1,0:T(8,128)}, f32[1024,896]{1,0:T(8,128)}) custom-call(s32[1,8]{1,0:T(1,128)} %get-tuple-element.173.refs_0_, s32[1,2560]{1,0:T(1,128)} %squeeze.145.refs_1_, f32[1,16512]{1,0:T(1,128)} %get-tuple-element.149.refs_2_, f32[2048,896]{1,0:T(8,128)} %shared_part.15.refs_3_, f32[2048,896]{1,0:T(8,128)} %collective-permute-done.29.refs_4_, ...), custom_call_target="tpu_custom_call" | custom-call | flops 73400320 | bytes 14680064 | tf_op jit(solution)/shard_map/combine/pallas_call | solution.py:249
  878.9 45.3 %collective-permute-done.32 = f32[1024,896]{1,0:T(8,128)} collective-permute-done((f32[1024,896]{1,0:T(8,128)}, f32[1024,896]{1,0:T(8,128)}, u32[]{:S(2)}, u32[]{:S(2)}) %collective-permute-start.32) | collective-permute-done | bytes 3670048 | tf_op jit(solution)/shard_map/ppermute | solution.py:305
  925.1 4.4 add.119
  929.8 4.5 add.118
  935.6 67.2 %collective-permute-done.31 = f32[1024,896]{1,0:T(8,128)} collective-permute-done((f32[1024,896]{1,0:T(8,128)}, f32[1024,896]{1,0:T(8,128)}, u32[]{:S(2)}, u32[]{:S(2)}) %collective-permute-start.31) | collective-permute-done | bytes 3670048 | tf_op jit(solution)/shard_map/ppermute | solution.py:305
  1003.7 9.4 add_add_fusion
  1013.1 68.1 %collective-permute-done.35.d_ref = f32[1024,896]{1,0:T(8,128)} collective-permute-done((f32[1024,896]{1,0:T(8,128)}, f32[1024,896]{1,0:T(8,128)}, u32[]{:S(2)}, u32[]{:S(2)}) %collective-permute-start.35) | collective-permute-done | bytes 3670048 | tf_op jit(solution)/shard_map/ppermute | solution.py:311
  1081.2 9.4 finish.1
  (156 shorter events, 62.1 us)
Async XLA Ops:
  0.0 7.7 copy-start.11
  2.4 89.5 %collective-permute-start.2 = (f32[16,2048]{1,0:T(8,128)}, f32[16,2048]{1,0:T(8,128)}, u32[]{:S(2)}, u32[]{:S(2)}) collective-permute-start(f32[16,2048]{1,0:T(8,128)} %pad_maximum_fusion.5), channel_id=1, source_target_pairs={{0,5},{1,4},{2,7},{3,6},{4,1},{5,0},{6,3},{7,2}} | collective-permute-start | bytes 393224 | tf_op jit(solution)/shard_map/ppermute | solution.py:315
  2.4 88.1 %collective-permute-start.1 = (f32[16,2048]{1,0:T(8,128)}, f32[16,2048]{1,0:T(8,128)}, u32[]{:S(2)}, u32[]{:S(2)}) collective-permute-start(f32[16,2048]{1,0:T(8,128)} %pad_maximum_fusion.5), channel_id=1, source_target_pairs={{0,1},{1,0},{2,3},{3,2},{4,5},{5,4},{6,7},{7,6}} | collective-permute-start | bytes 393224 | tf_op jit(solution)/shard_map/ppermute | solution.py:315
  3.1 33.6 %collective-permute-start = (f32[16,2048]{1,0:T(8,128)}, f32[16,2048]{1,0:T(8,128)}, u32[]{:S(2)}, u32[]{:S(2)}) collective-permute-start(f32[16,2048]{1,0:T(8,128)} %pad_maximum_fusion.5), channel_id=1, source_target_pairs={{0,4},{1,5},{2,6},{3,7},{4,0},{5,1},{6,2},{7,3}} | collective-permute-start | bytes 393224 | tf_op jit(solution)/shard_map/ppermute | solution.py:315
  4.6 85.4 %collective-permute-start.8 = (bf16[2048,896]{1,0:T(8,128)(2,1)}, bf16[2048,896]{1,0:T(8,128)(2,1)}, u32[]{:S(2)}, u32[]{:S(2)}) collective-permute-start(bf16[2048,896]{1,0:T(8,128)(2,1)} %x_ref.1), channel_id=1, source_target_pairs={{0,4},{4,0},{1,5},{5,1},{2,6},{6,2},{3,7},{7,3}} | collective-permute-start | bytes 11010056 | tf_op jit(solution)/shard_map/ppermute | solution.py:305
  5.1 85.5 %collective-permute-start.9 = (bf16[2048,896]{1,0:T(8,128)(2,1)}, bf16[2048,896]{1,0:T(8,128)(2,1)}, u32[]{:S(2)}, u32[]{:S(2)}) collective-permute-start(bf16[2048,896]{1,0:T(8,128)(2,1)} %x_ref.1), channel_id=1, source_target_pairs={{0,2},{1,3},{2,0},{3,1},{4,6},{5,7},{6,4},{7,5}} | collective-permute-start | bytes 11010056 | tf_op jit(solution)/shard_map/ppermute | solution.py:311
  6.6 2.5 copy-start.12
  12.6 2.7 copy-start.20
  15.3 17.8 %copy-start.21 = (pred[8]{0:T(512)(128)(4,1)}, pred[8]{0:T(512)(128)(4,1)S(1)}, u32[]{:S(2)}) copy-start(pred[8]{0:T(512)(128)(4,1)S(1)} %compare_and_fusion) | copy-start | bytes 28
  31.2 2.0 copy-start.14
  31.2 3.3 copy-start.3
  34.8 3.3 copy-start
  38.1 174.6 %collective-permute-start.7 = (bf16[2048,896]{1,0:T(8,128)(2,1)S(1)}, bf16[2048,896]{1,0:T(8,128)(2,1)S(1)}, u32[]{:S(2)}, u32[]{:S(2)}) collective-permute-start(bf16[2048,896]{1,0:T(8,128)(2,1)S(1)} %copy-done), channel_id=1, source_target_pairs={{0,1},{1,0},{2,3},{3,2},{4,5},{5,4},{6,7},{7,6}} | collective-permute-start | bytes 11010056 | tf_op jit(solution)/shard_map/ppermute | solution.py:308
  90.0 200.4 %collective-permute-start.12 = (bf16[2048,896]{1,0:T(8,128)(2,1)}, bf16[2048,896]{1,0:T(8,128)(2,1)}, u32[]{:S(2)}, u32[]{:S(2)}) collective-permute-start(bf16[2048,896]{1,0:T(8,128)(2,1)} %collective-permute-done.8.x_ref), channel_id=1, source_target_pairs={{0,2},{1,3},{2,0},{3,1},{4,6},{5,7},{6,4},{7,5}} | collective-permute-start | bytes 11010056 | tf_op jit(solution)/shard_map/ppermute | solution.py:311
  90.6 168.4 %collective-permute-start.10 = (bf16[2048,896]{1,0:T(8,128)(2,1)}, bf16[2048,896]{1,0:T(8,128)(2,1)}, u32[]{:S(2)}, u32[]{:S(2)}) collective-permute-start(bf16[2048,896]{1,0:T(8,128)(2,1)} %collective-permute-done.8.x_ref), channel_id=1, source_target_pairs={{0,1},{1,0},{2,3},{3,2},{4,5},{5,4},{6,7},{7,6}} | collective-permute-start | bytes 11010056 | tf_op jit(solution)/shard_map/ppermute | solution.py:308
  90.6 185.1 %collective-permute-start.11 = (bf16[2048,896]{1,0:T(8,128)(2,1)}, bf16[2048,896]{1,0:T(8,128)(2,1)}, u32[]{:S(2)}, u32[]{:S(2)}) collective-permute-start(bf16[2048,896]{1,0:T(8,128)(2,1)} %collective-permute-done.9.x_ref), channel_id=1, source_target_pairs={{0,1},{1,0},{2,3},{3,2},{4,5},{5,4},{6,7},{7,6}} | collective-permute-start | bytes 11010056 | tf_op jit(solution)/shard_map/ppermute | solution.py:308
  92.0 82.4 %collective-permute-start.3 = (f32[16,2048]{1,0:T(8,128)}, f32[16,2048]{1,0:T(8,128)S(1)}, u32[]{:S(2)}, u32[]{:S(2)}) collective-permute-start(f32[16,2048]{1,0:T(8,128)} %pad_maximum_fusion.5), channel_id=1, source_target_pairs={{0,2},{1,3},{2,0},{3,1},{4,6},{5,7},{6,4},{7,5}} | collective-permute-start | bytes 393224 | tf_op jit(solution)/shard_map/ppermute | solution.py:315
  174.4 6.1 collective-permute-start.4
  180.5 5.1 collective-permute-start.5
  185.5 6.3 collective-permute-start.6
  191.8 132.0 %collective-permute-start.22 = (bf16[3,112,640]{2,1,0:T(8,128)(2,1)}, bf16[3,112,640]{2,1,0:T(8,128)(2,1)S(1)}, u32[]{:S(2)}, u32[]{:S(2)}) collective-permute-start(bf16[3,112,640]{2,1,0:T(8,128)(2,1)} %get-tuple-element.132), channel_id=1, source_target_pairs={{0,7},{1,6},{2,5},{3,4},{4,3},{5,2},{6,1},{7,0}} | collective-permute-start | bytes 1290248 | tf_op jit(solution)/shard_map/ppermute | solution.py:315
  193.5 0.8 copy-start.5
  212.7 1.8 copy-start.2
  212.7 112.8 %collective-permute-start.21 = (bf16[3,112,640]{2,1,0:T(8,128)(2,1)}, bf16[3,112,640]{2,1,0:T(8,128)(2,1)}, u32[]{:S(2)}, u32[]{:S(2)}) collective-permute-start(bf16[3,112,640]{2,1,0:T(8,128)(2,1)} %get-tuple-element.133), channel_id=1, source_target_pairs={{0,3},{1,2},{2,1},{3,0},{4,7},{5,6},{6,5},{7,4}} | collective-permute-start | bytes 1290248 | tf_op jit(solution)/shard_map/ppermute | solution.py:315
  259.0 86.9 %collective-permute-start.14 = (bf16[3,2,448,640]{3,2,1,0:T(8,128)(2,1)}, bf16[3,2,448,640]{3,2,1,0:T(8,128)(2,1)}, u32[]{:S(2)}, u32[]{:S(2)}) collective-permute-start(bf16[3,2,448,640]{3,2,1,0:T(8,128)(2,1)} %pad_maximum_fusion), channel_id=1, source_target_pairs={{0,4},{4,0},{1,5},{5,1},{2,6},{6,2},{3,7},{7,3}} | collective-permute-start | bytes 10321928 | tf_op jit(solution)/shard_map/ppermute | solution.py:305
  275.7 143.9 %collective-permute-start.15 = (bf16[3,2,448,640]{3,2,1,0:T(8,128)(2,1)}, bf16[3,2,448,640]{3,2,1,0:T(8,128)(2,1)}, u32[]{:S(2)}, u32[]{:S(2)}) collective-permute-start(bf16[3,2,448,640]{3,2,1,0:T(8,128)(2,1)} %pad_maximum_fusion.1), channel_id=1, source_target_pairs={{0,4},{4,0},{1,5},{5,1},{2,6},{6,2},{3,7},{7,3}} | collective-permute-start | bytes 10321928 | tf_op jit(solution)/shard_map/ppermute | solution.py:305
  275.7 45.6 %copy-start.6 = (s32[8,8,2048]{2,1,0:T(8,128)S(1)}, s32[8,8,2048]{2,1,0:T(8,128)}, u32[]{:S(2)}) copy-start(s32[8,8,2048]{2,1,0:T(8,128)} %copy-done.5) | copy-start | bytes 1572868
  275.7 45.6 %copy-start.9 = (f32[8,8,2048]{2,1,0:T(8,128)S(1)}, f32[8,8,2048]{2,1,0:T(8,128)}, u32[]{:S(2)}) copy-start(f32[8,8,2048]{2,1,0:T(8,128)} %get-tuple-element.67) | copy-start | bytes 1572868
  290.4 33.4 %copy-start.13 = (bf16[3,112,640]{2,1,0:T(8,128)(2,1)S(1)}, bf16[3,112,640]{2,1,0:T(8,128)(2,1)}, u32[]{:S(2)}) copy-start(bf16[3,112,640]{2,1,0:T(8,128)(2,1)} %get-tuple-element.134) | copy-start | bytes 1290244
  290.4 129.1 %collective-permute-start.13 = (bf16[2048,896]{1,0:T(8,128)(2,1)}, bf16[2048,896]{1,0:T(8,128)(2,1)}, u32[]{:S(2)}, u32[]{:S(2)}) collective-permute-start(bf16[2048,896]{1,0:T(8,128)(2,1)} %collective-permute-done.12.x_ref), channel_id=1, source_target_pairs={{0,1},{1,0},{2,3},{3,2},{4,5},{5,4},{6,7},{7,6}} | collective-permute-start | bytes 11010056 | tf_op jit(solution)/shard_map/ppermute | solution.py:308
  323.9 13.2 %collective-permute-start.20 = (bf16[3,112,640]{2,1,0:T(8,128)(2,1)S(1)}, bf16[3,112,640]{2,1,0:T(8,128)(2,1)S(1)}, u32[]{:S(2)}, u32[]{:S(2)}) collective-permute-start(bf16[3,112,640]{2,1,0:T(8,128)(2,1)S(1)} %copy-done.13), channel_id=1, source_target_pairs={{0,6},{1,7},{2,4},{3,5},{4,2},{5,3},{6,0},{7,1}} | collective-permute-start | bytes 1290248 | tf_op jit(solution)/shard_map/ppermute | solution.py:315
  325.5 227.5 %collective-permute-start.23 = (bf16[3,2,448,640]{3,2,1,0:T(8,128)(2,1)}, bf16[3,2,448,640]{3,2,1,0:T(8,128)(2,1)}, u32[]{:S(2)}, u32[]{:S(2)}) collective-permute-start(bf16[3,2,448,640]{3,2,1,0:T(8,128)(2,1)} %pad_maximum_fusion.2), channel_id=1, source_target_pairs={{0,4},{4,0},{1,5},{5,1},{2,6},{6,2},{3,7},{7,3}} | collective-permute-start | bytes 10321928 | tf_op jit(solution)/shard_map/ppermute | solution.py:305
  337.1 173.4 %collective-permute-start.19 = (bf16[3,112,640]{2,1,0:T(8,128)(2,1)}, bf16[3,112,640]{2,1,0:T(8,128)(2,1)S(1)}, u32[]{:S(2)}, u32[]{:S(2)}) collective-permute-start(bf16[3,112,640]{2,1,0:T(8,128)(2,1)} %get-tuple-element.135), channel_id=1, source_target_pairs={{0,2},{1,3},{2,0},{3,1},{4,6},{5,7},{6,4},{7,5}} | collective-permute-start | bytes 1290248 | tf_op jit(solution)/shard_map/ppermute | solution.py:315
  345.8 164.7 %collective-permute-start.18 = (bf16[3,112,640]{2,1,0:T(8,128)(2,1)}, bf16[3,112,640]{2,1,0:T(8,128)(2,1)S(1)}, u32[]{:S(2)}, u32[]{:S(2)}) collective-permute-start(bf16[3,112,640]{2,1,0:T(8,128)(2,1)} %get-tuple-element.136), channel_id=1, source_target_pairs={{0,5},{1,4},{2,7},{3,6},{4,1},{5,0},{6,3},{7,2}} | collective-permute-start | bytes 1290248 | tf_op jit(solution)/shard_map/ppermute | solution.py:315
  419.6 93.0 %collective-permute-start.17 = (bf16[3,112,640]{2,1,0:T(8,128)(2,1)}, bf16[3,112,640]{2,1,0:T(8,128)(2,1)S(1)}, u32[]{:S(2)}, u32[]{:S(2)}) collective-permute-start(bf16[3,112,640]{2,1,0:T(8,128)(2,1)} %get-tuple-element.137), channel_id=1, source_target_pairs={{0,1},{1,0},{2,3},{3,2},{4,5},{5,4},{6,7},{7,6}} | collective-permute-start | bytes 1290248 | tf_op jit(solution)/shard_map/ppermute | solution.py:315
  419.6 93.0 %collective-permute-start.16 = (bf16[3,112,640]{2,1,0:T(8,128)(2,1)}, bf16[3,112,640]{2,1,0:T(8,128)(2,1)S(1)}, u32[]{:S(2)}, u32[]{:S(2)}) collective-permute-start(bf16[3,112,640]{2,1,0:T(8,128)(2,1)} %get-tuple-element.138), channel_id=1, source_target_pairs={{0,4},{1,5},{2,6},{3,7},{4,0},{5,1},{6,2},{7,3}} | collective-permute-start | bytes 1290248 | tf_op jit(solution)/shard_map/ppermute | solution.py:315
  481.2 31.4 %copy-start.10 = (bf16[3,112,640]{2,1,0:T(8,128)(2,1)S(1)}, bf16[3,112,640]{2,1,0:T(8,128)(2,1)}, u32[]{:S(2)}) copy-start(bf16[3,112,640]{2,1,0:T(8,128)(2,1)} %get-tuple-element.72) | copy-start | bytes 1290244
  510.5 101.5 %collective-permute-start.24 = (bf16[3,1,448,640]{3,2,1,0:T(8,128)(2,1)}, bf16[3,1,448,640]{3,2,1,0:T(8,128)(2,1)}, u32[]{:S(2)}, u32[]{:S(2)}) collective-permute-start(bf16[3,1,448,640]{3,2,1,0:T(8,128)(2,1)} %pad_maximum_fusion.3), channel_id=1, source_target_pairs={{0,4},{4,0},{1,5},{5,1},{2,6},{6,2},{3,7},{7,3}} | collective-permute-start | bytes 5160968 | tf_op jit(solution)/shard_map/ppermute | solution.py:305
  510.6 173.8 %collective-permute-start.25 = (bf16[3,1,448,640]{3,2,1,0:T(8,128)(2,1)}, bf16[3,1,448,640]{3,2,1,0:T(8,128)(2,1)}, u32[]{:S(2)}, u32[]{:S(2)}) collective-permute-start(bf16[3,1,448,640]{3,2,1,0:T(8,128)(2,1)} %pad_maximum_fusion.4), channel_id=1, source_target_pairs={{0,4},{4,0},{1,5},{5,1},{2,6},{6,2},{3,7},{7,3}} | collective-permute-start | bytes 5160968 | tf_op jit(solution)/shard_map/ppermute | solution.py:305
  520.0 3.3 copy-start.22
  700.9 13.1 %collective-permute-start.26 = (f32[2048,896]{1,0:T(8,128)}, f32[2048,896]{1,0:T(8,128)S(1)}, u32[]{:S(2)}, u32[]{:S(2)}) collective-permute-start(f32[2048,896]{1,0:T(8,128)} %combine.14), channel_id=1, source_target_pairs={{0,1},{1,0},{2,3},{3,2},{4,5},{5,4},{6,7},{7,6}} | collective-permute-start | bytes 22020104 | tf_op jit(solution)/shard_map/ppermute | solution.py:308
  714.0 2.9 copy-start.4
  729.7 9.6 copy-start.19
  739.0 19.7 %collective-permute-start.27 = (f32[2048,896]{1,0:T(8,128)}, f32[2048,896]{1,0:T(8,128)}, u32[]{:S(2)}, u32[]{:S(2)}) collective-permute-start(f32[2048,896]{1,0:T(8,128)} %combine.16), channel_id=1, source_target_pairs={{0,1},{1,0},{2,3},{3,2},{4,5},{5,4},{6,7},{7,6}} | collective-permute-start | bytes 22020104 | tf_op jit(solution)/shard_map/ppermute | solution.py:308
  739.9 16.7 %copy-start.18 = (s32[8,320]{1,0:T(8,128)S(1)}, s32[8,320]{1,0:T(8,128)}, u32[]{:S(2)}) copy-start(s32[8,320]{1,0:T(8,128)} %get-tuple-element.158) | copy-start | bytes 30724
  739.9 17.4 %copy-start.17 = (s32[8,320]{1,0:T(8,128)S(1)}, s32[8,320]{1,0:T(8,128)}, u32[]{:S(2)}) copy-start(s32[8,320]{1,0:T(8,128)} %get-tuple-element.163) | copy-start | bytes 30724
  739.9 18.1 %copy-start.16 = (s32[8,320]{1,0:T(8,128)S(1)}, s32[8,320]{1,0:T(8,128)}, u32[]{:S(2)}) copy-start(s32[8,320]{1,0:T(8,128)} %get-tuple-element.164) | copy-start | bytes 30724
  756.5 34.9 %collective-permute-start.28 = (f32[2048,896]{1,0:T(8,128)}, f32[2048,896]{1,0:T(8,128)}, u32[]{:S(2)}, u32[]{:S(2)}) collective-permute-start(f32[2048,896]{1,0:T(8,128)} %combine.17), channel_id=1, source_target_pairs={{0,1},{1,0},{2,3},{3,2},{4,5},{5,4},{6,7},{7,6}} | collective-permute-start | bytes 22020104 | tf_op jit(solution)/shard_map/ppermute | solution.py:308
  824.1 21.6 %copy-start.15 = (s32[8,320]{1,0:T(8,128)S(1)}, s32[8,320]{1,0:T(8,128)}, u32[]{:S(2)}) copy-start(s32[8,320]{1,0:T(8,128)} %get-tuple-element.165) | copy-start | bytes 30724
  840.5 19.5 %collective-permute-start.29 = (f32[2048,896]{1,0:T(8,128)}, f32[2048,896]{1,0:T(8,128)}, u32[]{:S(2)}, u32[]{:S(2)}) collective-permute-start(f32[2048,896]{1,0:T(8,128)} %combine.20), channel_id=1, source_target_pairs={{0,1},{1,0},{2,3},{3,2},{4,5},{5,4},{6,7},{7,6}} | collective-permute-start | bytes 22020104 | tf_op jit(solution)/shard_map/ppermute | solution.py:308
  841.7 82.5 %collective-permute-start.32 = (f32[1024,896]{1,0:T(8,128)}, f32[1024,896]{1,0:T(8,128)}, u32[]{:S(2)}, u32[]{:S(2)}) collective-permute-start(f32[1024,896]{1,0:T(8,128)} %get-tuple-element.105), channel_id=1, source_target_pairs={{0,4},{4,0},{1,5},{5,1},{2,6},{6,2},{3,7},{7,3}} | collective-permute-start | bytes 11010056 | tf_op jit(solution)/shard_map/ppermute | solution.py:305
  842.5 82.5 %collective-permute-start.33 = (f32[1024,896]{1,0:T(8,128)}, f32[1024,896]{1,0:T(8,128)}, u32[]{:S(2)}, u32[]{:S(2)}) collective-permute-start(f32[1024,896]{1,0:T(8,128)} %get-tuple-element.92), channel_id=1, source_target_pairs={{0,2},{1,3},{2,0},{3,1},{4,6},{5,7},{6,4},{7,5}} | collective-permute-start | bytes 11010056 | tf_op jit(solution)/shard_map/ppermute | solution.py:311
  842.9 159.9 %collective-permute-start.31 = (f32[1024,896]{1,0:T(8,128)}, f32[1024,896]{1,0:T(8,128)}, u32[]{:S(2)}, u32[]{:S(2)}) collective-permute-start(f32[1024,896]{1,0:T(8,128)} %get-tuple-element.103), channel_id=1, source_target_pairs={{0,4},{4,0},{1,5},{5,1},{2,6},{6,2},{3,7},{7,3}} | collective-permute-start | bytes 11010056 | tf_op jit(solution)/shard_map/ppermute | solution.py:305
  844.2 159.5 %collective-permute-start.30 = (f32[1024,896]{1,0:T(8,128)}, f32[1024,896]{1,0:T(8,128)}, u32[]{:S(2)}, u32[]{:S(2)}) collective-permute-start(f32[1024,896]{1,0:T(8,128)} %get-tuple-element.96), channel_id=1, source_target_pairs={{0,2},{1,3},{2,0},{3,1},{4,6},{5,7},{6,4},{7,5}} | collective-permute-start | bytes 11010056 | tf_op jit(solution)/shard_map/ppermute | solution.py:311
  860.0 65.1 %copy-start.7 = (f32[1024,896]{1,0:T(8,128)S(1)}, f32[1024,896]{1,0:T(8,128)}, u32[]{:S(2)}) copy-start(f32[1024,896]{1,0:T(8,128)} %get-tuple-element.110) | copy-start | bytes 11010052
  925.1 4.7 copy-start.8
  929.4 74.3 %copy-start.1 = (bf16[2048,896]{1,0:T(8,128)(2,1)S(1)}, bf16[2048,896]{1,0:T(8,128)(2,1)}, u32[]{:S(2)}) copy-start(bf16[2048,896]{1,0:T(8,128)(2,1)} %x_ref.1) | copy-start | bytes 11010052
  929.4 151.7 %collective-permute-start.35 = (f32[1024,896]{1,0:T(8,128)}, f32[1024,896]{1,0:T(8,128)}, u32[]{:S(2)}, u32[]{:S(2)}) collective-permute-start(f32[1024,896]{1,0:T(8,128)} %add.119), channel_id=1, source_target_pairs={{0,2},{1,3},{2,0},{3,1},{4,6},{5,7},{6,4},{7,5}} | collective-permute-start | bytes 11010056 | tf_op jit(solution)/shard_map/ppermute | solution.py:311
  934.2 146.9 %collective-permute-start.34 = (f32[1024,896]{1,0:T(8,128)}, f32[1024,896]{1,0:T(8,128)}, u32[]{:S(2)}, u32[]{:S(2)}) collective-permute-start(f32[1024,896]{1,0:T(8,128)} %add.118), channel_id=1, source_target_pairs={{0,4},{4,0},{1,5},{5,1},{2,6},{6,2},{3,7},{7,3}} | collective-permute-start | bytes 11010056 | tf_op jit(solution)/shard_map/ppermute | solution.py:305

commit v3 on v2

--- a/solution.py
+++ b/solution.py
@@ -124,25 +124,25 @@
     )(y_arr, xg, wg, wu, wdt, recv)
 
 
-def shared_kernel(x_ref, wg_ref, wu_ref, wd_ref, out_ref):
-    out_ref[...] = swiglu(x_ref[...], wg_ref[...], wu_ref[...], wd_ref[...])
-
-
-def shared_part(x_blk, wg, wu, wdt):
+def shared_kernel(x_ref, w_ref, out_ref):
+    out_ref[...] = swiglu(x_ref[...], w_ref[0], w_ref[1], w_ref[2])
+
+
+def shared_part(x_blk, w_all):
     tok_count, d_model = x_blk.shape
-    width = wdt.shape[1]
+    width = w_all.shape[2]
     tile = 512
     rows = pl.BlockSpec((tile, d_model), lambda i: (i, 0))
     return pl.pallas_call(
         shared_kernel,
         out_shape=jax.ShapeDtypeStruct((tok_count, d_model), F32),
         grid=(tok_count // tile,),
-        in_specs=[rows] + [pl.BlockSpec((d_model, width), lambda i: (0, 0))] * 3,
+        in_specs=[rows, pl.BlockSpec((3, d_model, width), lambda i: (0, 0, 0))],
         out_specs=rows,
         compiler_params=params(("arbitrary",)),
         cost_estimate=cost(6 * tok_count * d_model * width, 6 * tok_count * d_model),
         name="shared_part",
-    )(x_blk, wg, wu, wdt)
+    )(x_blk, w_all)
 
 
 def combine_kernel(n_base, where_of, halves, capacity, group, *refs):
@@ -266,6 +266,28 @@
     )(cnt, toks, gates, *bases, *outs)
 
 
+def assemble_kernel(me_ref, *refs):
+    out_ref = refs[-1]
+    for r, part in enumerate(refs[:-1]):
+        rows = part.shape[1]
+        at = pl.multiple_of((me_ref[0] ^ r) * rows, 16)
+        for k in range(part.shape[0]):
+            out_ref[k, pl.ds(at, rows), :] = part[k]
+
+
+def assemble(me_arr, parts):
+    n_arr, rows, width = parts[0].shape
+    vmem = pl.BlockSpec(memory_space=pltpu.VMEM)
+    return pl.pallas_call(
+        assemble_kernel,
+        out_shape=jax.ShapeDtypeStruct((n_arr, len(parts) * rows, width), BF16),
+        in_specs=[pl.BlockSpec(memory_space=pltpu.SMEM)] + [vmem] * len(parts),
+        out_specs=vmem,
+        compiler_params=pltpu.CompilerParams(vmem_limit_bytes=VMEM_LIMIT),
+        name="assemble",
+    )(me_arr, *parts)
+
+
 def finish_kernel(n_half, a_ref, b_ref, c_ref, d_ref, out_ref):
     @pl.when(pl.program_id(0) < n_half)
     def _():
@@ -315,7 +337,7 @@
         return lax.ppermute(v, ("data", "expert"), [(i, i ^ flip) for i in range(n_dev)])
 
     def device_fn(x_loc, idx_loc, gate_loc, wg_loc, wu_loc, wd_loc, wsg_loc, wsu_loc, wsd_loc):
-        tok_count, d_model = x_loc.shape
+        tok_count, _ = x_loc.shape
         top = idx_loc.shape[1]
         n_local, _, _ = wg_loc.shape
         n_mine = n_local // data_n
@@ -388,9 +410,9 @@
 
         def shared(r):
             if not shared_w:
-                whole = jnp.take(jnp.stack(after(*ws_parts)), by_rel, axis=0)
-                whole = whole.transpose(1, 0, 2, 3).reshape(3, d_model, width_s)
-                shared_w.extend([whole[0], whole[1], whole[2]])
+                whole = assemble(by_rel[:1], after(*ws_parts))
+                last[0] = whole
+                shared_w.append(whole)
             x_blk = after(blocks[r])
             base[r] = shared_part(x_blk, *shared_w)
             last[0] = base[r]
@@ -446,9 +468,6 @@
         pre5 = part(5, [base[5]], early, 0, False)
         early.append((experts(3), 0))
         shared(6)
-        pre6 = part(6, [base[6]], early, 0, False)
-        shared(4)
-        shared(3)
         tail = experts(4, (0, 2))
         late = [early[3], (tail, 0)]
         mate7 = over_core(part(7, [pre7], late, n_pre, False))
@@ -457,10 +476,12 @@
         diag = part(5, [pre5, mate7], late, n_pre, True)
         diag_x = over_x(diag[0])
         diag_y = over_y(diag[1])
-        mate6 = over_core(part(6, [pre6], [(rest, 2)], n_pre + CHUNKS[3], False))
-        mate3 = over_core(part(3, [base[3]], full, 0, False))
+        mate6 = over_core(part(6, [base[6]], full, 0, False))
+        shared(4)
+        shared(3)
         to_x = part(4, [base[4], mate6], full, 0, True)
         x_top = over_x(to_x[0])
+        mate3 = over_core(part(3, [base[3]], full, 0, False))
         shared(1)
         to_y = part(1, [base[1], mate3], full, 0, True)
         y_bot = over_y(to_y[1])

time: 1110 us -> 1190 us (1.072)
  waiting for transfers between devices: 419 us -> 521 us
  local copies, waits for them, and re-layouts: 50.6 us -> 33.7 us
    ppermute x14, waiting for transfers between devices: 105 us -> 341 us  [over_all(): lax.ppermute(v, ('data', 'expert'), [(i, i ^ flip) for i in range(n_dev)])]
    ppermute x9, waiting for transfers between devices: 245 us -> 44.7 us  [over_y(): return lax.ppermute(v, 'data', [(i, i ^ 1) for i in range(data_n)])]
    ppermute x5, waiting for transfers between devices: 69.8 us -> 136 us  [over_x(): return lax.ppermute(v, 'expert', [(i, i ^ 2) for i in range(exp_n)])]
    pallas_call x11 -> x10, Pallas kernels: 167 us -> 159 us  [combine(): pl.pallas_call(functools.partial(combine_kernel, n_base, tuple(where_of),...]
  transfers between devices with their start and end apart: 36 -> 36, of which waited for: 13 -> 10; matrix products, arithmetic and copies ran while one was open for 10% -> 8% of each run, Pallas kernels for 39% -> 33%
where the time goes in v3:
time: 1190 us; the launch traced here: 1170 us
  Pallas kernels  523 us (44%)
  waiting for transfers between devices  521 us (44%)
  other arithmetic  65.2 us (5%)
  local copies, waits for them, and re-layouts  33.7 us (3%)
  starting transfers between devices  28.3 us (2%)
    ppermute x14, waiting for transfers between devices, over_all(): lax.ppermute(v, ('data', 'expert'), [(i, i ^ flip) for i in range(n_dev)])  341 us
    pallas_call x10, Pallas kernels, combine(): pl.pallas_call(functools.partial(combine_kernel, n_base, tuple(where_of),...  159 us
    ppermute x5, waiting for transfers between devices, over_x(): return lax.ppermute(v, 'expert', [(i, i ^ 2) for i in range(exp_n)])  136 us
    pallas_call x6, Pallas kernels, expert_rows(): pl.pallas_call(functools.partial(expert_kernel, half), out_shape=jax.Shap...  124 us
    pallas_call x8, Pallas kernels, gather_rows(): pl.pallas_call(functools.partial(gather_kernel, per_step, capacity), out_...  118 us
    pallas_call x8, Pallas kernels, shared_part(): pl.pallas_call(shared_kernel, out_shape=jax.ShapeDtypeStruct((tok_count,...  109 us
    ppermute x9, waiting for transfers between devices, over_y(): return lax.ppermute(v, 'data', [(i, i ^ 1) for i in range(data_n)])  44.7 us
    reduce_sum x1, other arithmetic, make_lists(): jnp.sum(jnp.where(same, t_ids[None, None, :] - tok_count, 0), axis=2)  30.8 us
  transfers between devices with their start and end apart: 36, of which 10 were waited for; matrix products, arithmetic and copies ran while one was open for 8% of the time, Pallas kernels for 33%

profile of v3, /device:TPU:6, one launch (start us, length us, event | category | flops | bytes accessed | tf_op | source)
XLA Modules:
  0.0 1173.9 jit_solution(14036407285566540117)
XLA Ops:
  1.4 1.5 pad_maximum_fusion.5
  10.4 2.2 maximum_bitcast_fusion
  12.6 2.7 gather_fusion
  17.2 1.8 dynamic-slice_bitcast_fusion.10
  20.6 2.3 dynamic-slice_bitcast_fusion
  22.9 3.7 dynamic-slice_bitcast_fusion.1
  26.6 2.0 pad_maximum_fusion.2
  28.6 2.1 pad_maximum_fusion.1
  30.8 2.0 pad_maximum_fusion
  35.9 51.2 %collective-permute-done = f32[16,2048]{1,0:T(8,128)} collective-permute-done((f32[16,2048]{1,0:T(8,128)}, f32[16,2048]{1,0:T(8,128)}, u32[]{:S(2)}, u32[]{:S(2)}) %collective-permute-start) | collective-permute-done | bytes 131104 | tf_op jit(solution)/shard_map/ppermute | solution.py:337
  89.9 1.5 collective-permute-start.3
  92.4 80.4 %collective-permute-done.3 = f32[16,2048]{1,0:T(8,128)S(1)} collective-permute-done((f32[16,2048]{1,0:T(8,128)}, f32[16,2048]{1,0:T(8,128)S(1)}, u32[]{:S(2)}, u32[]{:S(2)}) %collective-permute-start.3) | collective-permute-done | bytes 131104 | tf_op jit(solution)/shard_map/ppermute | solution.py:337
  173.0 5.8 collective-permute-done.4
  178.9 5.1 collective-permute-done.5
  184.6 5.7 collective-permute-done.6
  191.3 1.6 compare_reduce_fusion
  193.8 2.5 collective-permute-start.20
  198.5 14.7 %gather_rows.8.refs_0_ = bf16[8,8,320,896]{3,2,1,0:T(8,128)(2,1)} custom-call(s32[16,2048]{1,0:T(8,128)} %get-tuple-element.153.pos_ref, bf16[2048,896]{1,0:T(8,128)(2,1)} %x_ref.1), custom_call_target="tpu_custom_call" | custom-call | flops 146800640 | bytes 4587520 | tf_op jit(solution)/shard_map/gather_rows/pallas_call | solution.py:61
  213.2 14.6 %gather_rows.9.refs_0_ = bf16[8,8,320,896]{3,2,1,0:T(8,128)(2,1)} custom-call(s32[16,2048]{1,0:T(8,128)} %get-tuple-element.152.pos_ref, bf16[2048,896]{1,0:T(8,128)(2,1)} %copy-done.2, bf16[8,8,320,896]{3,2,1,0:T(8,128)(2,1)} %gather_rows.8.refs_0_), custom_call_target="tpu_custom_call", output_to_operand_aliasing={{}: (2, {})} | custom-call | flops 146800640 | bytes 4587520 | tf_op jit(solution)/shard_map/gather_rows/pallas_call | solution.py:61
  227.8 14.9 %gather_rows.10.refs_0_ = bf16[8,8,320,896]{3,2,1,0:T(8,128)(2,1)} custom-call(s32[16,2048]{1,0:T(8,128)} %get-tuple-element.151.pos_ref, bf16[2048,896]{1,0:T(8,128)(2,1)} %collective-permute-done.8.x_ref, bf16[8,8,320,896]{3,2,1,0:T(8,128)(2,1)} %gather_rows.9.refs_0_), custom_call_target="tpu_custom_call", output_to_operand_aliasing={{}: (2, {})} | custom-call | flops 146800640 | bytes 4587520 | tf_op jit(solution)/shard_map/gather_rows/pallas_call | solution.py:61
  242.7 14.6 %gather_rows.11.refs_0_ = bf16[8,8,320,896]{3,2,1,0:T(8,128)(2,1)} custom-call(s32[16,2048]{1,0:T(8,128)} %get-tuple-element.150.pos_ref, bf16[2048,896]{1,0:T(8,128)(2,1)} %collective-permute-done.9.x_ref, bf16[8,8,320,896]{3,2,1,0:T(8,128)(2,1)} %gather_rows.10.refs_0_), custom_call_target="tpu_custom_call", output_to_operand_aliasing={{}: (2, {})} | custom-call | flops 146800640 | bytes 4587520 | tf_op jit(solution)/shard_map/gather_rows/pallas_call | solution.py:61
  257.3 14.6 %gather_rows.12.refs_0_ = bf16[8,8,320,896]{3,2,1,0:T(8,128)(2,1)} custom-call(s32[16,2048]{1,0:T(8,128)} %get-tuple-element.149.pos_ref, bf16[2048,896]{1,0:T(8,128)(2,1)} %collective-permute-done.10.x_ref, bf16[8,8,320,896]{3,2,1,0:T(8,128)(2,1)} %gather_rows.11.refs_0_), custom_call_target="tpu_custom_call", output_to_operand_aliasing={{}: (2, {})} | custom-call | flops 146800640 | bytes 4587520 | tf_op jit(solution)/shard_map/gather_rows/pallas_call | solution.py:61
  272.2 14.6 %gather_rows.13.refs_0_ = bf16[8,8,320,896]{3,2,1,0:T(8,128)(2,1)} custom-call(s32[16,2048]{1,0:T(8,128)} %get-tuple-element.155.pos_ref, bf16[2048,896]{1,0:T(8,128)(2,1)} %collective-permute-done.11.x_ref, bf16[8,8,320,896]{3,2,1,0:T(8,128)(2,1)} %gather_rows.12.refs_0_), custom_call_target="tpu_custom_call", output_to_operand_aliasing={{}: (2, {})} | custom-call | flops 146800640 | bytes 4587520 | tf_op jit(solution)/shard_map/gather_rows/pallas_call | solution.py:61
  289.6 30.8 %select_reduce_fusion = s32[64,320]{1,0:T(8,128)S(1)} fusion(s32[2048]{0:T(1024)S(1)} %iota_add_fusion, s32[64,2048]{1,0:T(8,128)S(1)} %fusion.3), kind=kLoop, calls=%fused_computation.1 | loop fusion | flops 125808640 | bytes 614400 | tf_op jit(solution)/shard_map/reduce_sum | solution.py:437
  321.8 1.5 collective-permute-start.18
  325.3 192.9 %collective-permute-done.18.refs_3_ = bf16[3,112,640]{2,1,0:T(8,128)(2,1)S(1)} collective-permute-done((bf16[3,112,640]{2,1,0:T(8,128)(2,1)}, bf16[3,112,640]{2,1,0:T(8,128)(2,1)S(1)}, u32[]{:S(2)}, u32[]{:S(2)}) %collective-permute-start.18) | collective-permute-done | bytes 430112 | tf_op jit(solution)/shard_map/ppermute | solution.py:337
  522.7 14.6 %gather_rows.14.refs_0_ = bf16[8,8,320,896]{3,2,1,0:T(8,128)(2,1)} custom-call(s32[16,2048]{1,0:T(8,128)} %get-tuple-element.148.pos_ref, bf16[2048,896]{1,0:T(8,128)(2,1)} %collective-permute-done.12.x_ref, bf16[8,8,320,896]{3,2,1,0:T(8,128)(2,1)} %gather_rows.13.refs_0_), custom_call_target="tpu_custom_call", output_to_operand_aliasing={{}: (2, {})} | custom-call | flops 146800640 | bytes 4587520 | tf_op jit(solution)/shard_map/gather_rows/pallas_call | solution.py:61
  538.2 15.0 %gather_rows.15.xg_ref = bf16[8,8,320,896]{3,2,1,0:T(8,128)(2,1)} custom-call(s32[16,2048]{1,0:T(8,128)} %get-tuple-element.154.pos_ref, bf16[2048,896]{1,0:T(8,128)(2,1)} %collective-permute-done.13.x_ref, bf16[8,8,320,896]{3,2,1,0:T(8,128)(2,1)} %gather_rows.14.refs_0_), custom_call_target="tpu_custom_call", output_to_operand_aliasing={{}: (2, {})} | custom-call | flops 146800640 | bytes 4587520 | tf_op jit(solution)/shard_map/gather_rows/pallas_call | solution.py:61
  553.2 29.2 %expert_rows.6.refs_4_.refs_5_ = bf16[2,8,320,896]{3,2,1,0:T(8,128)(2,1)} custom-call(s32[1]{0:T(128)} %bitcast.32.y_ref, bf16[8,8,320,896]{3,2,1,0:T(8,128)(2,1)} %gather_rows.15.xg_ref, bf16[16,448,640]{2,1,0:T(8,128)(2,1)} %og_ref.11, bf16[16,448,640]{2,1,0:T(8,128)(2,1)} %ou_ref.11, bf16[16,448,640]{2,1,0:T(8,128)(2,1)} %bitcast.149, ...), custom_call_target="tpu_custom_call" | custom-call | flops 275251200 | bytes 18350080 | tf_op jit(solution)/shard_map/expert_rows/pallas_call | solution.py:107
  582.5 29.3 %expert_rows.7.refs_5_.refs_6_ = bf16[2,8,320,896]{3,2,1,0:T(8,128)(2,1)} custom-call(s32[1]{0:T(128)} %bitcast.32.y_ref, bf16[8,8,320,896]{3,2,1,0:T(8,128)(2,1)} %gather_rows.15.xg_ref, bf16[16,448,640]{2,1,0:T(8,128)(2,1)} %og_ref.11, bf16[16,448,640]{2,1,0:T(8,128)(2,1)} %ou_ref.11, bf16[16,448,640]{2,1,0:T(8,128)(2,1)} %bitcast.150, ...), custom_call_target="tpu_custom_call" | custom-call | flops 275251200 | bytes 18350080 | tf_op jit(solution)/shard_map/expert_rows/pallas_call | solution.py:107
  612.7 4.5 assemble.1.w_ref
  617.2 13.6 %shared_part.8.refs_3_ = f32[2048,896]{1,0:T(8,128)} custom-call(bf16[2048,896]{1,0:T(8,128)(2,1)} %collective-permute-done.13.x_ref, bf16[3,896,640]{2,1,0:T(8,128)(2,1)} %assemble.1.w_ref), custom_call_target="tpu_custom_call" | custom-call | flops 110100480 | bytes 11010048 | tf_op jit(solution)/shard_map/shared_part/pallas_call | solution.py:136
  630.8 13.6 %shared_part.9.refs_3_ = f32[2048,896]{1,0:T(8,128)} custom-call(bf16[2048,896]{1,0:T(8,128)(2,1)} %collective-permute-done.12.x_ref, bf16[3,896,640]{2,1,0:T(8,128)(2,1)} %assemble.1.w_ref), custom_call_target="tpu_custom_call" | custom-call | flops 110100480 | bytes 11010048 | tf_op jit(solution)/shard_map/shared_part/pallas_call | solution.py:136
  644.4 29.5 %expert_rows.8.refs_6_.refs_7_ = bf16[2,8,320,896]{3,2,1,0:T(8,128)(2,1)} custom-call(s32[1]{0:T(128)} %bitcast.32.y_ref, bf16[8,8,320,896]{3,2,1,0:T(8,128)(2,1)} %gather_rows.15.xg_ref, bf16[16,448,640]{2,1,0:T(8,128)(2,1)} %og_ref.11, bf16[16,448,640]{2,1,0:T(8,128)(2,1)} %ou_ref.11, bf16[16,448,640]{2,1,0:T(8,128)(2,1)} %bitcast.151, ...), custom_call_target="tpu_custom_call" | custom-call | flops 275251200 | bytes 18350080 | tf_op jit(solution)/shard_map/expert_rows/pallas_call | solution.py:107
  673.9 14.8 %combine.10.refs_3_ = f32[2048,896]{1,0:T(8,128)} custom-call(s32[1,8]{1,0:T(1,128)} %get-tuple-element.165.refs_0_, s32[1,2560]{1,0:T(1,128)} %squeeze.156.refs_1_, f32[1,16512]{1,0:T(1,128)} %get-tuple-element.146.refs_2_, f32[2048,896]{1,0:T(8,128)} %shared_part.8.refs_3_, bf16[2,8,320,896]{3,2,1,0:T(8,128)(2,1)} %expert_rows.6.refs_4_.refs_5_, ...), custom_call_target="tpu_custom_call" | custom-call | flops 55050240 | bytes 14680064 | tf_op jit(solution)/shard_map/combine/pallas_call | solution.py:249
  688.7 14.7 %combine.11.refs_3_ = f32[2048,896]{1,0:T(8,128)} custom-call(s32[1,8]{1,0:T(1,128)} %get-tuple-element.166.refs_0_, s32[1,2560]{1,0:T(1,128)} %squeeze.151.refs_1_, f32[1,16512]{1,0:T(1,128)} %get-tuple-element.145.refs_2_, f32[2048,896]{1,0:T(8,128)} %shared_part.9.refs_3_, bf16[2,8,320,896]{3,2,1,0:T(8,128)(2,1)} %expert_rows.6.refs_4_.refs_5_, ...), custom_call_target="tpu_custom_call" | custom-call | flops 55050240 | bytes 14680064 | tf_op jit(solution)/shard_map/combine/pallas_call | solution.py:249
  704.7 16.0 %expert_rows.9.refs_4_.refs_5_.refs_7_.refs_8_ = bf16[1,8,320,896]{3,2,1,0:T(8,128)(2,1)} custom-call(s32[1]{0:T(128)} %bitcast.32.y_ref, bf16[8,8,320,896]{3,2,1,0:T(8,128)(2,1)} %gather_rows.15.xg_ref, bf16[16,448,640]{2,1,0:T(8,128)(2,1)} %og_ref.11, bf16[16,448,640]{2,1,0:T(8,128)(2,1)} %ou_ref.11, bf16[16,448,640]{2,1,0:T(8,128)(2,1)} %bitcast.152, ...), custom_call_target="tpu_custom_call" | custom-call | flops 137625600 | bytes 9175040 | tf_op jit(solution)/shard_map/expert_rows/pallas_call | solution.py:107
  720.7 13.6 %shared_part.10.refs_3_ = f32[2048,896]{1,0:T(8,128)} custom-call(bf16[2048,896]{1,0:T(8,128)(2,1)} %collective-permute-done.11.x_ref, bf16[3,896,640]{2,1,0:T(8,128)(2,1)} %assemble.1.w_ref), custom_call_target="tpu_custom_call" | custom-call | flops 110100480 | bytes 11010048 | tf_op jit(solution)/shard_map/shared_part/pallas_call | solution.py:136
  734.3 6.6 expert_rows.10.refs_5_.refs_6_
  740.9 10.2 combine.12
  751.8 12.9 %expert_rows.11.refs_8_.refs_9_ = bf16[1,6,320,896]{3,2,1,0:T(8,128)(2,1)} custom-call(s32[1]{0:T(128)} %bitcast.32.y_ref, bf16[8,8,320,896]{3,2,1,0:T(8,128)(2,1)} %gather_rows.15.xg_ref, bf16[16,448,640]{2,1,0:T(8,128)(2,1)} %og_ref.11, bf16[16,448,640]{2,1,0:T(8,128)(2,1)} %ou_ref.11, bf16[16,448,640]{2,1,0:T(8,128)(2,1)} %bitcast.154, ...), custom_call_target="tpu_custom_call" | custom-call | flops 103219200 | bytes 6881280 | tf_op jit(solution)/shard_map/expert_rows/pallas_call | solution.py:107
  764.7 12.8 %combine.13 = (f32[1024,896]{1,0:T(8,128)}, f32[1024,896]{1,0:T(8,128)}) custom-call(s32[1,8]{1,0:T(1,128)} %get-tuple-element.166.refs_0_, s32[1,2560]{1,0:T(1,128)} %squeeze.151.refs_1_, f32[1,16512]{1,0:T(1,128)} %get-tuple-element.145.refs_2_, f32[2048,896]{1,0:T(8,128)} %combine.11.refs_3_, f32[2048,896]{1,0:T(8,128)} %collective-permute-done.26.refs_4_, ...), custom_call_target="tpu_custom_call" | custom-call | flops 18350080 | bytes 14680064 | tf_op jit(solution)/shard_map/combine/pallas_call | solution.py:249
  777.5 16.7 %combine.14 = f32[2048,896]{1,0:T(8,128)} custom-call(s32[1,8]{1,0:T(1,128)} %get-tuple-element.167.refs_0_, s32[1,2560]{1,0:T(1,128)} %squeeze.148.refs_1_, f32[1,16512]{1,0:T(1,128)} %get-tuple-element.144.refs_2_, f32[2048,896]{1,0:T(8,128)} %shared_part.10.refs_3_, bf16[2,8,320,896]{3,2,1,0:T(8,128)(2,1)} %expert_rows.6.refs_4_.refs_5_, ...), custom_call_target="tpu_custom_call" | custom-call | flops 73400320 | bytes 14680064 | tf_op jit(solution)/shard_map/combine/pallas_call | solution.py:249
  795.9 13.6 %shared_part.11.refs_3_ = f32[2048,896]{1,0:T(8,128)} custom-call(bf16[2048,896]{1,0:T(8,128)(2,1)} %collective-permute-done.9.x_ref, bf16[3,896,640]{2,1,0:T(8,128)(2,1)} %assemble.1.w_ref), custom_call_target="tpu_custom_call" | custom-call | flops 110100480 | bytes 11010048 | tf_op jit(solution)/shard_map/shared_part/pallas_call | solution.py:136
  809.5 13.6 %shared_part.12.refs_3_ = f32[2048,896]{1,0:T(8,128)} custom-call(bf16[2048,896]{1,0:T(8,128)(2,1)} %collective-permute-done.10.x_ref, bf16[3,896,640]{2,1,0:T(8,128)(2,1)} %assemble.1.w_ref), custom_call_target="tpu_custom_call" | custom-call | flops 110100480 | bytes 11010048 | tf_op jit(solution)/shard_map/shared_part/pallas_call | solution.py:136
  823.1 19.1 %combine.15 = (f32[1024,896]{1,0:T(8,128)}, f32[1024,896]{1,0:T(8,128)}) custom-call(s32[1,8]{1,0:T(1,128)} %get-tuple-element.168.refs_0_, s32[1,2560]{1,0:T(1,128)} %squeeze.145.refs_1_, f32[1,16512]{1,0:T(1,128)} %get-tuple-element.143.refs_2_, f32[2048,896]{1,0:T(8,128)} %shared_part.11.refs_3_, f32[2048,896]{1,0:T(8,128)} %collective-permute-done.27.refs_4_, ...), custom_call_target="tpu_custom_call" | custom-call | flops 73400320 | bytes 14680064 | tf_op jit(solution)/shard_map/combine/pallas_call | solution.py:249
  842.2 16.7 %combine.16 = f32[2048,896]{1,0:T(8,128)} custom-call(s32[1,8]{1,0:T(1,128)} %get-tuple-element.164.refs_0_, s32[1,2560]{1,0:T(1,128)} %squeeze.142.refs_1_, f32[1,16512]{1,0:T(1,128)} %get-tuple-element.140.refs_2_, f32[2048,896]{1,0:T(8,128)} %shared_part.12.refs_3_, bf16[2,8,320,896]{3,2,1,0:T(8,128)(2,1)} %expert_rows.6.refs_4_.refs_5_, ...), custom_call_target="tpu_custom_call" | custom-call | flops 73400320 | bytes 14680064 | tf_op jit(solution)/shard_map/combine/pallas_call | solution.py:249
  860.4 13.6 %shared_part.13.refs_3_ = f32[2048,896]{1,0:T(8,128)} custom-call(bf16[2048,896]{1,0:T(8,128)(2,1)} %collective-permute-done.8.x_ref, bf16[3,896,640]{2,1,0:T(8,128)(2,1)} %assemble.1.w_ref), custom_call_target="tpu_custom_call" | custom-call | flops 110100480 | bytes 11010048 | tf_op jit(solution)/shard_map/shared_part/pallas_call | solution.py:136
  874.0 19.1 %combine.17 = (f32[1024,896]{1,0:T(8,128)}, f32[1024,896]{1,0:T(8,128)}) custom-call(s32[1,8]{1,0:T(1,128)} %get-tuple-element.169.refs_0_, s32[1,2560]{1,0:T(1,128)} %squeeze.139.refs_1_, f32[1,16512]{1,0:T(1,128)} %get-tuple-element.142.refs_2_, f32[2048,896]{1,0:T(8,128)} %shared_part.13.refs_3_, f32[2048,896]{1,0:T(8,128)} %collective-permute-done.28.refs_4_, ...), custom_call_target="tpu_custom_call" | custom-call | flops 73400320 | bytes 14680064 | tf_op jit(solution)/shard_map/combine/pallas_call | solution.py:249
  893.1 13.6 %shared_part.14.refs_3_ = f32[2048,896]{1,0:T(8,128)} custom-call(bf16[2048,896]{1,0:T(8,128)(2,1)} %copy-done.2, bf16[3,896,640]{2,1,0:T(8,128)(2,1)} %assemble.1.w_ref), custom_call_target="tpu_custom_call" | custom-call | flops 110100480 | bytes 11010048 | tf_op jit(solution)/shard_map/shared_part/pallas_call | solution.py:136
  906.7 16.3 %combine.18 = f32[2048,896]{1,0:T(8,128)} custom-call(s32[1,8]{1,0:T(1,128)} %get-tuple-element.170.refs_0_, s32[1,2560]{1,0:T(1,128)} %squeeze.136.refs_1_, f32[1,16512]{1,0:T(1,128)} %get-tuple-element.141.refs_2_, f32[2048,896]{1,0:T(8,128)} %shared_part.14.refs_3_, bf16[2,8,320,896]{3,2,1,0:T(8,128)(2,1)} %expert_rows.6.refs_4_.refs_5_, ...), custom_call_target="tpu_custom_call" | custom-call | flops 73400320 | bytes 14680064 | tf_op jit(solution)/shard_map/combine/pallas_call | solution.py:249
  925.2 2.0 collective-permute-start.33
  927.3 1.6 collective-permute-start.31
  929.6 13.6 %shared_part.15.refs_3_ = f32[2048,896]{1,0:T(8,128)} custom-call(bf16[2048,896]{1,0:T(8,128)(2,1)} %x_ref.1, bf16[3,896,640]{2,1,0:T(8,128)(2,1)} %assemble.1.w_ref), custom_call_target="tpu_custom_call" | custom-call | flops 110100480 | bytes 11010048 | tf_op jit(solution)/shard_map/shared_part/pallas_call | solution.py:136
  943.1 18.9 %combine.19 = (f32[1024,896]{1,0:T(8,128)}, f32[1024,896]{1,0:T(8,128)}) custom-call(s32[1,8]{1,0:T(1,128)} %get-tuple-element.171.refs_0_, s32[1,2560]{1,0:T(1,128)} %squeeze.133.refs_1_, f32[1,16512]{1,0:T(1,128)} %get-tuple-element.147.refs_2_, f32[2048,896]{1,0:T(8,128)} %shared_part.15.refs_3_, f32[2048,896]{1,0:T(8,128)} %collective-permute-done.29.refs_4_, ...), custom_call_target="tpu_custom_call" | custom-call | flops 73400320 | bytes 14680064 | tf_op jit(solution)/shard_map/combine/pallas_call | solution.py:249
  962.1 44.7 %collective-permute-done.32 = f32[1024,896]{1,0:T(8,128)} collective-permute-done((f32[1024,896]{1,0:T(8,128)}, f32[1024,896]{1,0:T(8,128)}, u32[]{:S(2)}, u32[]{:S(2)}) %collective-permute-start.32) | collective-permute-done | bytes 3670048 | tf_op jit(solution)/shard_map/ppermute | solution.py:327
  1007.8 4.4 add.133
  1012.2 2.0 collective-permute-start.35
  1014.2 4.2 add.132
  1018.4 1.6 collective-permute-start.34
  1020.0 66.4 %collective-permute-done.30 = f32[1024,896]{1,0:T(8,128)} collective-permute-done((f32[1024,896]{1,0:T(8,128)}, f32[1024,896]{1,0:T(8,128)}, u32[]{:S(2)}, u32[]{:S(2)}) %collective-permute-start.30) | collective-permute-done | bytes 3670048 | tf_op jit(solution)/shard_map/ppermute | solution.py:333
  1086.4 9.4 add_add_fusion
  1095.8 68.3 %collective-permute-done.35.d_ref = f32[1024,896]{1,0:T(8,128)} collective-permute-done((f32[1024,896]{1,0:T(8,128)}, f32[1024,896]{1,0:T(8,128)}, u32[]{:S(2)}, u32[]{:S(2)}) %collective-permute-start.35) | collective-permute-done | bytes 3670048 | tf_op jit(solution)/shard_map/ppermute | solution.py:333
  1164.1 9.4 finish.1
  (144 shorter events, 45.9 us)
Async XLA Ops:
  0.0 7.7 copy-start.7
  0.0 87.0 %collective-permute-start.8 = (bf16[2048,896]{1,0:T(8,128)(2,1)}, bf16[2048,896]{1,0:T(8,128)(2,1)}, u32[]{:S(2)}, u32[]{:S(2)}) collective-permute-start(bf16[2048,896]{1,0:T(8,128)(2,1)} %x_ref.1), channel_id=1, source_target_pairs={{0,4},{4,0},{1,5},{5,1},{2,6},{6,2},{3,7},{7,3}} | collective-permute-start | bytes 11010056 | tf_op jit(solution)/shard_map/ppermute | solution.py:327
  2.8 87.1 %collective-permute-start.2 = (f32[16,2048]{1,0:T(8,128)}, f32[16,2048]{1,0:T(8,128)}, u32[]{:S(2)}, u32[]{:S(2)}) collective-permute-start(f32[16,2048]{1,0:T(8,128)} %pad_maximum_fusion.5), channel_id=1, source_target_pairs={{0,5},{1,4},{2,7},{3,6},{4,1},{5,0},{6,3},{7,2}} | collective-permute-start | bytes 393224 | tf_op jit(solution)/shard_map/ppermute | solution.py:337
  3.5 84.9 %collective-permute-start.1 = (f32[16,2048]{1,0:T(8,128)}, f32[16,2048]{1,0:T(8,128)}, u32[]{:S(2)}, u32[]{:S(2)}) collective-permute-start(f32[16,2048]{1,0:T(8,128)} %pad_maximum_fusion.5), channel_id=1, source_target_pairs={{0,1},{1,0},{2,3},{3,2},{4,5},{5,4},{6,7},{7,6}} | collective-permute-start | bytes 393224 | tf_op jit(solution)/shard_map/ppermute | solution.py:337
  4.5 82.5 %collective-permute-start = (f32[16,2048]{1,0:T(8,128)}, f32[16,2048]{1,0:T(8,128)}, u32[]{:S(2)}, u32[]{:S(2)}) collective-permute-start(f32[16,2048]{1,0:T(8,128)} %pad_maximum_fusion.5), channel_id=1, source_target_pairs={{0,4},{1,5},{2,6},{3,7},{4,0},{5,1},{6,2},{7,3}} | collective-permute-start | bytes 393224 | tf_op jit(solution)/shard_map/ppermute | solution.py:337
  5.0 84.0 %collective-permute-start.9 = (bf16[2048,896]{1,0:T(8,128)(2,1)}, bf16[2048,896]{1,0:T(8,128)(2,1)}, u32[]{:S(2)}, u32[]{:S(2)}) collective-permute-start(bf16[2048,896]{1,0:T(8,128)(2,1)} %x_ref.1), channel_id=1, source_target_pairs={{0,2},{1,3},{2,0},{3,1},{4,6},{5,7},{6,4},{7,5}} | collective-permute-start | bytes 11010056 | tf_op jit(solution)/shard_map/ppermute | solution.py:333
  6.5 2.5 copy-start.8
  30.7 2.0 copy-start.15
  30.8 3.3 copy-start.3
  34.4 52.6 %copy-start = (bf16[2048,896]{1,0:T(8,128)(2,1)S(1)}, bf16[2048,896]{1,0:T(8,128)(2,1)}, u32[]{:S(2)}) copy-start(bf16[2048,896]{1,0:T(8,128)(2,1)} %x_ref.1) | copy-start | bytes 11010052
  87.0 105.9 %collective-permute-start.7 = (bf16[2048,896]{1,0:T(8,128)(2,1)S(1)}, bf16[2048,896]{1,0:T(8,128)(2,1)S(1)}, u32[]{:S(2)}, u32[]{:S(2)}) collective-permute-start(bf16[2048,896]{1,0:T(8,128)(2,1)S(1)} %copy-done), channel_id=1, source_target_pairs={{0,1},{1,0},{2,3},{3,2},{4,5},{5,4},{6,7},{7,6}} | collective-permute-start | bytes 11010056 | tf_op jit(solution)/shard_map/ppermute | solution.py:330
  87.0 106.8 %collective-permute-start.10 = (bf16[2048,896]{1,0:T(8,128)(2,1)}, bf16[2048,896]{1,0:T(8,128)(2,1)}, u32[]{:S(2)}, u32[]{:S(2)}) collective-permute-start(bf16[2048,896]{1,0:T(8,128)(2,1)} %collective-permute-done.8.x_ref), channel_id=1, source_target_pairs={{0,1},{1,0},{2,3},{3,2},{4,5},{5,4},{6,7},{7,6}} | collective-permute-start | bytes 11010056 | tf_op jit(solution)/shard_map/ppermute | solution.py:330
  88.5 201.1 %collective-permute-start.12 = (bf16[2048,896]{1,0:T(8,128)(2,1)}, bf16[2048,896]{1,0:T(8,128)(2,1)}, u32[]{:S(2)}, u32[]{:S(2)}) collective-permute-start(bf16[2048,896]{1,0:T(8,128)(2,1)} %collective-permute-done.8.x_ref), channel_id=1, source_target_pairs={{0,2},{1,3},{2,0},{3,1},{4,6},{5,7},{6,4},{7,5}} | collective-permute-start | bytes 11010056 | tf_op jit(solution)/shard_map/ppermute | solution.py:333
  89.0 182.9 %collective-permute-start.11 = (bf16[2048,896]{1,0:T(8,128)(2,1)}, bf16[2048,896]{1,0:T(8,128)(2,1)}, u32[]{:S(2)}, u32[]{:S(2)}) collective-permute-start(bf16[2048,896]{1,0:T(8,128)(2,1)} %collective-permute-done.9.x_ref), channel_id=1, source_target_pairs={{0,1},{1,0},{2,3},{3,2},{4,5},{5,4},{6,7},{7,6}} | collective-permute-start | bytes 11010056 | tf_op jit(solution)/shard_map/ppermute | solution.py:330
  89.9 82.8 %collective-permute-start.3 = (f32[16,2048]{1,0:T(8,128)}, f32[16,2048]{1,0:T(8,128)S(1)}, u32[]{:S(2)}, u32[]{:S(2)}) collective-permute-start(f32[16,2048]{1,0:T(8,128)} %pad_maximum_fusion.5), channel_id=1, source_target_pairs={{0,2},{1,3},{2,0},{3,1},{4,6},{5,7},{6,4},{7,5}} | collective-permute-start | bytes 393224 | tf_op jit(solution)/shard_map/ppermute | solution.py:337
  172.8 6.1 collective-permute-start.4
  178.8 5.1 collective-permute-start.5
  183.9 6.3 collective-permute-start.6
  190.2 96.6 %collective-permute-start.22 = (bf16[3,112,640]{2,1,0:T(8,128)(2,1)S(1)}, bf16[3,112,640]{2,1,0:T(8,128)(2,1)S(1)}, u32[]{:S(2)}, u32[]{:S(2)}) collective-permute-start(bf16[3,112,640]{2,1,0:T(8,128)(2,1)S(1)} %get-tuple-element.130), channel_id=1, source_target_pairs={{0,7},{1,6},{2,5},{3,4},{4,3},{5,2},{6,1},{7,0}} | collective-permute-start | bytes 1290248 | tf_op jit(solution)/shard_map/ppermute | solution.py:337
  192.9 5.6 copy-start.2
  192.9 94.6 %collective-permute-start.21 = (bf16[3,112,640]{2,1,0:T(8,128)(2,1)S(1)}, bf16[3,112,640]{2,1,0:T(8,128)(2,1)S(1)}, u32[]{:S(2)}, u32[]{:S(2)}) collective-permute-start(bf16[3,112,640]{2,1,0:T(8,128)(2,1)S(1)} %get-tuple-element.131), channel_id=1, source_target_pairs={{0,3},{1,2},{2,1},{3,0},{4,7},{5,6},{6,5},{7,4}} | collective-permute-start | bytes 1290248 | tf_op jit(solution)/shard_map/ppermute | solution.py:337
  193.8 95.1 %collective-permute-start.20 = (bf16[3,112,640]{2,1,0:T(8,128)(2,1)S(1)}, bf16[3,112,640]{2,1,0:T(8,128)(2,1)S(1)}, u32[]{:S(2)}, u32[]{:S(2)}) collective-permute-start(bf16[3,112,640]{2,1,0:T(8,128)(2,1)S(1)} %get-tuple-element.132), channel_id=1, source_target_pairs={{0,6},{1,7},{2,4},{3,5},{4,2},{5,3},{6,0},{7,1}} | collective-permute-start | bytes 1290248 | tf_op jit(solution)/shard_map/ppermute | solution.py:337
  271.9 49.9 %collective-permute-start.19 = (bf16[3,112,640]{2,1,0:T(8,128)(2,1)}, bf16[3,112,640]{2,1,0:T(8,128)(2,1)}, u32[]{:S(2)}, u32[]{:S(2)}) collective-permute-start(bf16[3,112,640]{2,1,0:T(8,128)(2,1)} %get-tuple-element.133), channel_id=1, source_target_pairs={{0,2},{1,3},{2,0},{3,1},{4,6},{5,7},{6,4},{7,5}} | collective-permute-start | bytes 1290248 | tf_op jit(solution)/shard_map/ppermute | solution.py:337
  286.9 2.7 copy-start.9
  286.9 232.4 %collective-permute-start.14 = (bf16[3,2,448,640]{3,2,1,0:T(8,128)(2,1)}, bf16[3,2,448,640]{3,2,1,0:T(8,128)(2,1)}, u32[]{:S(2)}, u32[]{:S(2)}) collective-permute-start(bf16[3,2,448,640]{3,2,1,0:T(8,128)(2,1)} %pad_maximum_fusion), channel_id=1, source_target_pairs={{0,4},{4,0},{1,5},{5,1},{2,6},{6,2},{3,7},{7,3}} | collective-permute-start | bytes 10321928 | tf_op jit(solution)/shard_map/ppermute | solution.py:327
  287.5 32.8 %copy-start.10 = (bf16[3,112,640]{2,1,0:T(8,128)(2,1)}, bf16[3,112,640]{2,1,0:T(8,128)(2,1)S(1)}, u32[]{:S(2)}) copy-start(bf16[3,112,640]{2,1,0:T(8,128)(2,1)S(1)} %collective-permute-done.21.refs_6_) | copy-start | bytes 1290244
  287.5 233.9 %collective-permute-start.15 = (bf16[3,2,448,640]{3,2,1,0:T(8,128)(2,1)}, bf16[3,2,448,640]{3,2,1,0:T(8,128)(2,1)}, u32[]{:S(2)}, u32[]{:S(2)}) collective-permute-start(bf16[3,2,448,640]{3,2,1,0:T(8,128)(2,1)} %pad_maximum_fusion.1), channel_id=1, source_target_pairs={{0,4},{4,0},{1,5},{5,1},{2,6},{6,2},{3,7},{7,3}} | collective-permute-start | bytes 10321928 | tf_op jit(solution)/shard_map/ppermute | solution.py:327
  288.9 31.5 %copy-start.11 = (bf16[3,112,640]{2,1,0:T(8,128)(2,1)}, bf16[3,112,640]{2,1,0:T(8,128)(2,1)S(1)}, u32[]{:S(2)}) copy-start(bf16[3,112,640]{2,1,0:T(8,128)(2,1)S(1)} %collective-permute-done.20.refs_5_) | copy-start | bytes 1290244
  288.9 355.5 %collective-permute-start.23 = (bf16[3,2,448,640]{3,2,1,0:T(8,128)(2,1)}, bf16[3,2,448,640]{3,2,1,0:T(8,128)(2,1)}, u32[]{:S(2)}, u32[]{:S(2)}) collective-permute-start(bf16[3,2,448,640]{3,2,1,0:T(8,128)(2,1)} %pad_maximum_fusion.2), channel_id=1, source_target_pairs={{0,4},{4,0},{1,5},{5,1},{2,6},{6,2},{3,7},{7,3}} | collective-permute-start | bytes 10321928 | tf_op jit(solution)/shard_map/ppermute | solution.py:327
  289.5 232.5 %collective-permute-start.13 = (bf16[2048,896]{1,0:T(8,128)(2,1)}, bf16[2048,896]{1,0:T(8,128)(2,1)}, u32[]{:S(2)}, u32[]{:S(2)}) collective-permute-start(bf16[2048,896]{1,0:T(8,128)(2,1)} %collective-permute-done.12.x_ref), channel_id=1, source_target_pairs={{0,1},{1,0},{2,3},{3,2},{4,5},{5,4},{6,7},{7,6}} | collective-permute-start | bytes 11010056 | tf_op jit(solution)/shard_map/ppermute | solution.py:330
  321.8 196.4 %collective-permute-start.18 = (bf16[3,112,640]{2,1,0:T(8,128)(2,1)}, bf16[3,112,640]{2,1,0:T(8,128)(2,1)S(1)}, u32[]{:S(2)}, u32[]{:S(2)}) collective-permute-start(bf16[3,112,640]{2,1,0:T(8,128)(2,1)} %get-tuple-element.134), channel_id=1, source_target_pairs={{0,5},{1,4},{2,7},{3,6},{4,1},{5,0},{6,3},{7,2}} | collective-permute-start | bytes 1290248 | tf_op jit(solution)/shard_map/ppermute | solution.py:337
  518.2 19.1 %copy-start.12 = (bf16[3,112,640]{2,1,0:T(8,128)(2,1)}, bf16[3,112,640]{2,1,0:T(8,128)(2,1)S(1)}, u32[]{:S(2)}) copy-start(bf16[3,112,640]{2,1,0:T(8,128)(2,1)S(1)} %collective-permute-done.18.refs_3_) | copy-start | bytes 1290244
  518.2 185.2 %collective-permute-start.24 = (bf16[3,1,448,640]{3,2,1,0:T(8,128)(2,1)S(1)}, bf16[3,1,448,640]{3,2,1,0:T(8,128)(2,1)S(1)}, u32[]{:S(2)}, u32[]{:S(2)}) collective-permute-start(bf16[3,1,448,640]{3,2,1,0:T(8,128)(2,1)S(1)} %pad_maximum_fusion.3), channel_id=1, source_target_pairs={{0,4},{4,0},{1,5},{5,1},{2,6},{6,2},{3,7},{7,3}} | collective-permute-start | bytes 5160968 | tf_op jit(solution)/shard_map/ppermute | solution.py:327
  519.3 215.0 %collective-permute-start.25 = (bf16[3,1,448,640]{3,2,1,0:T(8,128)(2,1)}, bf16[3,1,448,640]{3,2,1,0:T(8,128)(2,1)}, u32[]{:S(2)}, u32[]{:S(2)}) collective-permute-start(bf16[3,1,448,640]{3,2,1,0:T(8,128)(2,1)} %pad_maximum_fusion.4), channel_id=1, source_target_pairs={{0,4},{4,0},{1,5},{5,1},{2,6},{6,2},{3,7},{7,3}} | collective-permute-start | bytes 5160968 | tf_op jit(solution)/shard_map/ppermute | solution.py:327
  521.4 90.4 %collective-permute-start.17 = (bf16[3,112,640]{2,1,0:T(8,128)(2,1)}, bf16[3,112,640]{2,1,0:T(8,128)(2,1)S(1)}, u32[]{:S(2)}, u32[]{:S(2)}) collective-permute-start(bf16[3,112,640]{2,1,0:T(8,128)(2,1)} %get-tuple-element.135), channel_id=1, source_target_pairs={{0,1},{1,0},{2,3},{3,2},{4,5},{5,4},{6,7},{7,6}} | collective-permute-start | bytes 1290248 | tf_op jit(solution)/shard_map/ppermute | solution.py:337
  522.1 89.8 %collective-permute-start.16 = (bf16[3,112,640]{2,1,0:T(8,128)(2,1)}, bf16[3,112,640]{2,1,0:T(8,128)(2,1)S(1)}, u32[]{:S(2)}, u32[]{:S(2)}) collective-permute-start(bf16[3,112,640]{2,1,0:T(8,128)(2,1)} %get-tuple-element.136), channel_id=1, source_target_pairs={{0,4},{1,5},{2,6},{3,7},{4,0},{5,1},{6,2},{7,3}} | collective-permute-start | bytes 1290248 | tf_op jit(solution)/shard_map/ppermute | solution.py:337
  611.8 0.8 copy-start.13
  611.8 0.9 copy-start.14
  703.5 1.2 copy-start.6
  740.9 10.2 copy-start.21
  751.1 13.6 %collective-permute-start.26 = (f32[2048,896]{1,0:T(8,128)}, f32[2048,896]{1,0:T(8,128)}, u32[]{:S(2)}, u32[]{:S(2)}) collective-permute-start(f32[2048,896]{1,0:T(8,128)} %combine.12), channel_id=1, source_target_pairs={{0,1},{1,0},{2,3},{3,2},{4,5},{5,4},{6,7},{7,6}} | collective-permute-start | bytes 22020104 | tf_op jit(solution)/shard_map/ppermute | solution.py:330
  777.5 17.0 %copy-start.20 = (s32[8,320]{1,0:T(8,128)S(1)}, s32[8,320]{1,0:T(8,128)}, u32[]{:S(2)}) copy-start(s32[8,320]{1,0:T(8,128)} %get-tuple-element.156) | copy-start | bytes 30724
  777.5 17.7 %copy-start.19 = (s32[8,320]{1,0:T(8,128)S(1)}, s32[8,320]{1,0:T(8,128)}, u32[]{:S(2)}) copy-start(s32[8,320]{1,0:T(8,128)} %get-tuple-element.160) | copy-start | bytes 30724
  794.2 28.9 %collective-permute-start.27 = (f32[2048,896]{1,0:T(8,128)}, f32[2048,896]{1,0:T(8,128)}, u32[]{:S(2)}, u32[]{:S(2)}) collective-permute-start(f32[2048,896]{1,0:T(8,128)} %combine.14), channel_id=1, source_target_pairs={{0,1},{1,0},{2,3},{3,2},{4,5},{5,4},{6,7},{7,6}} | collective-permute-start | bytes 22020104 | tf_op jit(solution)/shard_map/ppermute | solution.py:330
  842.2 16.9 %copy-start.18 = (s32[8,320]{1,0:T(8,128)S(1)}, s32[8,320]{1,0:T(8,128)}, u32[]{:S(2)}) copy-start(s32[8,320]{1,0:T(8,128)} %get-tuple-element.161) | copy-start | bytes 30724
  842.2 17.5 %copy-start.17 = (s32[8,320]{1,0:T(8,128)S(1)}, s32[8,320]{1,0:T(8,128)}, u32[]{:S(2)}) copy-start(s32[8,320]{1,0:T(8,128)} %get-tuple-element.162) | copy-start | bytes 30724
  859.0 15.0 %collective-permute-start.28 = (f32[2048,896]{1,0:T(8,128)}, f32[2048,896]{1,0:T(8,128)}, u32[]{:S(2)}, u32[]{:S(2)}) collective-permute-start(f32[2048,896]{1,0:T(8,128)} %combine.16), channel_id=1, source_target_pairs={{0,1},{1,0},{2,3},{3,2},{4,5},{5,4},{6,7},{7,6}} | collective-permute-start | bytes 22020104 | tf_op jit(solution)/shard_map/ppermute | solution.py:330
  906.7 22.2 %copy-start.16 = (s32[8,320]{1,0:T(8,128)S(1)}, s32[8,320]{1,0:T(8,128)}, u32[]{:S(2)}) copy-start(s32[8,320]{1,0:T(8,128)} %get-tuple-element.163) | copy-start | bytes 30724
  923.0 20.1 %collective-permute-start.29 = (f32[2048,896]{1,0:T(8,128)}, f32[2048,896]{1,0:T(8,128)}, u32[]{:S(2)}, u32[]{:S(2)}) collective-permute-start(f32[2048,896]{1,0:T(8,128)} %combine.18), channel_id=1, source_target_pairs={{0,1},{1,0},{2,3},{3,2},{4,5},{5,4},{6,7},{7,6}} | collective-permute-start | bytes 22020104 | tf_op jit(solution)/shard_map/ppermute | solution.py:330
  924.3 82.5 %collective-permute-start.32 = (f32[1024,896]{1,0:T(8,128)}, f32[1024,896]{1,0:T(8,128)}, u32[]{:S(2)}, u32[]{:S(2)}) collective-permute-start(f32[1024,896]{1,0:T(8,128)} %get-tuple-element.106), channel_id=1, source_target_pairs={{0,4},{4,0},{1,5},{5,1},{2,6},{6,2},{3,7},{7,3}} | collective-permute-start | bytes 11010056 | tf_op jit(solution)/shard_map/ppermute | solution.py:327
  925.2 82.5 %collective-permute-start.33 = (f32[1024,896]{1,0:T(8,128)}, f32[1024,896]{1,0:T(8,128)}, u32[]{:S(2)}, u32[]{:S(2)}) collective-permute-start(f32[1024,896]{1,0:T(8,128)} %get-tuple-element.91), channel_id=1, source_target_pairs={{0,2},{1,3},{2,0},{3,1},{4,6},{5,7},{6,4},{7,5}} | collective-permute-start | bytes 11010056 | tf_op jit(solution)/shard_map/ppermute | solution.py:333
  927.2 159.2 %collective-permute-start.30 = (f32[1024,896]{1,0:T(8,128)}, f32[1024,896]{1,0:T(8,128)}, u32[]{:S(2)}, u32[]{:S(2)}) collective-permute-start(f32[1024,896]{1,0:T(8,128)} %get-tuple-element.96), channel_id=1, source_target_pairs={{0,2},{1,3},{2,0},{3,1},{4,6},{5,7},{6,4},{7,5}} | collective-permute-start | bytes 11010056 | tf_op jit(solution)/shard_map/ppermute | solution.py:333
  927.3 159.1 %collective-permute-start.31 = (f32[1024,896]{1,0:T(8,128)}, f32[1024,896]{1,0:T(8,128)}, u32[]{:S(2)}, u32[]{:S(2)}) collective-permute-start(f32[1024,896]{1,0:T(8,128)} %get-tuple-element.104), channel_id=1, source_target_pairs={{0,4},{4,0},{1,5},{5,1},{2,6},{6,2},{3,7},{7,3}} | collective-permute-start | bytes 11010056 | tf_op jit(solution)/shard_map/ppermute | solution.py:327
  943.1 64.6 %copy-start.4 = (f32[1024,896]{1,0:T(8,128)S(1)}, f32[1024,896]{1,0:T(8,128)}, u32[]{:S(2)}) copy-start(f32[1024,896]{1,0:T(8,128)} %get-tuple-element.111) | copy-start | bytes 11010052
  1007.8 6.4 copy-start.5
  1012.2 74.2 %copy-start.1 = (bf16[2048,896]{1,0:T(8,128)(2,1)S(1)}, bf16[2048,896]{1,0:T(8,128)(2,1)}, u32[]{:S(2)}) copy-start(bf16[2048,896]{1,0:T(8,128)(2,1)} %x_ref.1) | copy-start | bytes 11010052
  1012.2 151.9 %collective-permute-start.35 = (f32[1024,896]{1,0:T(8,128)}, f32[1024,896]{1,0:T(8,128)}, u32[]{:S(2)}, u32[]{:S(2)}) collective-permute-start(f32[1024,896]{1,0:T(8,128)} %add.133), channel_id=1, source_target_pairs={{0,2},{1,3},{2,0},{3,1},{4,6},{5,7},{6,4},{7,5}} | collective-permute-start | bytes 11010056 | tf_op jit(solution)/shard_map/ppermute | solution.py:333
  1018.4 145.7 %collective-permute-start.34 = (f32[1024,896]{1,0:T(8,128)}, f32[1024,896]{1,0:T(8,128)}, u32[]{:S(2)}, u32[]{:S(2)}) collective-permute-start(f32[1024,896]{1,0:T(8,128)} %add.132), channel_id=1, source_target_pairs={{0,4},{4,0},{1,5},{5,1},{2,6},{6,2},{3,7},{7,3}} | collective-permute-start | bytes 11010056 | tf_op jit(solution)/shard_map/ppermute | solution.py:327

commit v4 on v3

--- a/solution.py
+++ b/solution.py
@@ -459,39 +459,37 @@
         make_lists()
         gather(5)
         gather(7)
-        early = [(experts(0), 0), (experts(1), 0)]
+        early = [(experts(0), 0)]
         shared(7)
+        early.append((experts(1), 0))
         shared(5)
+        shared(3)
+        shared(1)
         early.append((experts(2), 0))
-        n_pre = sum(CHUNKS[:3])
-        pre7 = part(7, [base[7]], early, 0, False)
-        pre5 = part(5, [base[5]], early, 0, False)
+        shared(6)
+        shared(4)
         early.append((experts(3), 0))
-        shared(6)
-        tail = experts(4, (0, 2))
-        late = [early[3], (tail, 0)]
-        mate7 = over_core(part(7, [pre7], late, n_pre, False))
-        rest = experts(4, (2, n_dev))
-        full = early + [(rest, 2)]
-        diag = part(5, [pre5, mate7], late, n_pre, True)
+        diag_rows = early + [(experts(4, (0, 2)), 0)]
+        mate7 = over_core(part(7, [base[7]], diag_rows, 0, False))
+        full = early + [(experts(4, (2, n_dev)), 2)]
+        diag = part(5, [base[5], mate7], diag_rows, 0, True)
         diag_x = over_x(diag[0])
         diag_y = over_y(diag[1])
         mate6 = over_core(part(6, [base[6]], full, 0, False))
-        shared(4)
-        shared(3)
+        mate3 = over_core(part(3, [base[3]], full, 0, False))
         to_x = part(4, [base[4], mate6], full, 0, True)
         x_top = over_x(to_x[0])
-        mate3 = over_core(part(3, [base[3]], full, 0, False))
-        shared(1)
         to_y = part(1, [base[1], mate3], full, 0, True)
         y_bot = over_y(to_y[1])
         shared(2)
+        up_x, up_y, to_x1, to_y0 = after(diag_y, diag_x, to_x[1], to_y[0])
+        last_x, last_y = to_x1 + up_x, to_y0 + up_y
+        last[0] = (last_x, last_y)
+        x_bot = over_x(last_x)
+        y_top = over_y(last_y)
         mate2 = over_core(part(2, [base[2]], full, 0, False))
         shared(0)
         own = part(0, [base[0], mate2], full, 0, True)
-        up_x, up_y, to_x1, to_y0 = after(diag_y, diag_x, to_x[1], to_y[0])
-        x_bot = over_x(to_x1 + up_x)
-        y_top = over_y(to_y0 + up_y)
         h = tok_count // 2
         sum_top = x_loc[:h].astype(F32) + own[0] + x_top
         sum_bot = x_loc[h:].astype(F32) + own[1] + y_bot

time: 1190 us -> 1150 us (0.966)
  Pallas kernels: 523 us -> 507 us
  waiting for transfers between devices: 521 us -> 509 us
    ppermute x9, waiting for transfers between devices: 44.7 us -> 180 us  [over_y(): return lax.ppermute(v, 'data', [(i, i ^ 1) for i in range(data_n)])]
    ppermute x5, waiting for transfers between devices: 136 us -> 3.32 us  [over_x(): return lax.ppermute(v, 'expert', [(i, i ^ 2) for i in range(exp_n)])]
    pallas_call x10 -> x8, Pallas kernels: 159 us -> 142 us  [combine(): pl.pallas_call(functools.partial(combine_kernel, n_base, tuple(where_of),...]
    ppermute x14, waiting for transfers between devices: 341 us -> 326 us  [over_all(): lax.ppermute(v, ('data', 'expert'), [(i, i ^ flip) for i in range(n_dev)])]
  transfers between devices with their start and end apart: 36 -> 36, of which waited for: 10 -> 14; matrix products, arithmetic and copies ran while one was open for 8% -> 8% of each run, Pallas kernels for 33% -> 37%
where the time goes in v4:
time: 1150 us; the launch traced here: 1140 us
  waiting for transfers between devices  509 us (44%)
  Pallas kernels  507 us (44%)
  other arithmetic  66.1 us (6%)
  local copies, waits for them, and re-layouts  29.1 us (3%)
  starting transfers between devices  25.6 us (2%)
    ppermute x14, waiting for transfers between devices, over_all(): lax.ppermute(v, ('data', 'expert'), [(i, i ^ flip) for i in range(n_dev)])  326 us
    ppermute x9, waiting for transfers between devices, over_y(): return lax.ppermute(v, 'data', [(i, i ^ 1) for i in range(data_n)])  180 us
    pallas_call x8, Pallas kernels, combine(): pl.pallas_call(functools.partial(combine_kernel, n_base, tuple(where_of),...  142 us
    pallas_call x6, Pallas kernels, expert_rows(): pl.pallas_call(functools.partial(expert_kernel, half), out_shape=jax.Shap...  124 us
    pallas_call x8, Pallas kernels, gather_rows(): pl.pallas_call(functools.partial(gather_kernel, per_step, capacity), out_...  118 us
    pallas_call x8, Pallas kernels, shared_part(): pl.pallas_call(shared_kernel, out_shape=jax.ShapeDtypeStruct((tok_count,...  109 us
    reduce_sum x1, other arithmetic, make_lists(): jnp.sum(jnp.where(same, t_ids[None, None, :] - tok_count, 0), axis=2)  30.8 us
  transfers between devices with their start and end apart: 36, of which 14 were waited for; matrix products, arithmetic and copies ran while one was open for 8% of the time, Pallas kernels for 37%

profile of v4, /device:TPU:6, one launch (start us, length us, event | category | flops | bytes accessed | tf_op | source)
XLA Modules:
  0.0 1138.4 jit_solution(6214002893134645015)
XLA Ops:
  1.4 1.5 pad_maximum_fusion.5
  8.1 2.0 maximum_bitcast_fusion
  10.1 3.1 gather_fusion
  15.1 1.8 dynamic-slice_bitcast_fusion.10
  18.4 1.5 pad_maximum_fusion.3
  19.8 2.2 dynamic-slice_bitcast_fusion
  22.1 3.7 dynamic-slice_bitcast_fusion.1
  25.8 2.0 pad_maximum_fusion.2
  27.8 2.0 pad_maximum_fusion.1
  29.8 2.0 pad_maximum_fusion
  33.5 53.5 %collective-permute-done = f32[16,2048]{1,0:T(8,128)} collective-permute-done((f32[16,2048]{1,0:T(8,128)}, f32[16,2048]{1,0:T(8,128)}, u32[]{:S(2)}, u32[]{:S(2)}) %collective-permute-start) | collective-permute-done | bytes 131104 | tf_op jit(solution)/shard_map/ppermute | solution.py:337
  90.0 1.5 collective-permute-start.3
  92.4 80.9 %collective-permute-done.3 = f32[16,2048]{1,0:T(8,128)S(1)} collective-permute-done((f32[16,2048]{1,0:T(8,128)}, f32[16,2048]{1,0:T(8,128)S(1)}, u32[]{:S(2)}, u32[]{:S(2)}) %collective-permute-start.3) | collective-permute-done | bytes 131104 | tf_op jit(solution)/shard_map/ppermute | solution.py:337
  173.5 5.9 collective-permute-done.4
  179.4 5.1 collective-permute-done.5
  185.2 5.6 collective-permute-done.6
  191.9 1.6 compare_reduce_fusion
  193.5 10.1 collective-permute-done.21.refs_7_
  203.6 1.5 collective-permute-start.20
  210.1 14.7 %gather_rows.8.refs_0_ = bf16[8,8,320,896]{3,2,1,0:T(8,128)(2,1)} custom-call(s32[16,2048]{1,0:T(8,128)} %get-tuple-element.153.pos_ref, bf16[2048,896]{1,0:T(8,128)(2,1)} %x_ref.1), custom_call_target="tpu_custom_call" | custom-call | flops 146800640 | bytes 4587520 | tf_op jit(solution)/shard_map/gather_rows/pallas_call | solution.py:61
  224.8 14.6 %gather_rows.9.refs_0_ = bf16[8,8,320,896]{3,2,1,0:T(8,128)(2,1)} custom-call(s32[16,2048]{1,0:T(8,128)} %get-tuple-element.152.pos_ref, bf16[2048,896]{1,0:T(8,128)(2,1)} %copy-done.2, bf16[8,8,320,896]{3,2,1,0:T(8,128)(2,1)} %gather_rows.8.refs_0_), custom_call_target="tpu_custom_call", output_to_operand_aliasing={{}: (2, {})} | custom-call | flops 146800640 | bytes 4587520 | tf_op jit(solution)/shard_map/gather_rows/pallas_call | solution.py:61
  239.4 14.9 %gather_rows.10.refs_0_ = bf16[8,8,320,896]{3,2,1,0:T(8,128)(2,1)} custom-call(s32[16,2048]{1,0:T(8,128)} %get-tuple-element.151.pos_ref, bf16[2048,896]{1,0:T(8,128)(2,1)} %collective-permute-done.8.x_ref, bf16[8,8,320,896]{3,2,1,0:T(8,128)(2,1)} %gather_rows.9.refs_0_), custom_call_target="tpu_custom_call", output_to_operand_aliasing={{}: (2, {})} | custom-call | flops 146800640 | bytes 4587520 | tf_op jit(solution)/shard_map/gather_rows/pallas_call | solution.py:61
  254.3 14.6 %gather_rows.11.refs_0_ = bf16[8,8,320,896]{3,2,1,0:T(8,128)(2,1)} custom-call(s32[16,2048]{1,0:T(8,128)} %get-tuple-element.150.pos_ref, bf16[2048,896]{1,0:T(8,128)(2,1)} %collective-permute-done.9.x_ref, bf16[8,8,320,896]{3,2,1,0:T(8,128)(2,1)} %gather_rows.10.refs_0_), custom_call_target="tpu_custom_call", output_to_operand_aliasing={{}: (2, {})} | custom-call | flops 146800640 | bytes 4587520 | tf_op jit(solution)/shard_map/gather_rows/pallas_call | solution.py:61
  268.9 14.6 %gather_rows.12.refs_0_ = bf16[8,8,320,896]{3,2,1,0:T(8,128)(2,1)} custom-call(s32[16,2048]{1,0:T(8,128)} %get-tuple-element.149.pos_ref, bf16[2048,896]{1,0:T(8,128)(2,1)} %collective-permute-done.10.x_ref, bf16[8,8,320,896]{3,2,1,0:T(8,128)(2,1)} %gather_rows.11.refs_0_), custom_call_target="tpu_custom_call", output_to_operand_aliasing={{}: (2, {})} | custom-call | flops 146800640 | bytes 4587520 | tf_op jit(solution)/shard_map/gather_rows/pallas_call | solution.py:61
  283.6 14.8 %gather_rows.13.refs_0_ = bf16[8,8,320,896]{3,2,1,0:T(8,128)(2,1)} custom-call(s32[16,2048]{1,0:T(8,128)} %get-tuple-element.155.pos_ref, bf16[2048,896]{1,0:T(8,128)(2,1)} %collective-permute-done.11.x_ref, bf16[8,8,320,896]{3,2,1,0:T(8,128)(2,1)} %gather_rows.12.refs_0_), custom_call_target="tpu_custom_call", output_to_operand_aliasing={{}: (2, {})} | custom-call | flops 146800640 | bytes 4587520 | tf_op jit(solution)/shard_map/gather_rows/pallas_call | solution.py:61
  299.1 1.9 collective-permute-start.22
  301.2 30.8 %select_reduce_fusion = s32[64,320]{1,0:T(8,128)S(1)} fusion(s32[2048]{0:T(1024)S(1)} %iota_add_fusion, s32[64,2048]{1,0:T(8,128)S(1)} %fusion.3), kind=kLoop, calls=%fused_computation.1 | loop fusion | flops 125808640 | bytes 614400 | tf_op jit(solution)/shard_map/reduce_sum | solution.py:437
  333.4 1.9 collective-permute-start.24
  335.4 41.2 %collective-permute-done.14.rv_ref = bf16[3,2,448,640]{3,2,1,0:T(8,128)(2,1)} collective-permute-done((bf16[3,2,448,640]{3,2,1,0:T(8,128)(2,1)}, bf16[3,2,448,640]{3,2,1,0:T(8,128)(2,1)}, u32[]{:S(2)}, u32[]{:S(2)}) %collective-permute-start.14) | collective-permute-done | bytes 3440672 | tf_op jit(solution)/shard_map/ppermute | solution.py:327
  377.9 1.9 collective-permute-start.15
  381.1 14.6 %gather_rows.14.refs_0_ = bf16[8,8,320,896]{3,2,1,0:T(8,128)(2,1)} custom-call(s32[16,2048]{1,0:T(8,128)} %get-tuple-element.148.pos_ref, bf16[2048,896]{1,0:T(8,128)(2,1)} %collective-permute-done.12.x_ref, bf16[8,8,320,896]{3,2,1,0:T(8,128)(2,1)} %gather_rows.13.refs_0_), custom_call_target="tpu_custom_call", output_to_operand_aliasing={{}: (2, {})} | custom-call | flops 146800640 | bytes 4587520 | tf_op jit(solution)/shard_map/gather_rows/pallas_call | solution.py:61
  396.6 15.1 %gather_rows.15.xg_ref = bf16[8,8,320,896]{3,2,1,0:T(8,128)(2,1)} custom-call(s32[16,2048]{1,0:T(8,128)} %get-tuple-element.154.pos_ref, bf16[2048,896]{1,0:T(8,128)(2,1)} %collective-permute-done.13.x_ref, bf16[8,8,320,896]{3,2,1,0:T(8,128)(2,1)} %gather_rows.14.refs_0_), custom_call_target="tpu_custom_call", output_to_operand_aliasing={{}: (2, {})} | custom-call | flops 146800640 | bytes 4587520 | tf_op jit(solution)/shard_map/gather_rows/pallas_call | solution.py:61
  411.6 29.2 %expert_rows.6.refs_4_.refs_5_ = bf16[2,8,320,896]{3,2,1,0:T(8,128)(2,1)} custom-call(s32[1]{0:T(128)} %bitcast.32.y_ref, bf16[8,8,320,896]{3,2,1,0:T(8,128)(2,1)} %gather_rows.15.xg_ref, bf16[16,448,640]{2,1,0:T(8,128)(2,1)} %og_ref.11, bf16[16,448,640]{2,1,0:T(8,128)(2,1)} %ou_ref.11, bf16[16,448,640]{2,1,0:T(8,128)(2,1)} %bitcast.149, ...), custom_call_target="tpu_custom_call" | custom-call | flops 275251200 | bytes 18350080 | tf_op jit(solution)/shard_map/expert_rows/pallas_call | solution.py:107
  440.9 165.1 %collective-permute-done.15.refs_1_ = bf16[3,112,640]{2,1,0:T(8,128)(2,1)S(1)} collective-permute-done((bf16[3,112,640]{2,1,0:T(8,128)(2,1)}, bf16[3,112,640]{2,1,0:T(8,128)(2,1)S(1)}, u32[]{:S(2)}, u32[]{:S(2)}) %collective-permute-start.15) | collective-permute-done | bytes 430112 | tf_op jit(solution)/shard_map/ppermute | solution.py:337
  606.8 4.5 assemble.1.w_ref
  611.3 13.6 %shared_part.8.refs_3_ = f32[2048,896]{1,0:T(8,128)} custom-call(bf16[2048,896]{1,0:T(8,128)(2,1)} %collective-permute-done.13.x_ref, bf16[3,896,640]{2,1,0:T(8,128)(2,1)} %assemble.1.w_ref), custom_call_target="tpu_custom_call" | custom-call | flops 110100480 | bytes 11010048 | tf_op jit(solution)/shard_map/shared_part/pallas_call | solution.py:136
  624.9 29.3 %expert_rows.7.refs_5_.refs_6_ = bf16[2,8,320,896]{3,2,1,0:T(8,128)(2,1)} custom-call(s32[1]{0:T(128)} %bitcast.32.y_ref, bf16[8,8,320,896]{3,2,1,0:T(8,128)(2,1)} %gather_rows.15.xg_ref, bf16[16,448,640]{2,1,0:T(8,128)(2,1)} %og_ref.11, bf16[16,448,640]{2,1,0:T(8,128)(2,1)} %ou_ref.11, bf16[16,448,640]{2,1,0:T(8,128)(2,1)} %bitcast.150, ...), custom_call_target="tpu_custom_call" | custom-call | flops 275251200 | bytes 18350080 | tf_op jit(solution)/shard_map/expert_rows/pallas_call | solution.py:107
  654.3 13.6 %shared_part.9.refs_3_ = f32[2048,896]{1,0:T(8,128)} custom-call(bf16[2048,896]{1,0:T(8,128)(2,1)} %collective-permute-done.12.x_ref, bf16[3,896,640]{2,1,0:T(8,128)(2,1)} %assemble.1.w_ref), custom_call_target="tpu_custom_call" | custom-call | flops 110100480 | bytes 11010048 | tf_op jit(solution)/shard_map/shared_part/pallas_call | solution.py:136
  667.8 13.7 %shared_part.10.refs_3_ = f32[2048,896]{1,0:T(8,128)} custom-call(bf16[2048,896]{1,0:T(8,128)(2,1)} %collective-permute-done.10.x_ref, bf16[3,896,640]{2,1,0:T(8,128)(2,1)} %assemble.1.w_ref), custom_call_target="tpu_custom_call" | custom-call | flops 110100480 | bytes 11010048 | tf_op jit(solution)/shard_map/shared_part/pallas_call | solution.py:136
  681.5 13.6 %shared_part.11.refs_3_ = f32[2048,896]{1,0:T(8,128)} custom-call(bf16[2048,896]{1,0:T(8,128)(2,1)} %collective-permute-done.8.x_ref, bf16[3,896,640]{2,1,0:T(8,128)(2,1)} %assemble.1.w_ref), custom_call_target="tpu_custom_call" | custom-call | flops 110100480 | bytes 11010048 | tf_op jit(solution)/shard_map/shared_part/pallas_call | solution.py:136
  695.1 29.4 %expert_rows.8.refs_6_.refs_7_ = bf16[2,8,320,896]{3,2,1,0:T(8,128)(2,1)} custom-call(s32[1]{0:T(128)} %bitcast.32.y_ref, bf16[8,8,320,896]{3,2,1,0:T(8,128)(2,1)} %gather_rows.15.xg_ref, bf16[16,448,640]{2,1,0:T(8,128)(2,1)} %og_ref.11, bf16[16,448,640]{2,1,0:T(8,128)(2,1)} %ou_ref.11, bf16[16,448,640]{2,1,0:T(8,128)(2,1)} %bitcast.151, ...), custom_call_target="tpu_custom_call" | custom-call | flops 275251200 | bytes 18350080 | tf_op jit(solution)/shard_map/expert_rows/pallas_call | solution.py:107
  724.5 13.5 %shared_part.12.refs_3_ = f32[2048,896]{1,0:T(8,128)} custom-call(bf16[2048,896]{1,0:T(8,128)(2,1)} %collective-permute-done.11.x_ref, bf16[3,896,640]{2,1,0:T(8,128)(2,1)} %assemble.1.w_ref), custom_call_target="tpu_custom_call" | custom-call | flops 110100480 | bytes 11010048 | tf_op jit(solution)/shard_map/shared_part/pallas_call | solution.py:136
  738.0 13.6 %shared_part.13.refs_3_ = f32[2048,896]{1,0:T(8,128)} custom-call(bf16[2048,896]{1,0:T(8,128)(2,1)} %collective-permute-done.9.x_ref, bf16[3,896,640]{2,1,0:T(8,128)(2,1)} %assemble.1.w_ref), custom_call_target="tpu_custom_call" | custom-call | flops 110100480 | bytes 11010048 | tf_op jit(solution)/shard_map/shared_part/pallas_call | solution.py:136
  751.6 16.3 %expert_rows.9.refs_7_.refs_8_ = bf16[1,8,320,896]{3,2,1,0:T(8,128)(2,1)} custom-call(s32[1]{0:T(128)} %bitcast.32.y_ref, bf16[8,8,320,896]{3,2,1,0:T(8,128)(2,1)} %gather_rows.15.xg_ref, bf16[16,448,640]{2,1,0:T(8,128)(2,1)} %og_ref.11, bf16[16,448,640]{2,1,0:T(8,128)(2,1)} %ou_ref.11, bf16[16,448,640]{2,1,0:T(8,128)(2,1)} %bitcast.152, ...), custom_call_target="tpu_custom_call" | custom-call | flops 137625600 | bytes 9175040 | tf_op jit(solution)/shard_map/expert_rows/pallas_call | solution.py:107
  767.9 6.6 expert_rows.10.refs_8_.refs_9_
  774.5 16.3 %combine.8 = f32[2048,896]{1,0:T(8,128)} custom-call(s32[1,8]{1,0:T(1,128)} %get-tuple-element.165.refs_0_, s32[1,2560]{1,0:T(1,128)} %squeeze.150.refs_1_, f32[1,16512]{1,0:T(1,128)} %get-tuple-element.146.refs_2_, f32[2048,896]{1,0:T(8,128)} %shared_part.8.refs_3_, bf16[2,8,320,896]{3,2,1,0:T(8,128)(2,1)} %expert_rows.6.refs_4_.refs_5_, ...), custom_call_target="tpu_custom_call" | custom-call | flops 73400320 | bytes 14680064 | tf_op jit(solution)/shard_map/combine/pallas_call | solution.py:249
  792.2 12.9 %expert_rows.11.refs_8_.refs_9_ = bf16[1,6,320,896]{3,2,1,0:T(8,128)(2,1)} custom-call(s32[1]{0:T(128)} %bitcast.32.y_ref, bf16[8,8,320,896]{3,2,1,0:T(8,128)(2,1)} %gather_rows.15.xg_ref, bf16[16,448,640]{2,1,0:T(8,128)(2,1)} %og_ref.11, bf16[16,448,640]{2,1,0:T(8,128)(2,1)} %ou_ref.11, bf16[16,448,640]{2,1,0:T(8,128)(2,1)} %bitcast.154, ...), custom_call_target="tpu_custom_call" | custom-call | flops 103219200 | bytes 6881280 | tf_op jit(solution)/shard_map/expert_rows/pallas_call | solution.py:107
  805.1 19.0 %combine.9 = (f32[1024,896]{1,0:T(8,128)}, f32[1024,896]{1,0:T(8,128)}) custom-call(s32[1,8]{1,0:T(1,128)} %get-tuple-element.166.refs_0_, s32[1,2560]{1,0:T(1,128)} %squeeze.145.refs_1_, f32[1,16512]{1,0:T(1,128)} %get-tuple-element.145.refs_2_, f32[2048,896]{1,0:T(8,128)} %shared_part.9.refs_3_, f32[2048,896]{1,0:T(8,128)} %collective-permute-done.26.refs_4_, ...), custom_call_target="tpu_custom_call" | custom-call | flops 73400320 | bytes 14680064 | tf_op jit(solution)/shard_map/combine/pallas_call | solution.py:249
  824.2 16.7 %combine.10 = f32[2048,896]{1,0:T(8,128)} custom-call(s32[1,8]{1,0:T(1,128)} %get-tuple-element.167.refs_0_, s32[1,2560]{1,0:T(1,128)} %squeeze.142.refs_1_, f32[1,16512]{1,0:T(1,128)} %get-tuple-element.144.refs_2_, f32[2048,896]{1,0:T(8,128)} %shared_part.12.refs_3_, bf16[2,8,320,896]{3,2,1,0:T(8,128)(2,1)} %expert_rows.6.refs_4_.refs_5_, ...), custom_call_target="tpu_custom_call" | custom-call | flops 73400320 | bytes 14680064 | tf_op jit(solution)/shard_map/combine/pallas_call | solution.py:249
  841.8 16.7 %combine.11 = f32[2048,896]{1,0:T(8,128)} custom-call(s32[1,8]{1,0:T(1,128)} %get-tuple-element.168.refs_0_, s32[1,2560]{1,0:T(1,128)} %squeeze.139.refs_1_, f32[1,16512]{1,0:T(1,128)} %get-tuple-element.143.refs_2_, f32[2048,896]{1,0:T(8,128)} %shared_part.10.refs_3_, bf16[2,8,320,896]{3,2,1,0:T(8,128)(2,1)} %expert_rows.6.refs_4_.refs_5_, ...), custom_call_target="tpu_custom_call" | custom-call | flops 73400320 | bytes 14680064 | tf_op jit(solution)/shard_map/combine/pallas_call | solution.py:249
  858.6 1.6 collective-permute-start.29
  863.2 19.1 %combine.12 = (f32[1024,896]{1,0:T(8,128)}, f32[1024,896]{1,0:T(8,128)}) custom-call(s32[1,8]{1,0:T(1,128)} %get-tuple-element.169.refs_0_, s32[1,2560]{1,0:T(1,128)} %squeeze.136.refs_1_, f32[1,16512]{1,0:T(1,128)} %get-tuple-element.142.refs_2_, f32[2048,896]{1,0:T(8,128)} %shared_part.13.refs_3_, f32[2048,896]{1,0:T(8,128)} %collective-permute-done.27.refs_4_, ...), custom_call_target="tpu_custom_call" | custom-call | flops 73400320 | bytes 14680064 | tf_op jit(solution)/shard_map/combine/pallas_call | solution.py:249
  882.4 19.2 %combine.13 = (f32[1024,896]{1,0:T(8,128)}, f32[1024,896]{1,0:T(8,128)}) custom-call(s32[1,8]{1,0:T(1,128)} %get-tuple-element.164.refs_0_, s32[1,2560]{1,0:T(1,128)} %squeeze.133.refs_1_, f32[1,16512]{1,0:T(1,128)} %get-tuple-element.140.refs_2_, f32[2048,896]{1,0:T(8,128)} %shared_part.11.refs_3_, f32[2048,896]{1,0:T(8,128)} %collective-permute-done.28.refs_4_, ...), custom_call_target="tpu_custom_call" | custom-call | flops 73400320 | bytes 14680064 | tf_op jit(solution)/shard_map/combine/pallas_call | solution.py:249
  901.6 13.7 %shared_part.14.refs_3_ = f32[2048,896]{1,0:T(8,128)} custom-call(bf16[2048,896]{1,0:T(8,128)(2,1)} %copy-done.2, bf16[3,896,640]{2,1,0:T(8,128)(2,1)} %assemble.1.w_ref), custom_call_target="tpu_custom_call" | custom-call | flops 110100480 | bytes 11010048 | tf_op jit(solution)/shard_map/shared_part/pallas_call | solution.py:136
  915.3 25.3 %collective-permute-done.29 = f32[1024,896]{1,0:T(8,128)} collective-permute-done((f32[1024,896]{1,0:T(8,128)}, f32[1024,896]{1,0:T(8,128)}, u32[]{:S(2)}, u32[]{:S(2)}) %collective-permute-start.29) | collective-permute-done | bytes 3670048 | tf_op jit(solution)/shard_map/ppermute | solution.py:327
  942.0 4.4 add.128
  946.4 4.3 add.129
  950.7 16.3 %combine.14 = f32[2048,896]{1,0:T(8,128)} custom-call(s32[1,8]{1,0:T(1,128)} %get-tuple-element.170.refs_0_, s32[1,2560]{1,0:T(1,128)} %squeeze.130.refs_1_, f32[1,16512]{1,0:T(1,128)} %get-tuple-element.141.refs_2_, f32[2048,896]{1,0:T(8,128)} %shared_part.14.refs_3_, bf16[2,8,320,896]{3,2,1,0:T(8,128)(2,1)} %expert_rows.6.refs_4_.refs_5_, ...), custom_call_target="tpu_custom_call" | custom-call | flops 73400320 | bytes 14680064 | tf_op jit(solution)/shard_map/combine/pallas_call | solution.py:249
  971.9 13.6 %shared_part.15.refs_3_ = f32[2048,896]{1,0:T(8,128)} custom-call(bf16[2048,896]{1,0:T(8,128)(2,1)} %x_ref.1, bf16[3,896,640]{2,1,0:T(8,128)(2,1)} %assemble.1.w_ref), custom_call_target="tpu_custom_call" | custom-call | flops 110100480 | bytes 11010048 | tf_op jit(solution)/shard_map/shared_part/pallas_call | solution.py:136
  985.4 18.9 %combine.15 = (f32[1024,896]{1,0:T(8,128)}, f32[1024,896]{1,0:T(8,128)}) custom-call(s32[1,8]{1,0:T(1,128)} %get-tuple-element.171.refs_0_, s32[1,2560]{1,0:T(1,128)} %squeeze.127.refs_1_, f32[1,16512]{1,0:T(1,128)} %get-tuple-element.147.refs_2_, f32[2048,896]{1,0:T(8,128)} %shared_part.15.refs_3_, f32[2048,896]{1,0:T(8,128)} %collective-permute-done.31.refs_4_, ...), custom_call_target="tpu_custom_call" | custom-call | flops 73400320 | bytes 14680064 | tf_op jit(solution)/shard_map/combine/pallas_call | solution.py:249
  1004.4 45.3 %collective-permute-done.33 = f32[1024,896]{1,0:T(8,128)} collective-permute-done((f32[1024,896]{1,0:T(8,128)}, f32[1024,896]{1,0:T(8,128)}, u32[]{:S(2)}, u32[]{:S(2)}) %collective-permute-start.33) | collective-permute-done | bytes 3670048 | tf_op jit(solution)/shard_map/ppermute | solution.py:327
  1050.7 9.3 add_add_fusion
  1060.0 67.7 %collective-permute-done.34.b_ref = f32[1024,896]{1,0:T(8,128)} collective-permute-done((f32[1024,896]{1,0:T(8,128)}, f32[1024,896]{1,0:T(8,128)}, u32[]{:S(2)}, u32[]{:S(2)}) %collective-permute-start.34) | collective-permute-done | bytes 3670048 | tf_op jit(solution)/shard_map/ppermute | solution.py:327
  1128.6 9.3 finish.1
  (142 shorter events, 42.7 us)
Async XLA Ops:
  0.0 6.6 copy-start.6
  0.0 87.0 %collective-permute-start.8 = (bf16[2048,896]{1,0:T(8,128)(2,1)}, bf16[2048,896]{1,0:T(8,128)(2,1)}, u32[]{:S(2)}, u32[]{:S(2)}) collective-permute-start(bf16[2048,896]{1,0:T(8,128)(2,1)} %x_ref.1), channel_id=1, source_target_pairs={{0,4},{4,0},{1,5},{5,1},{2,6},{6,2},{3,7},{7,3}} | collective-permute-start | bytes 11010056 | tf_op jit(solution)/shard_map/ppermute | solution.py:327
  0.5 87.0 %collective-permute-start.9 = (bf16[2048,896]{1,0:T(8,128)(2,1)}, bf16[2048,896]{1,0:T(8,128)(2,1)}, u32[]{:S(2)}, u32[]{:S(2)}) collective-permute-start(bf16[2048,896]{1,0:T(8,128)(2,1)} %x_ref.1), channel_id=1, source_target_pairs={{0,2},{1,3},{2,0},{3,1},{4,6},{5,7},{6,4},{7,5}} | collective-permute-start | bytes 11010056 | tf_op jit(solution)/shard_map/ppermute | solution.py:333
  2.9 87.1 %collective-permute-start.2 = (f32[16,2048]{1,0:T(8,128)}, f32[16,2048]{1,0:T(8,128)}, u32[]{:S(2)}, u32[]{:S(2)}) collective-permute-start(f32[16,2048]{1,0:T(8,128)} %pad_maximum_fusion.5), channel_id=1, source_target_pairs={{0,5},{1,4},{2,7},{3,6},{4,1},{5,0},{6,3},{7,2}} | collective-permute-start | bytes 393224 | tf_op jit(solution)/shard_map/ppermute | solution.py:337
  3.8 84.7 %collective-permute-start.1 = (f32[16,2048]{1,0:T(8,128)}, f32[16,2048]{1,0:T(8,128)}, u32[]{:S(2)}, u32[]{:S(2)}) collective-permute-start(f32[16,2048]{1,0:T(8,128)} %pad_maximum_fusion.5), channel_id=1, source_target_pairs={{0,1},{1,0},{2,3},{3,2},{4,5},{5,4},{6,7},{7,6}} | collective-permute-start | bytes 393224 | tf_op jit(solution)/shard_map/ppermute | solution.py:337
  5.0 82.0 %collective-permute-start = (f32[16,2048]{1,0:T(8,128)}, f32[16,2048]{1,0:T(8,128)}, u32[]{:S(2)}, u32[]{:S(2)}) collective-permute-start(f32[16,2048]{1,0:T(8,128)} %pad_maximum_fusion.5), channel_id=1, source_target_pairs={{0,4},{1,5},{2,6},{3,7},{4,0},{5,1},{6,2},{7,3}} | collective-permute-start | bytes 393224 | tf_op jit(solution)/shard_map/ppermute | solution.py:337
  6.5 1.3 copy-start.7
  29.8 2.0 copy-start.14
  32.2 54.8 %copy-start = (bf16[2048,896]{1,0:T(8,128)(2,1)S(1)}, bf16[2048,896]{1,0:T(8,128)(2,1)}, u32[]{:S(2)}) copy-start(bf16[2048,896]{1,0:T(8,128)(2,1)} %x_ref.1) | copy-start | bytes 11010052
  87.0 118.0 %collective-permute-start.7 = (bf16[2048,896]{1,0:T(8,128)(2,1)S(1)}, bf16[2048,896]{1,0:T(8,128)(2,1)S(1)}, u32[]{:S(2)}, u32[]{:S(2)}) collective-permute-start(bf16[2048,896]{1,0:T(8,128)(2,1)S(1)} %copy-done), channel_id=1, source_target_pairs={{0,1},{1,0},{2,3},{3,2},{4,5},{5,4},{6,7},{7,6}} | collective-permute-start | bytes 11010056 | tf_op jit(solution)/shard_map/ppermute | solution.py:330
  87.0 118.6 %collective-permute-start.10 = (bf16[2048,896]{1,0:T(8,128)(2,1)}, bf16[2048,896]{1,0:T(8,128)(2,1)}, u32[]{:S(2)}, u32[]{:S(2)}) collective-permute-start(bf16[2048,896]{1,0:T(8,128)(2,1)} %collective-permute-done.8.x_ref), channel_id=1, source_target_pairs={{0,1},{1,0},{2,3},{3,2},{4,5},{5,4},{6,7},{7,6}} | collective-permute-start | bytes 11010056 | tf_op jit(solution)/shard_map/ppermute | solution.py:330
  87.5 119.1 %collective-permute-start.11 = (bf16[2048,896]{1,0:T(8,128)(2,1)}, bf16[2048,896]{1,0:T(8,128)(2,1)}, u32[]{:S(2)}, u32[]{:S(2)}) collective-permute-start(bf16[2048,896]{1,0:T(8,128)(2,1)} %collective-permute-done.9.x_ref), channel_id=1, source_target_pairs={{0,1},{1,0},{2,3},{3,2},{4,5},{5,4},{6,7},{7,6}} | collective-permute-start | bytes 11010056 | tf_op jit(solution)/shard_map/ppermute | solution.py:330
  88.5 212.7 %collective-permute-start.12 = (bf16[2048,896]{1,0:T(8,128)(2,1)}, bf16[2048,896]{1,0:T(8,128)(2,1)}, u32[]{:S(2)}, u32[]{:S(2)}) collective-permute-start(bf16[2048,896]{1,0:T(8,128)(2,1)} %collective-permute-done.8.x_ref), channel_id=1, source_target_pairs={{0,2},{1,3},{2,0},{3,1},{4,6},{5,7},{6,4},{7,5}} | collective-permute-start | bytes 11010056 | tf_op jit(solution)/shard_map/ppermute | solution.py:333
  90.0 83.3 %collective-permute-start.3 = (f32[16,2048]{1,0:T(8,128)}, f32[16,2048]{1,0:T(8,128)S(1)}, u32[]{:S(2)}, u32[]{:S(2)}) collective-permute-start(f32[16,2048]{1,0:T(8,128)} %pad_maximum_fusion.5), channel_id=1, source_target_pairs={{0,2},{1,3},{2,0},{3,1},{4,6},{5,7},{6,4},{7,5}} | collective-permute-start | bytes 393224 | tf_op jit(solution)/shard_map/ppermute | solution.py:337
  173.3 6.1 collective-permute-start.4
  179.4 5.1 collective-permute-start.5
  184.5 6.3 collective-permute-start.6
  190.8 12.8 %collective-permute-start.21 = (bf16[3,112,640]{2,1,0:T(8,128)(2,1)S(1)}, bf16[3,112,640]{2,1,0:T(8,128)(2,1)S(1)}, u32[]{:S(2)}, u32[]{:S(2)}) collective-permute-start(bf16[3,112,640]{2,1,0:T(8,128)(2,1)S(1)} %get-tuple-element.130), channel_id=1, source_target_pairs={{0,7},{1,6},{2,5},{3,4},{4,3},{5,2},{6,1},{7,0}} | collective-permute-start | bytes 1290248 | tf_op jit(solution)/shard_map/ppermute | solution.py:337
  203.5 6.6 copy-start.8
  203.6 94.8 %collective-permute-start.20 = (bf16[3,112,640]{2,1,0:T(8,128)(2,1)S(1)}, bf16[3,112,640]{2,1,0:T(8,128)(2,1)S(1)}, u32[]{:S(2)}, u32[]{:S(2)}) collective-permute-start(bf16[3,112,640]{2,1,0:T(8,128)(2,1)S(1)} %get-tuple-element.131), channel_id=1, source_target_pairs={{0,3},{1,2},{2,1},{3,0},{4,7},{5,6},{6,5},{7,4}} | collective-permute-start | bytes 1290248 | tf_op jit(solution)/shard_map/ppermute | solution.py:337
  205.0 5.1 copy-start.2
  205.0 94.0 %collective-permute-start.19 = (bf16[3,112,640]{2,1,0:T(8,128)(2,1)S(1)}, bf16[3,112,640]{2,1,0:T(8,128)(2,1)S(1)}, u32[]{:S(2)}, u32[]{:S(2)}) collective-permute-start(bf16[3,112,640]{2,1,0:T(8,128)(2,1)S(1)} %get-tuple-element.132), channel_id=1, source_target_pairs={{0,6},{1,7},{2,4},{3,5},{4,2},{5,3},{6,0},{7,1}} | collective-permute-start | bytes 1290248 | tf_op jit(solution)/shard_map/ppermute | solution.py:337
  205.6 93.5 %collective-permute-start.18 = (bf16[3,112,640]{2,1,0:T(8,128)(2,1)S(1)}, bf16[3,112,640]{2,1,0:T(8,128)(2,1)S(1)}, u32[]{:S(2)}, u32[]{:S(2)}) collective-permute-start(bf16[3,112,640]{2,1,0:T(8,128)(2,1)S(1)} %get-tuple-element.133), channel_id=1, source_target_pairs={{0,2},{1,3},{2,0},{3,1},{4,6},{5,7},{6,4},{7,5}} | collective-permute-start | bytes 1290248 | tf_op jit(solution)/shard_map/ppermute | solution.py:337
  206.6 94.4 %collective-permute-start.17 = (bf16[3,112,640]{2,1,0:T(8,128)(2,1)S(1)}, bf16[3,112,640]{2,1,0:T(8,128)(2,1)S(1)}, u32[]{:S(2)}, u32[]{:S(2)}) collective-permute-start(bf16[3,112,640]{2,1,0:T(8,128)(2,1)S(1)} %get-tuple-element.134), channel_id=1, source_target_pairs={{0,5},{1,4},{2,7},{3,6},{4,1},{5,0},{6,3},{7,2}} | collective-permute-start | bytes 1290248 | tf_op jit(solution)/shard_map/ppermute | solution.py:337
  283.6 49.9 %copy-start.5 = (bf16[3,1,448,640]{3,2,1,0:T(8,128)(2,1)S(1)}, bf16[3,1,448,640]{3,2,1,0:T(8,128)(2,1)}, u32[]{:S(2)}) copy-start(bf16[3,1,448,640]{3,2,1,0:T(8,128)(2,1)} %pad_maximum_fusion.3) | copy-start | bytes 5160964
  298.3 33.6 %copy-start.9 = (bf16[3,112,640]{2,1,0:T(8,128)(2,1)}, bf16[3,112,640]{2,1,0:T(8,128)(2,1)S(1)}, u32[]{:S(2)}) copy-start(bf16[3,112,640]{2,1,0:T(8,128)(2,1)S(1)} %collective-permute-done.20.refs_6_) | copy-start | bytes 1290244
  298.3 35.1 %collective-permute-start.16 = (bf16[3,112,640]{2,1,0:T(8,128)(2,1)}, bf16[3,112,640]{2,1,0:T(8,128)(2,1)}, u32[]{:S(2)}, u32[]{:S(2)}) collective-permute-start(bf16[3,112,640]{2,1,0:T(8,128)(2,1)} %get-tuple-element.135), channel_id=1, source_target_pairs={{0,1},{1,0},{2,3},{3,2},{4,5},{5,4},{6,7},{7,6}} | collective-permute-start | bytes 1290248 | tf_op jit(solution)/shard_map/ppermute | solution.py:337
  299.0 32.9 %copy-start.10 = (bf16[3,112,640]{2,1,0:T(8,128)(2,1)}, bf16[3,112,640]{2,1,0:T(8,128)(2,1)S(1)}, u32[]{:S(2)}) copy-start(bf16[3,112,640]{2,1,0:T(8,128)(2,1)S(1)} %collective-permute-done.19.refs_5_) | copy-start | bytes 1290244
  299.0 77.6 %collective-permute-start.14 = (bf16[3,2,448,640]{3,2,1,0:T(8,128)(2,1)}, bf16[3,2,448,640]{3,2,1,0:T(8,128)(2,1)}, u32[]{:S(2)}, u32[]{:S(2)}) collective-permute-start(bf16[3,2,448,640]{3,2,1,0:T(8,128)(2,1)} %pad_maximum_fusion), channel_id=1, source_target_pairs={{0,4},{4,0},{1,5},{5,1},{2,6},{6,2},{3,7},{7,3}} | collective-permute-start | bytes 10321928 | tf_op jit(solution)/shard_map/ppermute | solution.py:327
  299.1 32.8 %copy-start.11 = (bf16[3,112,640]{2,1,0:T(8,128)(2,1)}, bf16[3,112,640]{2,1,0:T(8,128)(2,1)S(1)}, u32[]{:S(2)}) copy-start(bf16[3,112,640]{2,1,0:T(8,128)(2,1)S(1)} %collective-permute-done.18.refs_4_) | copy-start | bytes 1290244
  299.1 325.8 %collective-permute-start.22 = (bf16[3,2,448,640]{3,2,1,0:T(8,128)(2,1)}, bf16[3,2,448,640]{3,2,1,0:T(8,128)(2,1)}, u32[]{:S(2)}, u32[]{:S(2)}) collective-permute-start(bf16[3,2,448,640]{3,2,1,0:T(8,128)(2,1)} %pad_maximum_fusion.1), channel_id=1, source_target_pairs={{0,4},{4,0},{1,5},{5,1},{2,6},{6,2},{3,7},{7,3}} | collective-permute-start | bytes 10321928 | tf_op jit(solution)/shard_map/ppermute | solution.py:327
  301.0 30.9 %copy-start.12 = (bf16[3,112,640]{2,1,0:T(8,128)(2,1)}, bf16[3,112,640]{2,1,0:T(8,128)(2,1)S(1)}, u32[]{:S(2)}) copy-start(bf16[3,112,640]{2,1,0:T(8,128)(2,1)S(1)} %collective-permute-done.17.refs_3_) | copy-start | bytes 1290244
  301.0 394.1 %collective-permute-start.23 = (bf16[3,2,448,640]{3,2,1,0:T(8,128)(2,1)}, bf16[3,2,448,640]{3,2,1,0:T(8,128)(2,1)}, u32[]{:S(2)}, u32[]{:S(2)}) collective-permute-start(bf16[3,2,448,640]{3,2,1,0:T(8,128)(2,1)} %pad_maximum_fusion.2), channel_id=1, source_target_pairs={{0,4},{4,0},{1,5},{5,1},{2,6},{6,2},{3,7},{7,3}} | collective-permute-start | bytes 10321928 | tf_op jit(solution)/shard_map/ppermute | solution.py:327
  301.2 76.7 %collective-permute-start.13 = (bf16[2048,896]{1,0:T(8,128)(2,1)}, bf16[2048,896]{1,0:T(8,128)(2,1)}, u32[]{:S(2)}, u32[]{:S(2)}) collective-permute-start(bf16[2048,896]{1,0:T(8,128)(2,1)} %collective-permute-done.12.x_ref), channel_id=1, source_target_pairs={{0,1},{1,0},{2,3},{3,2},{4,5},{5,4},{6,7},{7,6}} | collective-permute-start | bytes 11010056 | tf_op jit(solution)/shard_map/ppermute | solution.py:330
  333.4 418.2 %collective-permute-start.24 = (bf16[3,1,448,640]{3,2,1,0:T(8,128)(2,1)S(1)}, bf16[3,1,448,640]{3,2,1,0:T(8,128)(2,1)}, u32[]{:S(2)}, u32[]{:S(2)}) collective-permute-start(bf16[3,1,448,640]{3,2,1,0:T(8,128)(2,1)S(1)} %copy-done.5), channel_id=1, source_target_pairs={{0,4},{4,0},{1,5},{5,1},{2,6},{6,2},{3,7},{7,3}} | collective-permute-start | bytes 5160968 | tf_op jit(solution)/shard_map/ppermute | solution.py:327
  376.6 391.3 %collective-permute-start.25 = (bf16[3,1,448,640]{3,2,1,0:T(8,128)(2,1)}, bf16[3,1,448,640]{3,2,1,0:T(8,128)(2,1)}, u32[]{:S(2)}, u32[]{:S(2)}) collective-permute-start(bf16[3,1,448,640]{3,2,1,0:T(8,128)(2,1)} %pad_maximum_fusion.4), channel_id=1, source_target_pairs={{0,4},{4,0},{1,5},{5,1},{2,6},{6,2},{3,7},{7,3}} | collective-permute-start | bytes 5160968 | tf_op jit(solution)/shard_map/ppermute | solution.py:327
  377.9 228.1 %collective-permute-start.15 = (bf16[3,112,640]{2,1,0:T(8,128)(2,1)}, bf16[3,112,640]{2,1,0:T(8,128)(2,1)S(1)}, u32[]{:S(2)}, u32[]{:S(2)}) collective-permute-start(bf16[3,112,640]{2,1,0:T(8,128)(2,1)} %get-tuple-element.136), channel_id=1, source_target_pairs={{0,4},{1,5},{2,6},{3,7},{4,0},{5,1},{6,2},{7,3}} | collective-permute-start | bytes 1290248 | tf_op jit(solution)/shard_map/ppermute | solution.py:337
  606.0 0.8 copy-start.13
  774.5 16.3 %copy-start.21 = (s32[8,320]{1,0:T(8,128)S(1)}, s32[8,320]{1,0:T(8,128)}, u32[]{:S(2)}) copy-start(s32[8,320]{1,0:T(8,128)} %get-tuple-element.158) | copy-start | bytes 30724
  774.5 17.0 %copy-start.20 = (s32[8,320]{1,0:T(8,128)S(1)}, s32[8,320]{1,0:T(8,128)}, u32[]{:S(2)}) copy-start(s32[8,320]{1,0:T(8,128)} %get-tuple-element.159) | copy-start | bytes 30724
  790.8 14.3 %collective-permute-start.26 = (f32[2048,896]{1,0:T(8,128)}, f32[2048,896]{1,0:T(8,128)}, u32[]{:S(2)}, u32[]{:S(2)}) collective-permute-start(f32[2048,896]{1,0:T(8,128)} %combine.8), channel_id=1, source_target_pairs={{0,1},{1,0},{2,3},{3,2},{4,5},{5,4},{6,7},{7,6}} | collective-permute-start | bytes 22020104 | tf_op jit(solution)/shard_map/ppermute | solution.py:330
  824.2 17.0 %copy-start.19 = (s32[8,320]{1,0:T(8,128)S(1)}, s32[8,320]{1,0:T(8,128)}, u32[]{:S(2)}) copy-start(s32[8,320]{1,0:T(8,128)} %get-tuple-element.160) | copy-start | bytes 30724
  840.9 22.3 %collective-permute-start.27 = (f32[2048,896]{1,0:T(8,128)}, f32[2048,896]{1,0:T(8,128)}, u32[]{:S(2)}, u32[]{:S(2)}) collective-permute-start(f32[2048,896]{1,0:T(8,128)} %combine.10), channel_id=1, source_target_pairs={{0,1},{1,0},{2,3},{3,2},{4,5},{5,4},{6,7},{7,6}} | collective-permute-start | bytes 22020104 | tf_op jit(solution)/shard_map/ppermute | solution.py:330
  841.8 19.4 %copy-start.18 = (s32[8,320]{1,0:T(8,128)S(1)}, s32[8,320]{1,0:T(8,128)}, u32[]{:S(2)}) copy-start(s32[8,320]{1,0:T(8,128)} %get-tuple-element.156) | copy-start | bytes 30724
  841.8 20.0 %copy-start.17 = (s32[8,320]{1,0:T(8,128)S(1)}, s32[8,320]{1,0:T(8,128)}, u32[]{:S(2)}) copy-start(s32[8,320]{1,0:T(8,128)} %get-tuple-element.161) | copy-start | bytes 30724
  841.8 20.7 %copy-start.16 = (s32[8,320]{1,0:T(8,128)S(1)}, s32[8,320]{1,0:T(8,128)}, u32[]{:S(2)}) copy-start(s32[8,320]{1,0:T(8,128)} %get-tuple-element.162) | copy-start | bytes 30724
  858.5 23.8 %collective-permute-start.28 = (f32[2048,896]{1,0:T(8,128)}, f32[2048,896]{1,0:T(8,128)}, u32[]{:S(2)}, u32[]{:S(2)}) collective-permute-start(f32[2048,896]{1,0:T(8,128)} %combine.11), channel_id=1, source_target_pairs={{0,1},{1,0},{2,3},{3,2},{4,5},{5,4},{6,7},{7,6}} | collective-permute-start | bytes 22020104 | tf_op jit(solution)/shard_map/ppermute | solution.py:330
  858.6 82.0 %collective-permute-start.29 = (f32[1024,896]{1,0:T(8,128)}, f32[1024,896]{1,0:T(8,128)}, u32[]{:S(2)}, u32[]{:S(2)}) collective-permute-start(f32[1024,896]{1,0:T(8,128)} %get-tuple-element.100), channel_id=1, source_target_pairs={{0,4},{4,0},{1,5},{5,1},{2,6},{6,2},{3,7},{7,3}} | collective-permute-start | bytes 11010056 | tf_op jit(solution)/shard_map/ppermute | solution.py:327
  860.2 81.8 %collective-permute-start.30 = (f32[1024,896]{1,0:T(8,128)}, f32[1024,896]{1,0:T(8,128)}, u32[]{:S(2)}, u32[]{:S(2)}) collective-permute-start(f32[1024,896]{1,0:T(8,128)} %get-tuple-element.92), channel_id=1, source_target_pairs={{0,2},{1,3},{2,0},{3,1},{4,6},{5,7},{6,4},{7,5}} | collective-permute-start | bytes 11010056 | tf_op jit(solution)/shard_map/ppermute | solution.py:333
  901.6 40.4 %copy-start.3 = (f32[1024,896]{1,0:T(8,128)S(1)}, f32[1024,896]{1,0:T(8,128)}, u32[]{:S(2)}) copy-start(f32[1024,896]{1,0:T(8,128)} %get-tuple-element.102) | copy-start | bytes 11010052
  942.0 4.4 copy-start.4
  950.7 20.5 %copy-start.15 = (s32[8,320]{1,0:T(8,128)S(1)}, s32[8,320]{1,0:T(8,128)}, u32[]{:S(2)}) copy-start(s32[8,320]{1,0:T(8,128)} %get-tuple-element.163) | copy-start | bytes 30724
  967.0 18.4 %collective-permute-start.31 = (f32[2048,896]{1,0:T(8,128)}, f32[2048,896]{1,0:T(8,128)}, u32[]{:S(2)}, u32[]{:S(2)}) collective-permute-start(f32[2048,896]{1,0:T(8,128)} %combine.14), channel_id=1, source_target_pairs={{0,1},{1,0},{2,3},{3,2},{4,5},{5,4},{6,7},{7,6}} | collective-permute-start | bytes 22020104 | tf_op jit(solution)/shard_map/ppermute | solution.py:330
  967.1 82.5 %collective-permute-start.33 = (f32[1024,896]{1,0:T(8,128)}, f32[1024,896]{1,0:T(8,128)}, u32[]{:S(2)}, u32[]{:S(2)}) collective-permute-start(f32[1024,896]{1,0:T(8,128)} %get-tuple-element.110), channel_id=1, source_target_pairs={{0,4},{4,0},{1,5},{5,1},{2,6},{6,2},{3,7},{7,3}} | collective-permute-start | bytes 11010056 | tf_op jit(solution)/shard_map/ppermute | solution.py:327
  968.2 82.5 %collective-permute-start.32 = (f32[1024,896]{1,0:T(8,128)}, f32[1024,896]{1,0:T(8,128)}, u32[]{:S(2)}, u32[]{:S(2)}) collective-permute-start(f32[1024,896]{1,0:T(8,128)} %get-tuple-element.96), channel_id=1, source_target_pairs={{0,2},{1,3},{2,0},{3,1},{4,6},{5,7},{6,4},{7,5}} | collective-permute-start | bytes 11010056 | tf_op jit(solution)/shard_map/ppermute | solution.py:333
  969.4 158.3 %collective-permute-start.34 = (f32[1024,896]{1,0:T(8,128)}, f32[1024,896]{1,0:T(8,128)}, u32[]{:S(2)}, u32[]{:S(2)}) collective-permute-start(f32[1024,896]{1,0:T(8,128)} %add.129), channel_id=1, source_target_pairs={{0,4},{4,0},{1,5},{5,1},{2,6},{6,2},{3,7},{7,3}} | collective-permute-start | bytes 11010056 | tf_op jit(solution)/shard_map/ppermute | solution.py:327
  970.2 158.4 %collective-permute-start.35 = (f32[1024,896]{1,0:T(8,128)}, f32[1024,896]{1,0:T(8,128)}, u32[]{:S(2)}, u32[]{:S(2)}) collective-permute-start(f32[1024,896]{1,0:T(8,128)} %add.128), channel_id=1, source_target_pairs={{0,2},{1,3},{2,0},{3,1},{4,6},{5,7},{6,4},{7,5}} | collective-permute-start | bytes 11010056 | tf_op jit(solution)/shard_map/ppermute | solution.py:333
  985.4 65.3 %copy-start.1 = (bf16[2048,896]{1,0:T(8,128)(2,1)S(1)}, bf16[2048,896]{1,0:T(8,128)(2,1)}, u32[]{:S(2)}) copy-start(bf16[2048,896]{1,0:T(8,128)(2,1)} %x_ref.1) | copy-start | bytes 11010052
